TPU v7x, 8 devices: a whole 2x2x1 slice. The times are simulated.
8 devices in a mesh: dp: 1 (over z), tp: 2 (over y), sp: 4 (over x, core).
Axes of the slice: x: 2, y: 2, z: 1, core: 2. Of those that a mesh axis runs over, the one named last changes fastest.
Arguments:
- x_in: bfloat16 [256, 4608], P('dp')
- cur_pos: int32 [256], P('dp')
- w_pre: float32 [4608], replicated
- w_q: bfloat16 [4608, 4096], P(None, 'tp')
- w_k: bfloat16 [4608, 2048], P(None, 'tp')
- w_v: bfloat16 [4608, 2048], P(None, 'tp')
- w_o: bfloat16 [4096, 4608], P('tp')
- w_post: float32 [4608], replicated
- k_cache: bfloat16 [256, 256, 16, 128], P('dp', 'sp', 'tp')
- v_cache: bfloat16 [256, 256, 16, 128], P('dp', 'sp', 'tp')
Outputs:
- output 1: bfloat16 [256, 4608], P('dp')
- output 2: bfloat16 [256, 256, 16, 128], P('dp', 'sp', 'tp')
- output 3: bfloat16 [256, 256, 16, 128], P('dp', 'sp', 'tp')
All inputs are finite; a program needn't handle non-finite values.
Results may differ from a plain program's by a relative error of at most 0.00626649.
Values sent between devices are 32-bit elements.
A program may use at most 1 GiB of HBM per device.

v0:
```python
import jax
import jax.numpy as jnp
from jax import lax
from jax.sharding import PartitionSpec as P

SOFT_CAP = 50.0
ROPE_BASE = 10000.0
NORM_EPS = 1e-6
NEG_FILL = -1e30


def rms_scale(tensor, gain_w):
    mean_sq = jnp.mean(tensor * tensor, axis=-1, keepdims=True)
    return tensor * lax.rsqrt(mean_sq + NORM_EPS) * (1.0 + gain_w)


def rotary(tensor, positions):
    half_dim = tensor.shape[-1] // 2
    inv_freq = ROPE_BASE ** (-2.0 * jnp.arange(half_dim, dtype=jnp.float32) / (2 * half_dim))
    angles = positions.astype(jnp.float32)[:, None] * inv_freq[None, :]
    angles = angles.reshape((angles.shape[0],) + (1,) * (tensor.ndim - 2) + (half_dim,))
    cos_tab = jnp.cos(angles)
    sin_tab = jnp.sin(angles)
    lo_half = tensor[..., :half_dim]
    hi_half = tensor[..., half_dim:]
    return jnp.concatenate([lo_half * cos_tab - hi_half * sin_tab, hi_half * cos_tab + lo_half * sin_tab], axis=-1)


def solution(mesh):
    cache_spec = P('dp', 'sp', 'tp', None)

    def local_step(x_in, cur_pos, w_pre, w_q, w_k, w_v, w_o, w_post, k_cache, v_cache):
        row_count, seq_block, kv_local, head_dim = k_cache.shape
        heads_local = w_q.shape[1] // head_dim
        group_size = heads_local // kv_local
        sp_index = lax.axis_index('sp')
        normed = rms_scale(x_in.astype(jnp.float32), w_pre).astype(jnp.bfloat16)
        q_proj = jnp.dot(normed, w_q, preferred_element_type=jnp.float32)
        q_rot = rotary(q_proj.reshape(row_count, kv_local, group_size, head_dim), cur_pos).astype(jnp.bfloat16)
        k_proj = jnp.dot(normed, w_k, preferred_element_type=jnp.float32)
        k_new = rotary(k_proj.reshape(row_count, kv_local, head_dim), cur_pos).astype(jnp.bfloat16)
        v_new = jnp.dot(normed, w_v, preferred_element_type=jnp.float32).reshape(row_count, kv_local, head_dim).astype(jnp.bfloat16)
        block_pos = sp_index * seq_block + jnp.arange(seq_block)
        slot_hit = (block_pos[None, :] == cur_pos[:, None])[:, :, None, None]
        k_out = jnp.where(slot_hit, k_new[:, None], k_cache)
        v_out = jnp.where(slot_hit, v_new[:, None], v_cache)
        raw_score = jnp.einsum('bgrd,btgd->bgrt', q_rot, k_out, preferred_element_type=jnp.float32)
        capped = SOFT_CAP * jnp.tanh(raw_score * (head_dim ** -0.5 / SOFT_CAP))
        is_valid = (block_pos[None, :] <= cur_pos[:, None])[:, None, None, :]
        capped = jnp.where(is_valid, capped, NEG_FILL)
        block_max = jnp.max(capped, axis=-1)
        exp_w = jnp.where(is_valid, jnp.exp(capped - block_max[..., None]), 0.0)
        block_sum = jnp.sum(exp_w, axis=-1)
        block_out = jnp.einsum('bgrt,btgd->bgrd', exp_w.astype(jnp.bfloat16), v_out, preferred_element_type=jnp.float32)
        global_max = lax.pmax(block_max, 'sp')
        factor = jnp.exp(block_max - global_max)
        packed = jnp.concatenate([block_out * factor[..., None], (block_sum * factor)[..., None]], axis=-1)
        merged = lax.psum(packed, 'sp')
        attn_out = (merged[..., :head_dim] / merged[..., head_dim:]).reshape(row_count, heads_local * head_dim)
        proj_part = jnp.dot(attn_out.astype(jnp.bfloat16), w_o, preferred_element_type=jnp.float32)
        proj_sum = lax.psum(proj_part, 'tp')
        x_out = (x_in.astype(jnp.float32) + rms_scale(proj_sum, w_post)).astype(jnp.bfloat16)
        return x_out, k_out, v_out

    return jax.shard_map(local_step, mesh=mesh,
                         in_specs=(P('dp', None), P('dp'), P(None), P(None, 'tp'), P(None, 'tp'), P(None, 'tp'), P('tp', None), P(None), cache_spec, cache_spec),
                         out_specs=(P('dp', None), cache_spec, cache_spec), check_vma=False)
```

profile of v0, /device:TPU:0, one launch (start us, length us, event | category | flops | bytes accessed | tf_op | source)
XLA Modules:
  0.0 415.8 jit_solution(9243069278120575253)
XLA Ops:
  7.2 0.0 all-reduce.3.cloned.1.call-start
  7.2 0.7 broadcast_add_fusion.1
  8.0 0.0 slice-start.1
  8.0 2.4 fusion.4
  10.3 0.0 copy-start.6
  10.3 0.0 copy-start.1
  10.4 0.0 slice-start.2
  10.4 0.0 slice-start.3
  10.4 7.1 %convolution_bitcast_fusion = f32[32,8,8,128]{3,1,2,0:T(8,128)S(1)} fusion(bf16[4608,1024]{1,0:T(8,128)(2,1)} %param.14, bf16[256,4608]{1,0:T(8,128)(2,1)} %param.10, f32[4608]{0:T(1024)S(1)} %broadcast_add_fusion.1, f32[256]{0:T(256)S(1)} %add_rsqrt_fusion.1), kind=kOutput, calls=%fused_computation.22 | convolution fusion | flops 2420637696 | bytes 12864512 | tf_op jit(solution)/shard_map/dot_general | solution.py:40
  17.5 0.2 copy.31
  17.7 0.0 copy-done.6
  17.7 0.0 slice-done.1
  17.7 0.0 copy-done.1
  17.8 0.0 slice-done.2
  17.8 0.0 slice-done.3
  17.8 2.6 fusion.14
  20.4 0.9 copy.32
  21.3 0.1 broadcast_compare_fusion
  21.5 10.4 %fusion.24 = f32[256,2048]{1,0:T(8,128)} fusion(bf16[4608,2048]{1,0:T(8,128)(2,1)} %param.13, bf16[256,4608]{1,0:T(8,128)(2,1)S(1)} %copy-done.1, f32[4608]{0:T(1024)S(1)} %broadcast_add_fusion.1, f32[256]{0:T(256)S(1)} %add_rsqrt_fusion.1), kind=kOutput, calls=%fused_computation.47 | convolution fusion | flops 4836556800 | bytes 23350272 | tf_op jit(solution)/shard_map/dot_general | solution.py:38
  31.8 3.0 reshape.208
  34.9 0.5 multiply_cosine_fusion
  35.4 0.4 subtract_convert_fusion.1
  35.9 0.0 copy-start.3
  35.9 3.6 subtract_convert_fusion
  39.5 0.3 pad_maximum_fusion.1
  39.8 0.0 copy-done.3
  39.8 0.0 copy-start.4
  39.8 44.4 %broadcast_select_fusion = (bf16[256,64,8,128]{3,2,1,0:T(8,128)(2,1)}, bf16[256,64,8,128]{3,2,1,0:T(8,128)(2,1)}) fusion(bf16[256,64,8,128]{3,2,1,0:T(8,128)(2,1)} %param.19, pred[256,64]{1,0:T(8,128)(4,1)S(1)} %get-tuple-element.13, bf16[256,8,128]{2,1,0:T(8,128)(2,1)S(1)} %bitcast.17, bf16[256,64,8,128]{3,2,1,0:T(8,128)(2,1)} %param.18, ...), kind=kLoop, calls=%fused_computation.4 | loop fusion | flops 33554432 | bytes 135282688 | tf_op jit(solution)/shard_map/jit(_where)/select_n | solution.py:46
  84.3 0.0 copy-done.4
  84.3 24.1 %fusion.26 = (f32[256,8,2]{2,1,0:T(8,128)S(1)}, f32[256,8,2,64]{3,2,1,0:T(2,128)}) fusion(bf16[256,64,8,128]{3,2,1,0:T(8,128)(2,1)} %get-tuple-element.10, bf16[256,8,2,64]{3,2,1,0:T(2,128)(2,1)S(1)} %copy-done.4, bf16[256,8,2,64]{3,2,1,0:T(2,128)(2,1)S(1)} %get-tuple-element.5, pred[256,64]{1,0:T(8,128)(4,1)S(1)} %get-tuple-element.14), kind=kOutput, calls=%fused_computation.48 | convolution fusion | flops 70250496 | bytes 35684352 | tf_op jit(solution)/shard_map/bgrd,btgd->bgrt/dot_general | solution.py:47
  108.4 28.2 %pmax.7 = f32[256,8,2]{2,1,0:T(8,128)S(1)} all-reduce(f32[256,8,2]{2,1,0:T(8,128)S(1)} %get-tuple-element.15), channel_id=1, replica_groups=mesh['dp'=1,'tp'=2,'sp'=4] {'sp'}, use_global_device_ids=true, to_apply=%region_2.3 | all-reduce | flops 4096 | bytes 32768 | tf_op jit(solution)/shard_map/pmax | solution.py:55
  136.6 6.7 %fusion.19 = f32[256,8,2]{2,1,0:T(8,128)S(1)} fusion(f32[256,8,2,64]{3,2,1,0:T(2,128)} %get-tuple-element.16, f32[256,8,2]{2,1,0:T(8,128)S(1)} %get-tuple-element.15, pred[256,64]{1,0:T(8,128)(4,1)S(1)} %get-tuple-element.14), kind=kLoop, calls=%fused_computation.36 | loop fusion | flops 782336 | bytes 1097728 | tf_op jit(solution)/shard_map/reduce_sum | solution.py:53
  143.3 1.6 multiply_bitcast_fusion
  144.9 13.8 %copy.25 = f32[256,8,2,1]{3,2,1,0:T(2,128)S(1)} copy(f32[256,8,2,1]{2,1,0,3:T(8,128)} %get-tuple-element.3) | data formatting | bytes 32768 | tf_op jit(solution)/shard_map/broadcast_in_dim | solution.py:57
  158.7 15.0 %fusion.11 = f32[256,8,2,128]{3,2,1,0:T(2,128)S(1)} fusion(bf16[256,64,8,128]{3,2,1,0:T(8,128)(2,1)} %get-tuple-element.9, f32[256,8,2]{2,1,0:T(8,128)} %get-tuple-element.4, f32[256,8,2,64]{3,2,1,0:T(2,128)} %get-tuple-element.16, pred[256,64]{1,0:T(8,128)(4,1)S(1)} %get-tuple-element.14, f32[256,8,2]{2,1,0:T(8,128)S(1)} %get-tuple-element.15), kind=kOutput, calls=%fused_computation.21 | convolution fusion | flops 68419584 | bytes 36749312 | tf_op jit(solution)/shard_map/bgrt,btgd->bgrd/dot_general | solution.py:54
  173.7 4.3 %pad_maximum_fusion = f32[256,8,2,129]{3,2,1,0:T(2,128)} fusion(f32[256,8,2,1]{3,2,1,0:T(2,128)S(1)} %copy.25, f32[256,8,2,128]{3,2,1,0:T(2,128)S(1)} %fusion.11), kind=kLoop, calls=%fused_computation.14 | loop fusion | flops 528384 | bytes 4227072 | tf_op jit(solution)/shard_map/concatenate | solution.py:57
  178.0 0.0 all-reduce.3.cloned.1.call-update
  178.1 0.0 all-reduce.5.cloned.1.call-start
  178.1 80.1 %all-reduce.3.cloned.1.call-done = f32[256,8,2,129]{3,2,1,0:T(2,128)} async-done(((f32[256,8,2,129]{3,2,1,0:T(2,128)}), f32[256,8,2,129]{3,2,1,0:T(2,128)}) %all-reduce.3.cloned.1.call-update) | async-done | bytes 2113552 | tf_op jit(solution)/shard_map/psum | solution.py:58
  258.2 0.0 slice-start
  258.2 1.6 slice-done
  259.8 12.4 %copy.30 = f32[256,8,2,1]{2,1,0,3:T(8,128)S(1)} copy(f32[256,8,2,1]{3,2,1,0:T(2,128)S(1)} %slice-done) | data formatting | bytes 32768 | tf_op jit(solution)/shard_map/div | solution.py:59
  272.2 4.9 %fusion.8 = bf16[256,8,2,128]{3,2,1,0:T(2,128)(2,1)S(1)} fusion(f32[256,8,2,129]{3,2,1,0:T(2,128)} %all-reduce.3.cloned.1.call-done, f32[256,8,2]{2,1,0:T(8,128)S(1)} %bitcast.16), kind=kLoop, calls=%fused_computation.20 | loop fusion | flops 1048576 | bytes 3162112 | tf_op jit(solution)/shard_map/convert_element_type | solution.py:60
  277.1 0.8 convert_element_type.46
  278.0 11.1 %fusion.27 = f32[256,4608]{1,0:T(8,128)} fusion(bf16[256,2048]{1,0:T(8,128)(2,1)S(1)} %convert_element_type.46, bf16[2048,4608]{1,0:T(8,128)(2,1)} %param.16), kind=kOutput, calls=%fused_computation.49 | convolution fusion | flops 4831838208 | bytes 24641536 | tf_op jit(solution)/shard_map/dot_general | solution.py:60
  289.1 0.0 copy-start.5
  289.1 0.0 copy-start.2
  289.1 0.0 all-reduce.5.cloned.1.call-update
  289.1 0.7 copy-done.5
  289.8 113.0 %all-reduce.5.cloned.1.call-done = f32[256,4608]{1,0:T(8,128)} async-done(((f32[256,4608]{1,0:T(8,128)}), f32[256,4608]{1,0:T(8,128)}) %all-reduce.5.cloned.1.call-update) | async-done | bytes 4718608 | tf_op jit(solution)/shard_map/psum | solution.py:61
  402.8 0.0 copy-start
  402.8 2.9 multiply_reduce_fusion
  405.7 0.0 copy-done.2
  405.7 0.9 copy-done
  406.6 2.4 fusion.7
  (7 shorter events, 0.0 us)
Async XLA Ops:
  7.2 251.0 %all-reduce.3.cloned.1.call-start = ((), (), s32[]{:S(2)}) async-start(), calls=%async_computation | async-start | bytes 8388608 | tf_op jit(solution)/shard_map/psum | solution.py:58
  8.0 9.8 %slice-start.1 = ((s8[9437184]{0:T(1024)(128)(4,1)}), s8[4194304]{0:T(1024)(128)(4,1)S(1)}, s32[]{:S(2)}) async-start(s8[9437184]{0:T(1024)(128)(4,1)} %bitcast.18), calls=%async_computation.3 | async-start | bytes 8388608
  10.3 7.4 %copy-start.6 = (s32[256]{0:T(256)S(1)}, s32[256]{0:T(256)}, u32[]{:S(2)}) copy-start(s32[256]{0:T(256)} %param.11) | copy-start | bytes 3076
  10.3 7.4 %copy-start.1 = (bf16[256,4608]{1,0:T(8,128)(2,1)S(1)}, bf16[256,4608]{1,0:T(8,128)(2,1)}, u32[]{:S(2)}) copy-start(bf16[256,4608]{1,0:T(8,128)(2,1)} %param.10) | copy-start | bytes 7077892
  10.4 7.4 %slice-start.2 = ((s8[9437184]{0:T(1024)(128)(4,1)}), s8[4194304]{0:T(1024)(128)(4,1)S(1)}, s32[]{:S(2)}) async-start(s8[9437184]{0:T(1024)(128)(4,1)} %bitcast.18), calls=%async_computation.4 | async-start | bytes 8388608
  10.4 7.4 %slice-start.3 = ((s8[9437184]{0:T(1024)(128)(4,1)}), s8[1048576]{0:T(1024)(128)(4,1)S(1)}, s32[]{:S(2)}) async-start(s8[9437184]{0:T(1024)(128)(4,1)} %bitcast.18), calls=%async_computation.5 | async-start | bytes 2097152
  35.9 3.9 copy-start.3
  39.8 44.4 %copy-start.4 = (bf16[256,8,2,64]{3,2,1,0:T(2,128)(2,1)S(1)}, bf16[256,8,2,64]{3,2,1,0:T(2,128)(2,1)}, u32[]{:S(2)}) copy-start(bf16[256,8,2,64]{3,2,1,0:T(2,128)(2,1)} %get-tuple-element.6) | copy-start | bytes 1572868
  178.1 224.8 %all-reduce.5.cloned.1.call-start = ((), (), s32[]{:S(2)}) async-start(), calls=%async_computation.1 | async-start | bytes 9437184 | tf_op jit(solution)/shard_map/psum | solution.py:61
  258.2 1.6 slice-start
  289.1 0.7 copy-start.5
  289.1 116.6 %copy-start.2 = (bf16[256,4608]{1,0:T(8,128)(2,1)S(1)}, bf16[256,4608]{1,0:T(8,128)(2,1)}, u32[]{:S(2)}) copy-start(bf16[256,4608]{1,0:T(8,128)(2,1)} %param.10) | copy-start | bytes 7077892
  402.8 3.8 copy-start
Sparse Core Ops, SparseCore 0:
  178.2 79.9 all-reduce.2
  289.3 113.5 all-reduce.4
where the time goes:
time: 416 us
  waiting for transfers between devices  193 us (46%)
  other arithmetic  75.3 us (18%)
  matrix products  70.4 us (17%)
  local copies, waits for them, and re-layouts  34.4 us (8%)
  blocking collectives  28.2 us (7%)
  between operations  14.3 us (3%)
    psum x1, waiting for transfers between devices, local_step(): proj_sum = lax.psum(proj_part, 'tp')  113 us
    psum x1, waiting for transfers between devices, local_step(): merged = lax.psum(packed, 'sp')  80.1 us
    select_n x1, other arithmetic, local_step(): v_out = jnp.where(slot_hit, v_new[:, None], v_cache)  44.4 us
    pmax x1, blocking collectives, local_step(): global_max = lax.pmax(block_max, 'sp')  28.2 us
    dot_general x1, matrix products, local_step(): jnp.einsum('bgrd,btgd->bgrt', q_rot, k_out, preferred_element_type=jnp.fl...  24.1 us
    dot_general x1, matrix products, local_step(): jnp.einsum('bgrt,btgd->bgrd', exp_w.astype(jnp.bfloat16), v_out, preferre...  15 us
    broadcast_in_dim x1, local copies, waits for them, and re-layouts, local_step(): (block_sum * factor)[..., None]  13.8 us
    div x1, local copies, waits for them, and re-layouts, local_step(): merged[..., :head_dim] / merged[..., head_dim:]  12.4 us
  transfers between devices with their start and end apart: 2, of which 2 were waited for; matrix products, arithmetic and copies ran while one was open for 0% of the time, Pallas kernels for 0%

commit v1 on v0

v1 whole, which is shorter than its diff:
```python
import functools

import jax
import jax.numpy as jnp
from jax import lax
from jax.experimental import pallas as pl
from jax.experimental.pallas import tpu as pltpu
from jax.sharding import PartitionSpec as P

SOFT_CAP = 50.0
ROPE_BASE = 10000.0
NORM_EPS = 1e-6
LOG2E = 1.4426950408889634

ROWS_STEP = 8
SLOTS = 6
AHEAD = 4


def rms_scale(tensor, gain_w):
    mean_sq = jnp.mean(tensor * tensor, axis=-1, keepdims=True)
    return tensor * lax.rsqrt(mean_sq + NORM_EPS) * (1.0 + gain_w)


def rotary(tensor, positions):
    half_dim = tensor.shape[-1] // 2
    inv_freq = ROPE_BASE ** (-2.0 * jnp.arange(half_dim, dtype=jnp.float32) / (2 * half_dim))
    angles = positions.astype(jnp.float32)[:, None] * inv_freq[None, :]
    angles = angles.reshape((angles.shape[0],) + (1,) * (tensor.ndim - 2) + (half_dim,))
    cos_tab = jnp.cos(angles)
    sin_tab = jnp.sin(angles)
    lo_half = tensor[..., :half_dim]
    hi_half = tensor[..., half_dim:]
    return jnp.concatenate([lo_half * cos_tab - hi_half * sin_tab, hi_half * cos_tab + lo_half * sin_tab], axis=-1)


def attend_kernel(n_steps, first_row, kv_heads, seq_block, pos_ref, base_ref, q_hbm, kn_hbm, vn_hbm, k_hbm, v_hbm,
                  *rest):
    (ko_hbm, vo_hbm, o_hbm, m_ref, l_ref, kbuf, vbuf, qbuf, knbuf, vnbuf, obuf, key_ref, in_sem, out_sem, o_sem) = rest[-15:]
    step_rows = ROWS_STEP
    heads, head_dim = qbuf.shape[2], qbuf.shape[3]
    cols = seq_block * kv_heads
    base = base_ref[0]

    row_id = lax.broadcasted_iota(jnp.int32, (heads, cols), 0)
    col_id = lax.broadcasted_iota(jnp.int32, (heads, cols), 1)
    mine = lax.rem(col_id, kv_heads) == row_id // (heads // kv_heads)
    key_ref[...] = jnp.where(mine, col_id, cols * 4)
    lane_id = lax.broadcasted_iota(jnp.int32, m_ref.shape, 1)
    half_id = lax.broadcasted_iota(jnp.int32, (2 * kv_heads, head_dim), 0) // kv_heads

    def loads(step, slot):
        rows = pl.ds(first_row + step * step_rows, step_rows)
        return (pltpu.make_async_copy(k_hbm.at[rows], kbuf.at[slot], in_sem.at[slot, 0]),
                pltpu.make_async_copy(v_hbm.at[rows], vbuf.at[slot], in_sem.at[slot, 1]),
                pltpu.make_async_copy(q_hbm.at[rows], qbuf.at[slot], in_sem.at[slot, 2]),
                pltpu.make_async_copy(kn_hbm.at[rows], knbuf.at[slot], in_sem.at[slot, 3]),
                pltpu.make_async_copy(vn_hbm.at[rows], vnbuf.at[slot], in_sem.at[slot, 4]))

    def stores(step, slot):
        rows = pl.ds(first_row + step * step_rows, step_rows)
        return (pltpu.make_async_copy(kbuf.at[slot], ko_hbm.at[rows], out_sem.at[slot, 0]),
                pltpu.make_async_copy(vbuf.at[slot], vo_hbm.at[rows], out_sem.at[slot, 1]))

    def o_store(step, slot):
        rows = pl.ds(step * step_rows, step_rows)
        return pltpu.make_async_copy(obuf.at[slot], o_hbm.at[rows], o_sem.at[slot])

    for step in range(min(AHEAD, n_steps)):
        for copy in loads(step, step):
            copy.start()
    m_ref[...] = jnp.zeros_like(m_ref)
    l_ref[...] = jnp.zeros_like(l_ref)
    scale = head_dim ** -0.5 / SOFT_CAP

    def body(step, carry):
        slot = lax.rem(step, SLOTS)
        oslot = lax.rem(step, 2)
        for copy in loads(step, slot):
            copy.wait()

        for r in range(step_rows):
            local = pos_ref[first_row + step * step_rows + r] - base

            @pl.when((local >= 0) & (local < seq_block))
            def _():
                pair = pl.ds(pl.multiple_of((local // 2) * (2 * kv_heads), 2 * kv_heads), 2 * kv_heads)
                hit = half_id == lax.rem(local, 2)
                kbuf[slot, r, pair, :] = jnp.where(hit, knbuf[slot, r], kbuf[slot, r, pair, :])
                vbuf[slot, r, pair, :] = jnp.where(hit, vnbuf[slot, r], vbuf[slot, r, pair, :])

        @pl.when(step >= 2)
        def _():
            o_store(step - 2, oslot).wait()

        m_all = m_ref[...]
        l_all = l_ref[...]
        for r in range(step_rows):
            local = pos_ref[first_row + step * step_rows + r] - base
            raw = lax.dot_general(qbuf[slot, r], kbuf[slot, r], (((1,), (1,)), ((), ())),
                                  preferred_element_type=jnp.float32)
            seen = key_ref[...] < (local + 1) * kv_heads
            soft = jnp.where(seen, jnp.tanh(raw * scale), -4.0)
            top = jnp.maximum(jnp.max(soft, axis=-1, keepdims=True), -1.0)
            weight = jnp.exp2((soft - top) * (SOFT_CAP * LOG2E))
            total = jnp.sum(weight, axis=-1, keepdims=True)
            weight = weight.astype(jnp.bfloat16)
            half = cols // 2
            left = jnp.concatenate([weight[:, :half], weight[:, half:]], axis=0)
            right = jnp.concatenate([vbuf[slot, r, :half, :], vbuf[slot, r, half:, :]], axis=1)
            both = jnp.dot(left, right, preferred_element_type=jnp.float32)
            obuf[oslot, r] = both[:heads, :head_dim] + both[heads:, head_dim:]
            here = lane_id == step * step_rows + r
            m_all = jnp.where(here, top * SOFT_CAP, m_all)
            l_all = jnp.where(here, total, l_all)
        m_ref[...] = m_all
        l_ref[...] = l_all
        o_store(step, oslot).start()
        for copy in stores(step, slot):
            copy.start()

        @pl.when(step + AHEAD < n_steps)
        def _():
            nxt = step + AHEAD
            nslot = lax.rem(nxt, SLOTS)

            @pl.when(nxt >= SLOTS)
            def _():
                for copy in stores(nxt - SLOTS, nslot):
                    copy.wait()
            for copy in loads(nxt, nslot):
                copy.start()
        return carry

    lax.fori_loop(0, n_steps, body, 0)
    for step in range(max(0, n_steps - SLOTS), n_steps):
        for copy in stores(step, step % SLOTS):
            copy.wait()
    for step in range(max(0, n_steps - 2), n_steps):
        o_store(step, step % 2).wait()


def attend(pos, base, q, kn, vn, k_cache, v_cache, prev, first_row, n_rows):
    rows, cols, head_dim = k_cache.shape
    heads = q.shape[1]
    kv_heads = kn.shape[1] // 2
    seq_block = cols // kv_heads
    n_steps = n_rows // ROWS_STEP
    hbm = pl.BlockSpec(memory_space=pl.ANY)
    vmem = pl.BlockSpec(memory_space=pltpu.VMEM)
    smem = pl.BlockSpec(memory_space=pltpu.SMEM)
    bf = jnp.bfloat16
    aliases = {} if prev is None else {7: 0, 8: 1}
    extra = () if prev is None else tuple(prev)
    return pl.pallas_call(
        functools.partial(attend_kernel, n_steps, first_row, kv_heads, seq_block),
        out_shape=(jax.ShapeDtypeStruct(k_cache.shape, bf), jax.ShapeDtypeStruct(v_cache.shape, bf),
                   jax.ShapeDtypeStruct((n_rows, heads, head_dim), jnp.float32),
                   jax.ShapeDtypeStruct((heads, n_rows), jnp.float32),
                   jax.ShapeDtypeStruct((heads, n_rows), jnp.float32)),
        in_specs=[smem, smem, hbm, hbm, hbm, hbm, hbm] + [hbm] * len(extra),
        out_specs=(hbm, hbm, hbm, vmem, vmem),
        scratch_shapes=[
            pltpu.VMEM((SLOTS, ROWS_STEP, cols, head_dim), bf),
            pltpu.VMEM((SLOTS, ROWS_STEP, cols, head_dim), bf),
            pltpu.VMEM((SLOTS, ROWS_STEP, heads, head_dim), bf),
            pltpu.VMEM((SLOTS, ROWS_STEP, 2 * kv_heads, head_dim), bf),
            pltpu.VMEM((SLOTS, ROWS_STEP, 2 * kv_heads, head_dim), bf),
            pltpu.VMEM((2, ROWS_STEP, heads, head_dim), jnp.float32),
            pltpu.VMEM((heads, cols), jnp.int32),
            pltpu.SemaphoreType.DMA((SLOTS, 5)),
            pltpu.SemaphoreType.DMA((SLOTS, 2)),
            pltpu.SemaphoreType.DMA((2,)),
        ],
        input_output_aliases=aliases,
        compiler_params=pltpu.CompilerParams(vmem_limit_bytes=40 * 1024 * 1024),
        cost_estimate=pl.CostEstimate(flops=n_rows * heads * cols * head_dim * 4,
                                      bytes_accessed=n_rows * cols * head_dim * 8, transcendentals=0),
        name='attend',
    )(pos, base, q, kn, vn, k_cache, v_cache, *extra)


def solution(mesh):
    cache_spec = P('dp', 'sp', 'tp', None)
    sp_size = mesh.shape['sp']
    tp_size = mesh.shape['tp']

    def swap(value, axis, size, bit):
        return lax.ppermute(value, axis, [(i, i ^ bit) for i in range(size)])

    def local_step(x_in, cur_pos, w_pre, w_q, w_k, w_v, w_o, w_post, k_cache, v_cache):
        row_count, seq_block, kv_local, head_dim = k_cache.shape
        heads_local = w_q.shape[1] // head_dim
        sp_index = lax.axis_index('sp')
        x_f = x_in.astype(jnp.float32)
        normed = rms_scale(x_f, w_pre).astype(jnp.bfloat16)
        q_proj = jnp.dot(normed, w_q, preferred_element_type=jnp.float32)
        q_rot = rotary(q_proj.reshape(row_count, heads_local, head_dim), cur_pos).astype(jnp.bfloat16)
        k_proj = jnp.dot(normed, w_k, preferred_element_type=jnp.float32)
        k_new = rotary(k_proj.reshape(row_count, kv_local, head_dim), cur_pos).astype(jnp.bfloat16)
        v_new = jnp.dot(normed, w_v, preferred_element_type=jnp.float32).reshape(row_count, kv_local, head_dim).astype(jnp.bfloat16)
        kn2 = jnp.concatenate([k_new, k_new], axis=1)
        vn2 = jnp.concatenate([v_new, v_new], axis=1)
        base = (sp_index * seq_block).astype(jnp.int32).reshape(1)
        kc = k_cache.reshape(row_count, seq_block * kv_local, head_dim)
        vc = v_cache.reshape(row_count, seq_block * kv_local, head_dim)
        k_out, v_out, o, m, l = attend(cur_pos, base, q_rot, kn2, vn2, kc, vc, None, 0, row_count)

        stat = jnp.concatenate([m, l], axis=0).T[:, :, None]
        stat = jnp.broadcast_to(stat, stat.shape[:2] + (4,)).reshape(row_count, 1, head_dim)
        pack = jnp.concatenate([o, stat], axis=1)

        def unpack(p):
            s = p[:, heads_local:].reshape(p.shape[0], 2 * heads_local, 4)[:, :, :1]
            return p[:, :heads_local], s[:, :heads_local], s[:, heads_local:]

        def merge(a, b):
            oa, ma, la = unpack(a)
            ob, mb, lb = unpack(b)
            mm = jnp.maximum(ma, mb)
            fa, fb = jnp.exp(ma - mm), jnp.exp(mb - mm)
            return oa * fa + ob * fb, mm, la * fa + lb * fb

        def repack(om, mm, lm):
            s = jnp.concatenate([mm, lm], axis=1)
            s = jnp.broadcast_to(s, s.shape[:2] + (4,)).reshape(om.shape[0], 1, head_dim)
            return jnp.concatenate([om, s], axis=1)

        half = row_count // 2
        core = sp_index % 2
        xpos = sp_index // 2
        keep = lax.dynamic_slice_in_dim(pack, core * half, half, 0)
        give = lax.dynamic_slice_in_dim(pack, (1 - core) * half, half, 0)
        got = swap(give, 'sp', sp_size, 1)
        pack = repack(*merge(keep, got))
        quarter = half // 2
        keep = lax.dynamic_slice_in_dim(pack, xpos * quarter, quarter, 0)
        give = lax.dynamic_slice_in_dim(pack, (1 - xpos) * quarter, quarter, 0)
        got = swap(give, 'sp', sp_size, 2)
        om, mm, lm = merge(keep, got)
        attn = (om / lm).reshape(quarter, heads_local * head_dim).astype(jnp.bfloat16)
        part = jnp.dot(attn, w_o, preferred_element_type=jnp.float32)
        proj_sum = part + swap(part, 'tp', tp_size, 1)
        y = rms_scale(proj_sum, w_post)
        other = swap(y, 'sp', sp_size, 2)
        y2 = jnp.where(xpos == 0, jnp.concatenate([y, other], 0), jnp.concatenate([other, y], 0))
        other = swap(y2, 'sp', sp_size, 1)
        y4 = jnp.where(core == 0, jnp.concatenate([y2, other], 0), jnp.concatenate([other, y2], 0))
        x_out = (x_f + y4).astype(jnp.bfloat16)
        return x_out, k_out.reshape(k_cache.shape), v_out.reshape(v_cache.shape)

    return jax.shard_map(local_step, mesh=mesh,
                         in_specs=(P('dp', None), P('dp'), P(None), P(None, 'tp'), P(None, 'tp'), P(None, 'tp'), P('tp', None), P(None), cache_spec, cache_spec),
                         out_specs=(P('dp', None), cache_spec, cache_spec), check_vma=False)
```

time: 416 us -> 205 us (0.49)
  waiting for transfers between devices: 193 us -> 70.3 us
  Pallas kernels: 0 us -> 80.3 us
  other arithmetic: 75.3 us -> 19.2 us
  matrix products: 70.4 us -> 22.3 us
  local copies, waits for them, and re-layouts: 34.4 us -> 4.36 us
  blocking collectives: 28.2 us -> 0 us
  between operations: 14.3 us -> 1.13 us
  starting transfers between devices: 0.08 us -> 7.01 us
    psum x2 -> x0, waiting for transfers between devices: 193 us -> none  [the longest x1 113 us: local_step(): proj_sum = lax.psum(proj_part, 'tp')]
    pallas_call x0 -> x1, Pallas kernels: none -> 80.3 us  [attend(): pl.pallas_call(functools.partial(attend_kernel, n_steps, first_row, kv_he...]
    ppermute x0 -> x5, waiting for transfers between devices: none -> 70.3 us  [swap(): return lax.ppermute(value, axis, [(i, i ^ bit) for i in range(size)])]
    dot_general x3 -> x1, matrix products: 50.3 us -> 8.13 us  [local_step(): part = jnp.dot(attn, w_o, preferred_element_type=jnp.float32)]
    select_n x1, other arithmetic: 44.4 us -> 3.24 us  [local_step(): jnp.where(xpos == 0, jnp.concatenate([y, other], 0), jnp.concatenate([oth...]
    pmax x1 -> x0, blocking collectives: 28.2 us -> none  [local_step(): global_max = lax.pmax(block_max, 'sp')]
    broadcast_in_dim x1 -> x2, local copies, waits for them, and re-layouts: 13.8 us -> 0.04 us  [the longest x1 0.02 us: local_step(): jnp.broadcast_to(stat, stat.shape[:2] + (4,))]
    div x1, local copies, waits for them, and re-layouts: 12.4 us -> 0.08 us  [local_step(): om / lm]
  transfers between devices with their start and end apart: 2 -> 5, of which waited for: 2 -> 5; matrix products, arithmetic and copies ran while one was open for 0% -> 0% of each run, Pallas kernels for 0% -> 0%
where the time goes in v1:
time: 205 us
  Pallas kernels  80.3 us (39%)
  waiting for transfers between devices  70.3 us (34%)
  matrix products  22.3 us (11%)
  other arithmetic  19.2 us (9%)
  starting transfers between devices  7.01 us (3%)
  local copies, waits for them, and re-layouts  4.36 us (2%)
    pallas_call x1, Pallas kernels, attend(): pl.pallas_call(functools.partial(attend_kernel, n_steps, first_row, kv_he...  80.3 us
    ppermute x5, waiting for transfers between devices, swap(): return lax.ppermute(value, axis, [(i, i ^ bit) for i in range(size)])  70.3 us
    dot_general x1, matrix products, local_step(): part = jnp.dot(attn, w_o, preferred_element_type=jnp.float32)  8.13 us
    ppermute x5, starting transfers between devices, swap(): return lax.ppermute(value, axis, [(i, i ^ bit) for i in range(size)])  7.01 us
    dot_general x1, matrix products, local_step(): jnp.dot(normed, w_v, preferred_element_type=jnp.float32)  6.48 us
    convert_element_type x1, other arithmetic, local_step(): x_out = (x_f + y4).astype(jnp.bfloat16)  5.27 us
    dot_general x1, matrix products, local_step(): q_proj = jnp.dot(normed, w_q, preferred_element_type=jnp.float32)  5.07 us
  transfers between devices with their start and end apart: 5, of which 5 were waited for; matrix products, arithmetic and copies ran while one was open for 0% of the time, Pallas kernels for 0%

profile of v1, /device:TPU:0, one launch (start us, length us, event | category | flops | bytes accessed | tf_op | source)
XLA Modules:
  0.0 204.5 jit_solution(17645270403994431166)
XLA Ops:
  0.6 0.0 copy-start.1
  0.6 0.0 copy-start.4
  0.7 0.8 convert_element_type.29
  1.5 2.4 %fusion = f32[256]{0:T(256)S(1)} fusion(bf16[256,4608]{1,0:T(8,128)(2,1)} %param.10), kind=kLoop, calls=%fused_computation.3 | loop fusion | flops 3538688 | bytes 2360320 | tf_op jit(solution)/shard_map/reduce_sum | solution.py:21
  3.9 0.0 slice-start.6
  3.9 0.0 slice-start.7
  4.0 0.0 slice-start
  4.0 0.0 slice-start.1
  4.0 0.0 slice-start.2
  4.0 6.5 %fusion.6 = bf16[32,8,8,128]{3,1,2,0:T(8,128)(2,1)S(1)} fusion(bf16[4608,1024]{1,0:T(8,128)(2,1)} %param.15, bf16[256,4608]{1,0:T(8,128)(2,1)S(1)} %copy-done.1, f32[4608]{0:T(1024)S(1)} %broadcast_add_fusion.1, f32[256]{0:T(256)S(1)} %add_rsqrt_fusion), kind=kOutput, calls=%fused_computation.24 | convolution fusion | flops 2420899840 | bytes 12340224 | tf_op jit(solution)/shard_map/dot_general | solution.py:201
  10.5 0.1 copy.54
  10.6 0.1 pad_maximum_fusion.1.vn_hbm
  10.8 0.0 slice-start.3
  10.8 0.0 slice-start.4
  10.8 2.6 %convolution_bitcast_fusion.1 = f32[32,8,8,128]{3,1,2,0:T(8,128)S(1)} fusion(bf16[4608,1024]{1,0:T(8,128)(2,1)S(1)} %bitcast.59, bf16[256,4608]{1,0:T(8,128)(2,1)S(1)} %copy-done.1, f32[4608]{0:T(1024)S(1)} %broadcast_add_fusion.1, f32[256]{0:T(256)S(1)} %add_rsqrt_fusion), kind=kOutput, calls=%fused_computation.22 | convolution fusion | flops 2420637696 | bytes 12864512 | tf_op jit(solution)/shard_map/dot_general | solution.py:199
  13.4 0.2 copy.53
  13.6 0.0 slice-done
  13.6 0.0 slice-done.1
  13.7 0.0 slice-done.2
  13.7 0.0 slice-done.3
  13.7 1.0 slice-done.4
  14.7 5.1 %convolution_bitcast_fusion = f32[32,8,16,128]{3,1,2,0:T(8,128)S(1)} fusion(bf16[4608,2048]{1,0:T(8,128)(2,1)S(1)} %bitcast.57, bf16[256,4608]{1,0:T(8,128)(2,1)S(1)} %copy-done.1, f32[4608]{0:T(1024)S(1)} %broadcast_add_fusion.1, f32[256]{0:T(256)S(1)} %add_rsqrt_fusion), kind=kOutput, calls=%fused_computation.19 | convolution fusion | flops 4836556800 | bytes 23350272 | tf_op jit(solution)/shard_map/dot_general | solution.py:197
  19.8 0.4 copy.52
  20.2 0.5 multiply_cosine_fusion
  20.7 0.5 subtract_convert_fusion.1
  21.2 0.9 subtract_convert_fusion
  22.1 0.0 copy-start
  22.1 1.4 pad_maximum_fusion
  23.5 80.3 %attend.1 = (bf16[256,512,128]{2,1,0:T(8,128)(2,1)}, bf16[256,512,128]{2,1,0:T(8,128)(2,1)}, f32[256,16,128]{2,1,0:T(8,128)S(1)}, f32[16,256]{1,0:T(8,128)S(1)}, f32[16,256]{1,0:T(8,128)S(1)}) custom-call(s32[256]{0:T(256)S(1)} %copy-done, s32[1]{0:T(128)} %bitcast.base_ref, bf16[256,16,128]{2,1,0:T(8,128)(2,1)S(1)} %get-tuple-element.32.q_hbm, ...), custom_call_target="tpu_custom_call" | custom-call | flops 1073741824 | bytes 134217728 | tf_op jit(solution)/shard_map/attend/pallas_call | solution.py:155
  103.9 0.1 copy.33
  104.0 1.4 fusion.4
  105.3 1.2 copy.35
  106.6 1.0 collective-permute-start
  107.6 0.1 copy.34
  107.7 2.2 %collective-permute-done = f32[128,17,128]{2,0,1:T(8,128)S(1)} collective-permute-done((f32[128,17,128]{2,0,1:T(8,128)}, f32[128,17,128]{2,0,1:T(8,128)S(1)}, u32[]{:S(2)}, u32[]{:S(2)}) %collective-permute-start) | collective-permute-done | bytes 1114144 | tf_op jit(solution)/shard_map/ppermute | solution.py:189
  109.9 0.1 copy.48
  110.1 0.1 copy.40
  110.2 0.1 copy.37
  110.3 0.1 copy.39
  110.4 0.1 slice.101
  110.5 1.5 fusion.7
  112.0 0.1 fusion.9
  112.1 0.1 copy.42
  112.2 2.8 %collective-permute-start.1 = (f32[64,17,128]{2,0,1:T(8,128)S(1)}, f32[64,17,128]{2,0,1:T(8,128)S(1)}, u32[]{:S(2)}, u32[]{:S(2)}) collective-permute-start(f32[64,17,128]{2,0,1:T(8,128)S(1)} %copy.42), channel_id=1, source_target_pairs={{0,2},{1,3},{2,0},{3,1},{4,6},{5,7},{6,4},{7,5}} | collective-permute-start | bytes 1671176 | tf_op jit(solution)/shard_map/ppermute | solution.py:189
  115.0 0.1 copy.41
  115.1 12.8 %collective-permute-done.1 = f32[64,17,128]{2,0,1:T(8,128)S(1)} collective-permute-done((f32[64,17,128]{2,0,1:T(8,128)S(1)}, f32[64,17,128]{2,0,1:T(8,128)S(1)}, u32[]{:S(2)}, u32[]{:S(2)}) %collective-permute-start.1) | collective-permute-done | bytes 557088 | tf_op jit(solution)/shard_map/ppermute | solution.py:189
  127.9 0.1 copy.50
  128.1 0.1 copy.44
  128.1 0.1 copy.47
  128.2 0.1 copy.46
  128.4 0.5 fusion.12
  128.8 0.0 copy-start.5
  128.9 8.1 %fusion.13 = f32[64,4608]{1,0:T(8,128)S(1)} fusion(bf16[2048,4608]{1,0:T(8,128)(2,1)} %param.16, bf16[8,8,16,128]{3,2,1,0:T(8,128)(2,1)S(1)} %bitcast.42), kind=kOutput, calls=%fused_computation.42 | convolution fusion | flops 1207959552 | bytes 20316160 | tf_op jit(solution)/shard_map/dot_general | solution.py:242
  137.0 1.8 collective-permute-start.2
  138.8 25.6 %collective-permute-done.2 = f32[64,4608]{1,0:T(8,128)S(1)} collective-permute-done((f32[64,4608]{1,0:T(8,128)S(1)}, f32[64,4608]{1,0:T(8,128)S(1)}, u32[]{:S(2)}, u32[]{:S(2)}) %collective-permute-start.2) | collective-permute-done | bytes 1179680 | tf_op jit(solution)/shard_map/ppermute | solution.py:189
  164.5 0.3 multiply_reduce_fusion
  164.7 0.2 multiply_multiply_fusion
  164.9 1.5 collective-permute-start.3
  166.4 25.1 %collective-permute-done.3 = f32[64,4608]{1,0:T(8,128)} collective-permute-done((f32[64,4608]{1,0:T(8,128)S(1)}, f32[64,4608]{1,0:T(8,128)}, u32[]{:S(2)}, u32[]{:S(2)}) %collective-permute-start.3) | collective-permute-done | bytes 1179680 | tf_op jit(solution)/shard_map/ppermute | solution.py:189
  191.5 3.2 %maximum_select_fusion.1 = f32[128,4608]{1,0:T(8,128)} fusion(f32[64,4608]{1,0:T(8,128)} %collective-permute-done.3, f32[64,4608]{1,0:T(8,128)S(1)} %multiply_multiply_fusion, pred[]{:T(512)S(6)} %eq.9), kind=kLoop, calls=%fused_computation.12 | loop fusion | flops 1769472 | bytes 4718593 | tf_op jit(solution)/shard_map/jit(_where)/select_n | solution.py:246
  194.8 0.0 collective-permute-start.4
  194.8 4.5 %collective-permute-done.4 = f32[128,4608]{1,0:T(8,128)} collective-permute-done((f32[128,4608]{1,0:T(8,128)}, f32[128,4608]{1,0:T(8,128)}, u32[]{:S(2)}, u32[]{:S(2)}) %collective-permute-start.4) | collective-permute-done | bytes 2359328 | tf_op jit(solution)/shard_map/ppermute | solution.py:189
  199.3 0.0 copy-done.2
  199.3 5.3 %fusion.3 = bf16[256,4608]{1,0:T(8,128)(2,1)} fusion(bf16[256,4608]{1,0:T(8,128)(2,1)S(1)} %copy-done.2, f32[128,4608]{1,0:T(8,128)} %collective-permute-done.4, f32[128,4608]{1,0:T(8,128)} %maximum_select_fusion.1, pred[]{:T(512)S(6)} %eq.8), kind=kLoop, calls=%fused_computation.6 | loop fusion | flops 7077888 | bytes 9437185 | tf_op jit(solution)/shard_map/convert_element_type | solution.py:249
  (30 shorter events, 0.3 us)
Async XLA Ops:
  0.6 3.3 %copy-start.1 = (bf16[256,4608]{1,0:T(8,128)(2,1)S(1)}, bf16[256,4608]{1,0:T(8,128)(2,1)}, u32[]{:S(2)}) copy-start(bf16[256,4608]{1,0:T(8,128)(2,1)} %param.10) | copy-start | bytes 7077892
  0.6 3.3 %copy-start.4 = (f32[4608]{0:T(1024)S(1)}, f32[4608]{0:T(1024)}, u32[]{:S(2)}) copy-start(f32[4608]{0:T(1024)} %param.12) | copy-start | bytes 55300
  1.5 9.2 %slice-start.5 = ((s8[9437184]{0:T(1024)(128)(4,1)}), s8[4194304]{0:T(1024)(128)(4,1)S(1)}, s32[]{:S(2)}) async-start(s8[9437184]{0:T(1024)(128)(4,1)} %bitcast.58), calls=%async_computation.5 | async-start | bytes 8388608
  3.9 6.8 %slice-start.6 = ((s8[9437184]{0:T(1024)(128)(4,1)}), s8[4194304]{0:T(1024)(128)(4,1)S(1)}, s32[]{:S(2)}) async-start(s8[9437184]{0:T(1024)(128)(4,1)} %bitcast.58), calls=%async_computation.6 | async-start | bytes 8388608
  3.9 6.8 %slice-start.7 = ((s8[9437184]{0:T(1024)(128)(4,1)}), s8[1048576]{0:T(1024)(128)(4,1)S(1)}, s32[]{:S(2)}) async-start(s8[9437184]{0:T(1024)(128)(4,1)} %bitcast.58), calls=%async_computation.7 | async-start | bytes 2097152
  4.0 9.7 %slice-start = ((s8[18874368]{0:T(1024)(128)(4,1)}), s8[2097152]{0:T(1024)(128)(4,1)S(1)}, s32[]{:S(2)}) async-start(s8[18874368]{0:T(1024)(128)(4,1)} %bitcast.56), calls=%async_computation | async-start | bytes 4194304
  4.0 9.7 %slice-start.1 = ((s8[18874368]{0:T(1024)(128)(4,1)}), s8[4194304]{0:T(1024)(128)(4,1)S(1)}, s32[]{:S(2)}) async-start(s8[18874368]{0:T(1024)(128)(4,1)} %bitcast.56), calls=%async_computation.1 | async-start | bytes 8388608
  4.0 9.7 %slice-start.2 = ((s8[18874368]{0:T(1024)(128)(4,1)}), s8[4194304]{0:T(1024)(128)(4,1)S(1)}, s32[]{:S(2)}) async-start(s8[18874368]{0:T(1024)(128)(4,1)} %bitcast.56), calls=%async_computation.2 | async-start | bytes 8388608
  10.8 2.9 %slice-start.3 = ((s8[18874368]{0:T(1024)(128)(4,1)}), s8[4194304]{0:T(1024)(128)(4,1)S(1)}, s32[]{:S(2)}) async-start(s8[18874368]{0:T(1024)(128)(4,1)} %bitcast.56), calls=%async_computation.3 | async-start | bytes 8388608
  10.8 3.9 %slice-start.4 = ((s8[18874368]{0:T(1024)(128)(4,1)}), s8[4194304]{0:T(1024)(128)(4,1)S(1)}, s32[]{:S(2)}) async-start(s8[18874368]{0:T(1024)(128)(4,1)} %bitcast.56), calls=%async_computation.4 | async-start | bytes 8388608
  22.1 1.4 copy-start
  105.3 2.2 %copy-start.3 = (f32[128,17,128]{2,1,0:T(8,128)S(1)}, f32[128,17,128]{2,1,0:T(8,128)}, u32[]{:S(2)}) copy-start(f32[128,17,128]{2,1,0:T(8,128)} %get-tuple-element.25) | copy-start | bytes 3342340
  106.6 3.3 %collective-permute-start = (f32[128,17,128]{2,0,1:T(8,128)}, f32[128,17,128]{2,0,1:T(8,128)S(1)}, u32[]{:S(2)}, u32[]{:S(2)}) collective-permute-start(f32[128,17,128]{2,0,1:T(8,128)} %copy.35), channel_id=1, source_target_pairs={{0,1},{1,0},{2,3},{3,2},{4,5},{5,4},{6,7},{7,6}} | collective-permute-start | bytes 3342344 | tf_op jit(solution)/shard_map/ppermute | solution.py:189
  112.2 15.7 %collective-permute-start.1 = (f32[64,17,128]{2,0,1:T(8,128)S(1)}, f32[64,17,128]{2,0,1:T(8,128)S(1)}, u32[]{:S(2)}, u32[]{:S(2)}) collective-permute-start(f32[64,17,128]{2,0,1:T(8,128)S(1)} %copy.42), channel_id=1, source_target_pairs={{0,2},{1,3},{2,0},{3,1},{4,6},{5,7},{6,4},{7,5}} | collective-permute-start | bytes 1671176 | tf_op jit(solution)/shard_map/ppermute | solution.py:189
  128.8 10.0 %copy-start.5 = (f32[4608]{0:T(1024)S(1)}, f32[4608]{0:T(1024)}, u32[]{:S(2)}) copy-start(f32[4608]{0:T(1024)} %param.17) | copy-start | bytes 55300
  137.0 27.5 %collective-permute-start.2 = (f32[64,4608]{1,0:T(8,128)S(1)}, f32[64,4608]{1,0:T(8,128)S(1)}, u32[]{:S(2)}, u32[]{:S(2)}) collective-permute-start(f32[64,4608]{1,0:T(8,128)S(1)} %fusion.13), channel_id=1, source_target_pairs={{0,4},{4,0},{1,5},{5,1},{2,6},{6,2},{3,7},{7,3}} | collective-permute-start | bytes 3538952 | tf_op jit(solution)/shard_map/ppermute | solution.py:189
  164.9 26.6 %collective-permute-start.3 = (f32[64,4608]{1,0:T(8,128)S(1)}, f32[64,4608]{1,0:T(8,128)}, u32[]{:S(2)}, u32[]{:S(2)}) collective-permute-start(f32[64,4608]{1,0:T(8,128)S(1)} %multiply_multiply_fusion), channel_id=1, source_target_pairs={{0,2},{1,3},{2,0},{3,1},{4,6},{5,7},{6,4},{7,5}} | collective-permute-start | bytes 3538952 | tf_op jit(solution)/shard_map/ppermute | solution.py:189
  166.4 32.9 %copy-start.2 = (bf16[256,4608]{1,0:T(8,128)(2,1)S(1)}, bf16[256,4608]{1,0:T(8,128)(2,1)}, u32[]{:S(2)}) copy-start(bf16[256,4608]{1,0:T(8,128)(2,1)} %param.10) | copy-start | bytes 7077892
  194.8 4.5 %collective-permute-start.4 = (f32[128,4608]{1,0:T(8,128)}, f32[128,4608]{1,0:T(8,128)}, u32[]{:S(2)}, u32[]{:S(2)}) collective-permute-start(f32[128,4608]{1,0:T(8,128)} %maximum_select_fusion.1), channel_id=1, source_target_pairs={{0,1},{1,0},{2,3},{3,2},{4,5},{5,4},{6,7},{7,6}} | collective-permute-start | bytes 7077896 | tf_op jit(solution)/shard_map/ppermute | solution.py:189

commit v2 on v1

--- a/solution.py
+++ b/solution.py
@@ -12,9 +12,11 @@
 NORM_EPS = 1e-6
 LOG2E = 1.4426950408889634
 
-ROWS_STEP = 8
-SLOTS = 6
-AHEAD = 4
+ROWS_STEP = 16
+SLOTS = 5
+AHEAD = 3
+LAG_SOFT = 2
+LAG_OUT = 4
 
 
 def rms_scale(tensor, gain_w):
@@ -36,7 +38,7 @@
 
 def attend_kernel(n_steps, first_row, kv_heads, seq_block, pos_ref, base_ref, q_hbm, kn_hbm, vn_hbm, k_hbm, v_hbm,
                   *rest):
-    (ko_hbm, vo_hbm, o_hbm, m_ref, l_ref, kbuf, vbuf, qbuf, knbuf, vnbuf, obuf, key_ref, in_sem, out_sem, o_sem) = rest[-15:]
+    (ko_hbm, vo_hbm, o_hbm, m_ref, l_ref, kbuf, vbuf, qbuf, knbuf, vnbuf, obuf, key_ref, s_ref, p_ref, in_sem, out_sem, o_sem) = rest[-17:]
     step_rows = ROWS_STEP
     heads, head_dim = qbuf.shape[2], qbuf.shape[3]
     cols = seq_block * kv_heads
@@ -81,13 +83,12 @@
 
         for r in range(step_rows):
             local = pos_ref[first_row + step * step_rows + r] - base
-
-            @pl.when((local >= 0) & (local < seq_block))
-            def _():
-                pair = pl.ds(pl.multiple_of((local // 2) * (2 * kv_heads), 2 * kv_heads), 2 * kv_heads)
-                hit = half_id == lax.rem(local, 2)
-                kbuf[slot, r, pair, :] = jnp.where(hit, knbuf[slot, r], kbuf[slot, r, pair, :])
-                vbuf[slot, r, pair, :] = jnp.where(hit, vnbuf[slot, r], vbuf[slot, r, pair, :])
+            inside = (local >= 0) & (local < seq_block)
+            at = jnp.clip(local, 0, seq_block - 1)
+            pair = pl.ds(pl.multiple_of((at // 2) * (2 * kv_heads), 2 * kv_heads), 2 * kv_heads)
+            hit = half_id == jnp.where(inside, lax.rem(at, 2), 2)
+            kbuf[slot, r, pair, :] = jnp.where(hit, knbuf[slot, r], kbuf[slot, r, pair, :])
+            vbuf[slot, r, pair, :] = jnp.where(hit, vnbuf[slot, r], vbuf[slot, r, pair, :])
 
         @pl.when(step >= 2)
         def _():
@@ -95,24 +96,32 @@
 
         m_all = m_ref[...]
         l_all = l_ref[...]
-        for r in range(step_rows):
-            local = pos_ref[first_row + step * step_rows + r] - base
-            raw = lax.dot_general(qbuf[slot, r], kbuf[slot, r], (((1,), (1,)), ((), ())),
-                                  preferred_element_type=jnp.float32)
-            seen = key_ref[...] < (local + 1) * kv_heads
-            soft = jnp.where(seen, jnp.tanh(raw * scale), -4.0)
-            top = jnp.maximum(jnp.max(soft, axis=-1, keepdims=True), -1.0)
-            weight = jnp.exp2((soft - top) * (SOFT_CAP * LOG2E))
-            total = jnp.sum(weight, axis=-1, keepdims=True)
-            weight = weight.astype(jnp.bfloat16)
-            half = cols // 2
-            left = jnp.concatenate([weight[:, :half], weight[:, half:]], axis=0)
-            right = jnp.concatenate([vbuf[slot, r, :half, :], vbuf[slot, r, half:, :]], axis=1)
-            both = jnp.dot(left, right, preferred_element_type=jnp.float32)
-            obuf[oslot, r] = both[:heads, :head_dim] + both[heads:, head_dim:]
-            here = lane_id == step * step_rows + r
-            m_all = jnp.where(here, top * SOFT_CAP, m_all)
-            l_all = jnp.where(here, total, l_all)
+        half = cols // 2
+        for tick in range(step_rows + LAG_OUT):
+            r = tick
+            if r < step_rows:
+                raw = lax.dot_general(qbuf[slot, r], kbuf[slot, r], (((1,), (1,)), ((), ())),
+                                      preferred_element_type=jnp.float32)
+                s_ref[r] = raw
+            r = tick - LAG_SOFT
+            if 0 <= r < step_rows:
+                local = pos_ref[first_row + step * step_rows + r] - base
+                seen = key_ref[...] < (local + 1) * kv_heads
+                soft = jnp.where(seen, jnp.tanh(s_ref[r] * scale), -4.0)
+                top = jnp.maximum(jnp.max(soft, axis=-1, keepdims=True), -1.0)
+                weight = jnp.exp2((soft - top) * (SOFT_CAP * LOG2E))
+                total = jnp.sum(weight, axis=-1, keepdims=True)
+                weight = weight.astype(jnp.bfloat16)
+                p_ref[r, :heads] = weight[:, :half]
+                p_ref[r, heads:] = weight[:, half:]
+                here = lane_id == step * step_rows + r
+                m_all = jnp.where(here, top * SOFT_CAP, m_all)
+                l_all = jnp.where(here, total, l_all)
+            r = tick - LAG_OUT
+            if 0 <= r < step_rows:
+                right = jnp.concatenate([vbuf[slot, r, :half, :], vbuf[slot, r, half:, :]], axis=1)
+                both = jnp.dot(p_ref[r], right, preferred_element_type=jnp.float32)
+                obuf[oslot, r] = both[:heads, :head_dim] + both[heads:, head_dim:]
         m_ref[...] = m_all
         l_ref[...] = l_all
         o_store(step, oslot).start()
@@ -168,6 +177,8 @@
             pltpu.VMEM((SLOTS, ROWS_STEP, 2 * kv_heads, head_dim), bf),
             pltpu.VMEM((2, ROWS_STEP, heads, head_dim), jnp.float32),
             pltpu.VMEM((heads, cols), jnp.int32),
+            pltpu.VMEM((ROWS_STEP, heads, cols), jnp.float32),
+            pltpu.VMEM((ROWS_STEP, 2 * heads, cols // 2), bf),
             pltpu.SemaphoreType.DMA((SLOTS, 5)),
             pltpu.SemaphoreType.DMA((SLOTS, 2)),
             pltpu.SemaphoreType.DMA((2,)),

time: 205 us -> 170 us (0.83)
  Pallas kernels: 80.3 us -> 45.8 us
    pallas_call x1, Pallas kernels: 80.3 us -> 45.8 us  [attend(): pl.pallas_call(functools.partial(attend_kernel, n_steps, first_row, kv_he...]
where the time goes in v2:
time: 170 us
  waiting for transfers between devices  70.3 us (41%)
  Pallas kernels  45.8 us (27%)
  matrix products  22.3 us (13%)
  other arithmetic  19.2 us (11%)
  starting transfers between devices  7.01 us (4%)
  local copies, waits for them, and re-layouts  4.36 us (3%)
    ppermute x5, waiting for transfers between devices, swap(): return lax.ppermute(value, axis, [(i, i ^ bit) for i in range(size)])  70.3 us
    pallas_call x1, Pallas kernels, attend(): pl.pallas_call(functools.partial(attend_kernel, n_steps, first_row, kv_he...  45.8 us
    dot_general x1, matrix products, local_step(): part = jnp.dot(attn, w_o, preferred_element_type=jnp.float32)  8.13 us
    ppermute x5, starting transfers between devices, swap(): return lax.ppermute(value, axis, [(i, i ^ bit) for i in range(size)])  7.01 us
    dot_general x1, matrix products, local_step(): jnp.dot(normed, w_v, preferred_element_type=jnp.float32)  6.48 us
    convert_element_type x1, other arithmetic, local_step(): x_out = (x_f + y4).astype(jnp.bfloat16)  5.27 us
    dot_general x1, matrix products, local_step(): q_proj = jnp.dot(normed, w_q, preferred_element_type=jnp.float32)  5.07 us
  transfers between devices with their start and end apart: 5, of which 5 were waited for; matrix products, arithmetic and copies ran while one was open for 0% of the time, Pallas kernels for 0%

profile of v2, /device:TPU:0, one launch (start us, length us, event | category | flops | bytes accessed | tf_op | source)
XLA Modules:
  0.0 170.1 jit_solution(4933919356074825972)
XLA Ops:
  0.6 0.0 copy-start.1
  0.6 0.0 copy-start.4
  0.7 0.8 convert_element_type.29
  1.5 2.4 %fusion = f32[256]{0:T(256)S(1)} fusion(bf16[256,4608]{1,0:T(8,128)(2,1)} %param.10), kind=kLoop, calls=%fused_computation.3 | loop fusion | flops 3538688 | bytes 2360320 | tf_op jit(solution)/shard_map/reduce_sum | solution.py:23
  3.9 0.0 copy-done.4
  3.9 0.0 copy-done.1
  3.9 0.0 slice-start.6
  3.9 0.0 slice-start.7
  4.0 0.0 slice-start
  4.0 0.0 slice-start.1
  4.0 0.0 slice-start.2
  4.0 6.5 %fusion.6 = bf16[32,8,8,128]{3,1,2,0:T(8,128)(2,1)S(1)} fusion(bf16[4608,1024]{1,0:T(8,128)(2,1)} %param.15, bf16[256,4608]{1,0:T(8,128)(2,1)S(1)} %copy-done.1, f32[4608]{0:T(1024)S(1)} %broadcast_add_fusion.1, f32[256]{0:T(256)S(1)} %add_rsqrt_fusion), kind=kOutput, calls=%fused_computation.24 | convolution fusion | flops 2420899840 | bytes 12340224 | tf_op jit(solution)/shard_map/dot_general | solution.py:212
  10.5 0.1 copy.54
  10.6 0.1 pad_maximum_fusion.1.vn_hbm
  10.8 0.0 slice-start.3
  10.8 0.0 slice-start.4
  10.8 2.6 %convolution_bitcast_fusion.1 = f32[32,8,8,128]{3,1,2,0:T(8,128)S(1)} fusion(bf16[4608,1024]{1,0:T(8,128)(2,1)S(1)} %bitcast.59, bf16[256,4608]{1,0:T(8,128)(2,1)S(1)} %copy-done.1, f32[4608]{0:T(1024)S(1)} %broadcast_add_fusion.1, f32[256]{0:T(256)S(1)} %add_rsqrt_fusion), kind=kOutput, calls=%fused_computation.22 | convolution fusion | flops 2420637696 | bytes 12864512 | tf_op jit(solution)/shard_map/dot_general | solution.py:210
  13.4 0.2 copy.53
  13.7 1.0 slice-done.4
  14.7 5.1 %convolution_bitcast_fusion = f32[32,8,16,128]{3,1,2,0:T(8,128)S(1)} fusion(bf16[4608,2048]{1,0:T(8,128)(2,1)S(1)} %bitcast.57, bf16[256,4608]{1,0:T(8,128)(2,1)S(1)} %copy-done.1, f32[4608]{0:T(1024)S(1)} %broadcast_add_fusion.1, f32[256]{0:T(256)S(1)} %add_rsqrt_fusion), kind=kOutput, calls=%fused_computation.19 | convolution fusion | flops 4836556800 | bytes 23350272 | tf_op jit(solution)/shard_map/dot_general | solution.py:208
  19.8 0.4 copy.52
  20.2 0.5 multiply_cosine_fusion
  20.7 0.5 subtract_convert_fusion.1
  21.2 0.9 subtract_convert_fusion
  22.1 0.0 copy-start
  22.1 1.4 pad_maximum_fusion
  23.5 45.8 %attend.1 = (bf16[256,512,128]{2,1,0:T(8,128)(2,1)}, bf16[256,512,128]{2,1,0:T(8,128)(2,1)}, f32[256,16,128]{2,1,0:T(8,128)S(1)}, f32[16,256]{1,0:T(8,128)S(1)}, f32[16,256]{1,0:T(8,128)S(1)}) custom-call(s32[256]{0:T(256)S(1)} %copy-done, s32[1]{0:T(128)} %bitcast.base_ref, bf16[256,16,128]{2,1,0:T(8,128)(2,1)S(1)} %get-tuple-element.32.q_hbm, ...), custom_call_target="tpu_custom_call" | custom-call | flops 1073741824 | bytes 134217728 | tf_op jit(solution)/shard_map/attend/pallas_call | solution.py:164
  69.4 0.1 copy.33
  69.5 1.4 fusion.4
  70.8 1.2 copy.35
  72.1 0.9 collective-permute-start
  72.9 0.0 copy-done.3
  73.0 0.1 copy.34
  73.1 2.2 %collective-permute-done = f32[128,17,128]{2,0,1:T(8,128)S(1)} collective-permute-done((f32[128,17,128]{2,0,1:T(8,128)}, f32[128,17,128]{2,0,1:T(8,128)S(1)}, u32[]{:S(2)}, u32[]{:S(2)}) %collective-permute-start) | collective-permute-done | bytes 1114144 | tf_op jit(solution)/shard_map/ppermute | solution.py:200
  75.3 0.1 copy.48
  75.5 0.1 copy.40
  75.6 0.1 copy.37
  75.7 0.1 copy.39
  75.8 0.1 slice.101
  75.9 1.5 fusion.7
  77.4 0.1 fusion.9
  77.5 0.1 copy.42
  77.6 2.9 %collective-permute-start.1 = (f32[64,17,128]{2,0,1:T(8,128)S(1)}, f32[64,17,128]{2,0,1:T(8,128)S(1)}, u32[]{:S(2)}, u32[]{:S(2)}) collective-permute-start(f32[64,17,128]{2,0,1:T(8,128)S(1)} %copy.42), channel_id=1, source_target_pairs={{0,2},{1,3},{2,0},{3,1},{4,6},{5,7},{6,4},{7,5}} | collective-permute-start | bytes 1671176 | tf_op jit(solution)/shard_map/ppermute | solution.py:200
  80.5 0.1 copy.41
  80.6 12.8 %collective-permute-done.1 = f32[64,17,128]{2,0,1:T(8,128)S(1)} collective-permute-done((f32[64,17,128]{2,0,1:T(8,128)S(1)}, f32[64,17,128]{2,0,1:T(8,128)S(1)}, u32[]{:S(2)}, u32[]{:S(2)}) %collective-permute-start.1) | collective-permute-done | bytes 557088 | tf_op jit(solution)/shard_map/ppermute | solution.py:200
  93.4 0.1 copy.50
  93.6 0.1 copy.44
  93.7 0.1 copy.47
  93.7 0.1 copy.46
  93.9 0.5 fusion.12
  94.4 0.0 copy-start.5
  94.4 8.1 %fusion.13 = f32[64,4608]{1,0:T(8,128)S(1)} fusion(bf16[2048,4608]{1,0:T(8,128)(2,1)} %param.16, bf16[8,8,16,128]{3,2,1,0:T(8,128)(2,1)S(1)} %bitcast.42), kind=kOutput, calls=%fused_computation.42 | convolution fusion | flops 1207959552 | bytes 20316160 | tf_op jit(solution)/shard_map/dot_general | solution.py:253
  102.5 1.8 %collective-permute-start.2 = (f32[64,4608]{1,0:T(8,128)S(1)}, f32[64,4608]{1,0:T(8,128)S(1)}, u32[]{:S(2)}, u32[]{:S(2)}) collective-permute-start(f32[64,4608]{1,0:T(8,128)S(1)} %fusion.13), channel_id=1, source_target_pairs={{0,4},{4,0},{1,5},{5,1},{2,6},{6,2},{3,7},{7,3}} | collective-permute-start | bytes 3538952 | tf_op jit(solution)/shard_map/ppermute | solution.py:200
  104.3 0.0 copy-done.5
  104.3 25.7 %collective-permute-done.2 = f32[64,4608]{1,0:T(8,128)S(1)} collective-permute-done((f32[64,4608]{1,0:T(8,128)S(1)}, f32[64,4608]{1,0:T(8,128)S(1)}, u32[]{:S(2)}, u32[]{:S(2)}) %collective-permute-start.2) | collective-permute-done | bytes 1179680 | tf_op jit(solution)/shard_map/ppermute | solution.py:200
  130.0 0.3 multiply_reduce_fusion
  130.3 0.2 multiply_multiply_fusion
  130.4 1.5 collective-permute-start.3
  131.9 25.1 %collective-permute-done.3 = f32[64,4608]{1,0:T(8,128)} collective-permute-done((f32[64,4608]{1,0:T(8,128)S(1)}, f32[64,4608]{1,0:T(8,128)}, u32[]{:S(2)}, u32[]{:S(2)}) %collective-permute-start.3) | collective-permute-done | bytes 1179680 | tf_op jit(solution)/shard_map/ppermute | solution.py:200
  157.0 3.2 %maximum_select_fusion.1 = f32[128,4608]{1,0:T(8,128)} fusion(f32[64,4608]{1,0:T(8,128)} %collective-permute-done.3, f32[64,4608]{1,0:T(8,128)S(1)} %multiply_multiply_fusion, pred[]{:T(512)S(6)} %eq.9), kind=kLoop, calls=%fused_computation.12 | loop fusion | flops 1769472 | bytes 4718593 | tf_op jit(solution)/shard_map/jit(_where)/select_n | solution.py:257
  160.3 0.0 collective-permute-start.4
  160.3 4.5 %collective-permute-done.4 = f32[128,4608]{1,0:T(8,128)} collective-permute-done((f32[128,4608]{1,0:T(8,128)}, f32[128,4608]{1,0:T(8,128)}, u32[]{:S(2)}, u32[]{:S(2)}) %collective-permute-start.4) | collective-permute-done | bytes 2359328 | tf_op jit(solution)/shard_map/ppermute | solution.py:200
  164.8 0.0 copy-done.2
  164.8 5.3 %fusion.3 = bf16[256,4608]{1,0:T(8,128)(2,1)} fusion(bf16[256,4608]{1,0:T(8,128)(2,1)S(1)} %copy-done.2, f32[128,4608]{1,0:T(8,128)} %collective-permute-done.4, f32[128,4608]{1,0:T(8,128)} %maximum_select_fusion.1, pred[]{:T(512)S(6)} %eq.8), kind=kLoop, calls=%fused_computation.6 | loop fusion | flops 7077888 | bytes 9437185 | tf_op jit(solution)/shard_map/convert_element_type | solution.py:260
  (30 shorter events, 0.3 us)
Async XLA Ops:
  0.6 3.3 %copy-start.1 = (bf16[256,4608]{1,0:T(8,128)(2,1)S(1)}, bf16[256,4608]{1,0:T(8,128)(2,1)}, u32[]{:S(2)}) copy-start(bf16[256,4608]{1,0:T(8,128)(2,1)} %param.10) | copy-start | bytes 7077892
  0.6 3.3 %copy-start.4 = (f32[4608]{0:T(1024)S(1)}, f32[4608]{0:T(1024)}, u32[]{:S(2)}) copy-start(f32[4608]{0:T(1024)} %param.12) | copy-start | bytes 55300
  1.5 9.2 %slice-start.5 = ((s8[9437184]{0:T(1024)(128)(4,1)}), s8[4194304]{0:T(1024)(128)(4,1)S(1)}, s32[]{:S(2)}) async-start(s8[9437184]{0:T(1024)(128)(4,1)} %bitcast.58), calls=%async_computation.5 | async-start | bytes 8388608
  3.9 6.8 %slice-start.6 = ((s8[9437184]{0:T(1024)(128)(4,1)}), s8[4194304]{0:T(1024)(128)(4,1)S(1)}, s32[]{:S(2)}) async-start(s8[9437184]{0:T(1024)(128)(4,1)} %bitcast.58), calls=%async_computation.6 | async-start | bytes 8388608
  3.9 6.8 %slice-start.7 = ((s8[9437184]{0:T(1024)(128)(4,1)}), s8[1048576]{0:T(1024)(128)(4,1)S(1)}, s32[]{:S(2)}) async-start(s8[9437184]{0:T(1024)(128)(4,1)} %bitcast.58), calls=%async_computation.7 | async-start | bytes 2097152
  4.0 9.7 %slice-start = ((s8[18874368]{0:T(1024)(128)(4,1)}), s8[2097152]{0:T(1024)(128)(4,1)S(1)}, s32[]{:S(2)}) async-start(s8[18874368]{0:T(1024)(128)(4,1)} %bitcast.56), calls=%async_computation | async-start | bytes 4194304
  4.0 9.7 %slice-start.1 = ((s8[18874368]{0:T(1024)(128)(4,1)}), s8[4194304]{0:T(1024)(128)(4,1)S(1)}, s32[]{:S(2)}) async-start(s8[18874368]{0:T(1024)(128)(4,1)} %bitcast.56), calls=%async_computation.1 | async-start | bytes 8388608
  4.0 9.7 %slice-start.2 = ((s8[18874368]{0:T(1024)(128)(4,1)}), s8[4194304]{0:T(1024)(128)(4,1)S(1)}, s32[]{:S(2)}) async-start(s8[18874368]{0:T(1024)(128)(4,1)} %bitcast.56), calls=%async_computation.2 | async-start | bytes 8388608
  10.8 2.9 %slice-start.3 = ((s8[18874368]{0:T(1024)(128)(4,1)}), s8[4194304]{0:T(1024)(128)(4,1)S(1)}, s32[]{:S(2)}) async-start(s8[18874368]{0:T(1024)(128)(4,1)} %bitcast.56), calls=%async_computation.3 | async-start | bytes 8388608
  10.8 3.9 %slice-start.4 = ((s8[18874368]{0:T(1024)(128)(4,1)}), s8[4194304]{0:T(1024)(128)(4,1)S(1)}, s32[]{:S(2)}) async-start(s8[18874368]{0:T(1024)(128)(4,1)} %bitcast.56), calls=%async_computation.4 | async-start | bytes 8388608
  22.1 1.4 copy-start
  70.8 2.1 %copy-start.3 = (f32[128,17,128]{2,1,0:T(8,128)S(1)}, f32[128,17,128]{2,1,0:T(8,128)}, u32[]{:S(2)}) copy-start(f32[128,17,128]{2,1,0:T(8,128)} %get-tuple-element.25) | copy-start | bytes 3342340
  72.1 3.2 %collective-permute-start = (f32[128,17,128]{2,0,1:T(8,128)}, f32[128,17,128]{2,0,1:T(8,128)S(1)}, u32[]{:S(2)}, u32[]{:S(2)}) collective-permute-start(f32[128,17,128]{2,0,1:T(8,128)} %copy.35), channel_id=1, source_target_pairs={{0,1},{1,0},{2,3},{3,2},{4,5},{5,4},{6,7},{7,6}} | collective-permute-start | bytes 3342344 | tf_op jit(solution)/shard_map/ppermute | solution.py:200
  77.6 15.8 %collective-permute-start.1 = (f32[64,17,128]{2,0,1:T(8,128)S(1)}, f32[64,17,128]{2,0,1:T(8,128)S(1)}, u32[]{:S(2)}, u32[]{:S(2)}) collective-permute-start(f32[64,17,128]{2,0,1:T(8,128)S(1)} %copy.42), channel_id=1, source_target_pairs={{0,2},{1,3},{2,0},{3,1},{4,6},{5,7},{6,4},{7,5}} | collective-permute-start | bytes 1671176 | tf_op jit(solution)/shard_map/ppermute | solution.py:200
  94.4 9.9 %copy-start.5 = (f32[4608]{0:T(1024)S(1)}, f32[4608]{0:T(1024)}, u32[]{:S(2)}) copy-start(f32[4608]{0:T(1024)} %param.17) | copy-start | bytes 55300
  102.5 27.5 %collective-permute-start.2 = (f32[64,4608]{1,0:T(8,128)S(1)}, f32[64,4608]{1,0:T(8,128)S(1)}, u32[]{:S(2)}, u32[]{:S(2)}) collective-permute-start(f32[64,4608]{1,0:T(8,128)S(1)} %fusion.13), channel_id=1, source_target_pairs={{0,4},{4,0},{1,5},{5,1},{2,6},{6,2},{3,7},{7,3}} | collective-permute-start | bytes 3538952 | tf_op jit(solution)/shard_map/ppermute | solution.py:200
  130.4 26.6 %collective-permute-start.3 = (f32[64,4608]{1,0:T(8,128)S(1)}, f32[64,4608]{1,0:T(8,128)}, u32[]{:S(2)}, u32[]{:S(2)}) collective-permute-start(f32[64,4608]{1,0:T(8,128)S(1)} %multiply_multiply_fusion), channel_id=1, source_target_pairs={{0,2},{1,3},{2,0},{3,1},{4,6},{5,7},{6,4},{7,5}} | collective-permute-start | bytes 3538952 | tf_op jit(solution)/shard_map/ppermute | solution.py:200
  131.9 32.8 %copy-start.2 = (bf16[256,4608]{1,0:T(8,128)(2,1)S(1)}, bf16[256,4608]{1,0:T(8,128)(2,1)}, u32[]{:S(2)}) copy-start(bf16[256,4608]{1,0:T(8,128)(2,1)} %param.10) | copy-start | bytes 7077892
  160.3 4.5 %collective-permute-start.4 = (f32[128,4608]{1,0:T(8,128)}, f32[128,4608]{1,0:T(8,128)}, u32[]{:S(2)}, u32[]{:S(2)}) collective-permute-start(f32[128,4608]{1,0:T(8,128)} %maximum_select_fusion.1), channel_id=1, source_target_pairs={{0,1},{1,0},{2,3},{3,2},{4,5},{5,4},{6,7},{7,6}} | collective-permute-start | bytes 7077896 | tf_op jit(solution)/shard_map/ppermute | solution.py:200

commit v3 on v2

--- a/solution.py
+++ b/solution.py
@@ -191,13 +191,192 @@
     )(pos, base, q, kn, vn, k_cache, v_cache, *extra)
 
 
+def merge_kernel(halves, sp_axis, tp_axis, o_ref, m_ref, l_ref, x_ref, wpost_ref, wo_hbm, out_ref,
+                 wo, scaled, stats, core_in, x_in, lhs, y_out, y_in, sums, far_sum,
+                 w_sem, st_send, st_recv, c_send, c_recv, r_send, r_recv, y_send, y_recv, g_send, g_recv,
+                 d_send, d_recv, f_send, f_recv):
+    sp = lax.axis_index(sp_axis)
+    tp = lax.axis_index(tp_axis)
+    core = lax.rem(sp, 2)
+    xpos = sp // 2
+    heads = m_ref.shape[0]
+    rows, width = x_ref.shape
+    quarter = rows // 4
+    part = quarter // halves
+    q_rows = quarter * heads
+    h_rows = part * heads
+    n_chunks = wo.shape[0]
+    chunk = width // n_chunks
+    core_peer = {sp_axis: 2 * xpos + (1 - core)}
+    x_peer = {sp_axis: 2 * (1 - xpos) + core}
+    far_peer = {sp_axis: 2 * (1 - xpos) + (1 - core)}
+    y_peer = {tp_axis: 1 - tp}
+    mesh_id = pl.DeviceIdType.MESH
+
+    def remote(src, dst, send, recv, peer):
+        return pltpu.make_async_remote_copy(src_ref=src, dst_ref=dst, send_sem=send, recv_sem=recv,
+                                            device_id=peer, device_id_type=mesh_id)
+
+    def w_load(n):
+        return pltpu.make_async_copy(wo_hbm.at[:, pl.ds(n * chunk, chunk)], wo.at[n], w_sem.at[n])
+
+    for n in range(n_chunks):
+        w_load(n).start()
+    barrier = pltpu.get_barrier_semaphore()
+    for peer in (core_peer, x_peer, far_peer, y_peer):
+        pl.semaphore_signal(barrier, inc=1, device_id=peer, device_id_type=mesh_id)
+    pl.semaphore_wait(barrier, 4)
+
+    stats[sp, :heads] = m_ref[...]
+    stats[sp, heads:] = l_ref[...]
+    st = [remote(stats.at[sp], stats.at[sp], st_send.at[i], st_recv.at[i], peer)
+          for i, peer in enumerate((core_peer, x_peer, far_peer))]
+    for copy in st:
+        copy.start()
+    for copy in st:
+        copy.wait()
+    tops = [stats[j, :heads] for j in range(4)]
+    top = jnp.maximum(jnp.maximum(tops[0], tops[1]), jnp.maximum(tops[2], tops[3]))
+    total = sum(stats[j, heads:] * jnp.exp(tops[j] - top) for j in range(4))
+    factor = jnp.exp(m_ref[...] - top) / total
+    for b in range(rows):
+        at = pl.ds((b % quarter) * heads, heads)
+        scaled[b // quarter, at, :] = o_ref[b * heads:(b + 1) * heads, :] * factor[:, b:b + 1]
+
+    q_own = 2 * xpos + core
+    q_far = 2 * (1 - xpos) + core
+    p_own = 2 * xpos + (1 - core)
+    p_far = 2 * (1 - xpos) + (1 - core)
+    to_core = [remote(scaled.at[p_far], core_in.at[0], c_send.at[0], c_recv.at[0], core_peer),
+               remote(scaled.at[p_own], core_in.at[1], c_send.at[1], c_recv.at[1], core_peer)]
+    for copy in to_core:
+        copy.start()
+    to_core[0].wait_recv()
+    to_x = []
+    for i in range(halves):
+        at = pl.ds(i * h_rows, h_rows)
+        far_sum[at, :] = scaled[q_far, at, :] + core_in[0, at, :]
+        copy = remote(far_sum.at[at], x_in.at[at], r_send.at[i], r_recv.at[i], x_peer)
+        copy.start()
+        to_x.append(copy)
+    to_core[1].wait_recv()
+    for copy in to_core:
+        copy.wait_send()
+
+    to_y = []
+    for i in range(halves):
+        to_x[i].wait_recv()
+        for h in range(heads):
+            at = pl.ds(i * h_rows + h, part, stride=heads)
+            value = (scaled[q_own, at, :] + core_in[1, at, :]) + x_in[at, :]
+            lhs[pl.ds(i * part, part), h * 128:(h + 1) * 128] = value.astype(jnp.bfloat16)
+        at = pl.ds(i * part, part)
+
+        def project(n, carry):
+            if i == 0:
+                w_load(n).wait()
+            y_out[n, at, :] = jnp.dot(lhs[at, :], wo[n], preferred_element_type=jnp.float32)
+            remote(y_out.at[n, at], y_in.at[n, at], y_send.at[i, n], y_recv.at[i, n], y_peer).start()
+            return carry
+
+        lax.fori_loop(0, n_chunks, project, 0)
+
+    own = sums.at[sp]
+
+    def piece(i, n):
+        return pl.ds(i * part, part), pl.ds(n * chunk, chunk)
+
+    def to_x_gather(i, n):
+        r, c = piece(i, n)
+        return remote(sums.at[sp, n, r], sums.at[sp, n, r], g_send.at[i, n], g_recv.at[i, n], x_peer)
+
+    def to_core_gather(i, n):
+        r, c = piece(i, n)
+        return remote(sums.at[sp, n, r], sums.at[sp, n, r], d_send.at[i, n], d_recv.at[i, n], core_peer)
+
+    def relay(i, n):
+        r, c = piece(i, n)
+        other = 2 * (1 - xpos) + core
+        return remote(sums.at[other, n, r], sums.at[other, n, r], f_send.at[i, n], f_recv.at[i, n], core_peer)
+
+    order = [(i, n) for i in range(halves) for n in range(n_chunks)]
+    for t in range(len(order) + 1):
+        if t < len(order):
+            i, n = order[t]
+            r, c = piece(i, n)
+            remote(y_out.at[n, r], y_in.at[n, r], y_send.at[i, n], y_recv.at[i, n], y_peer).wait()
+            sums[sp, n, r, :] = y_out[n, r, :] + y_in[n, r, :]
+            to_x_gather(i, n).start()
+            to_core_gather(i, n).start()
+        if t >= 1:
+            i, n = order[t - 1]
+            to_x_gather(i, n).wait_recv()
+            relay(i, n).start()
+    for i, n in order:
+        to_x_gather(i, n).wait_send()
+        to_core_gather(i, n).wait()
+        relay(i, n).wait()
+    for copy in to_x:
+        copy.wait_send()
+
+    block = 16
+    for q in range(4):
+        def finish(k, carry):
+            at = pl.ds(pl.multiple_of(k * block, block), block)
+            out_at = pl.ds(pl.multiple_of(q * quarter + k * block, block), block)
+            square = jnp.zeros((block, 1), jnp.float32)
+            for n in range(n_chunks):
+                u = sums[q, n, at, :]
+                square = square + jnp.sum(u * u, axis=-1, keepdims=True)
+            inv = lax.rsqrt(square * (1.0 / width) + NORM_EPS)
+            for n in range(n_chunks):
+                col = slice(n * chunk, (n + 1) * chunk)
+                u = sums[q, n, at, :]
+                y = x_ref[out_at, col].astype(jnp.float32) + u * inv * (1.0 + wpost_ref[:, col])
+                out_ref[out_at, col] = y.astype(jnp.bfloat16)
+            return carry
+        lax.fori_loop(0, quarter // block, finish, 0)
+
+
+def merge(o, m, l, x_in, w_post, w_o, halves, n_chunks):
+    rows, width = x_in.shape
+    inner = w_o.shape[0]
+    heads = m.shape[0]
+    head_dim = inner // heads
+    quarter = rows // 4
+    chunk = width // n_chunks
+    vmem = pl.BlockSpec(memory_space=pltpu.VMEM)
+    hbm = pl.BlockSpec(memory_space=pl.ANY)
+    f32 = jnp.float32
+    dma = pltpu.SemaphoreType.DMA
+    pieces = dma((halves, n_chunks))
+    return pl.pallas_call(
+        functools.partial(merge_kernel, halves, 'sp', 'tp'),
+        out_shape=jax.ShapeDtypeStruct(x_in.shape, x_in.dtype),
+        in_specs=[vmem, vmem, vmem, vmem, vmem, hbm],
+        out_specs=vmem,
+        scratch_shapes=[
+            pltpu.VMEM((n_chunks, inner, chunk), jnp.bfloat16),
+            pltpu.VMEM((4, quarter * heads, head_dim), f32),
+            pltpu.VMEM((4, 2 * heads, rows), f32),
+            pltpu.VMEM((2, quarter * heads, head_dim), f32),
+            pltpu.VMEM((quarter * heads, head_dim), f32),
+            pltpu.VMEM((quarter, inner), jnp.bfloat16),
+            pltpu.VMEM((n_chunks, quarter, chunk), f32),
+            pltpu.VMEM((n_chunks, quarter, chunk), f32),
+            pltpu.VMEM((4, n_chunks, quarter, chunk), f32),
+            pltpu.VMEM((quarter * heads, head_dim), f32),
+            dma((n_chunks,)), dma((3,)), dma((3,)), dma((2,)), dma((2,)), dma((halves,)), dma((halves,)),
+            pieces, pieces, pieces, pieces, pieces, pieces, pieces, pieces,
+        ],
+        compiler_params=pltpu.CompilerParams(vmem_limit_bytes=56 * 1024 * 1024, collective_id=0, has_side_effects=True),
+        cost_estimate=pl.CostEstimate(flops=2 * quarter * inner * width, bytes_accessed=2 * inner * width, transcendentals=0),
+        name='merge',
+    )(o, m, l, x_in, w_post, w_o)
+
+
 def solution(mesh):
     cache_spec = P('dp', 'sp', 'tp', None)
-    sp_size = mesh.shape['sp']
-    tp_size = mesh.shape['tp']
-
-    def swap(value, axis, size, bit):
-        return lax.ppermute(value, axis, [(i, i ^ bit) for i in range(size)])
 
     def local_step(x_in, cur_pos, w_pre, w_q, w_k, w_v, w_o, w_post, k_cache, v_cache):
         row_count, seq_block, kv_local, head_dim = k_cache.shape
@@ -217,47 +396,7 @@
         vc = v_cache.reshape(row_count, seq_block * kv_local, head_dim)
         k_out, v_out, o, m, l = attend(cur_pos, base, q_rot, kn2, vn2, kc, vc, None, 0, row_count)
 
-        stat = jnp.concatenate([m, l], axis=0).T[:, :, None]
-        stat = jnp.broadcast_to(stat, stat.shape[:2] + (4,)).reshape(row_count, 1, head_dim)
-        pack = jnp.concatenate([o, stat], axis=1)
-
-        def unpack(p):
-            s = p[:, heads_local:].reshape(p.shape[0], 2 * heads_local, 4)[:, :, :1]
-            return p[:, :heads_local], s[:, :heads_local], s[:, heads_local:]
-
-        def merge(a, b):
-            oa, ma, la = unpack(a)
-            ob, mb, lb = unpack(b)
-            mm = jnp.maximum(ma, mb)
-            fa, fb = jnp.exp(ma - mm), jnp.exp(mb - mm)
-            return oa * fa + ob * fb, mm, la * fa + lb * fb
-
-        def repack(om, mm, lm):
-            s = jnp.concatenate([mm, lm], axis=1)
-            s = jnp.broadcast_to(s, s.shape[:2] + (4,)).reshape(om.shape[0], 1, head_dim)
-            return jnp.concatenate([om, s], axis=1)
-
-        half = row_count // 2
-        core = sp_index % 2
-        xpos = sp_index // 2
-        keep = lax.dynamic_slice_in_dim(pack, core * half, half, 0)
-        give = lax.dynamic_slice_in_dim(pack, (1 - core) * half, half, 0)
-        got = swap(give, 'sp', sp_size, 1)
-        pack = repack(*merge(keep, got))
-        quarter = half // 2
-        keep = lax.dynamic_slice_in_dim(pack, xpos * quarter, quarter, 0)
-        give = lax.dynamic_slice_in_dim(pack, (1 - xpos) * quarter, quarter, 0)
-        got = swap(give, 'sp', sp_size, 2)
-        om, mm, lm = merge(keep, got)
-        attn = (om / lm).reshape(quarter, heads_local * head_dim).astype(jnp.bfloat16)
-        part = jnp.dot(attn, w_o, preferred_element_type=jnp.float32)
-        proj_sum = part + swap(part, 'tp', tp_size, 1)
-        y = rms_scale(proj_sum, w_post)
-        other = swap(y, 'sp', sp_size, 2)
-        y2 = jnp.where(xpos == 0, jnp.concatenate([y, other], 0), jnp.concatenate([other, y], 0))
-        other = swap(y2, 'sp', sp_size, 1)
-        y4 = jnp.where(core == 0, jnp.concatenate([y2, other], 0), jnp.concatenate([other, y2], 0))
-        x_out = (x_f + y4).astype(jnp.bfloat16)
+        x_out = merge(o.reshape(row_count * heads_local, head_dim), m, l, x_in, w_post.reshape(1, -1), w_o, 2, 9)
         return x_out, k_out.reshape(k_cache.shape), v_out.reshape(v_cache.shape)
 
     return jax.shard_map(local_step, mesh=mesh,

time: 170 us -> 144 us (0.85)
  waiting for transfers between devices: 70.3 us -> 0 us
  Pallas kernels: 45.8 us -> 114 us
  other arithmetic: 19.2 us -> 6.39 us
  matrix products: 22.3 us -> 14.8 us
  starting transfers between devices: 7.01 us -> 0 us
  local copies, waits for them, and re-layouts: 4.36 us -> 7.36 us
    ppermute x5 -> x0, waiting for transfers between devices: 70.3 us -> none  [swap(): return lax.ppermute(value, axis, [(i, i ^ bit) for i in range(size)])]
    pallas_call x0 -> x1, Pallas kernels: none -> 68.5 us  [merge(): pl.pallas_call(functools.partial(merge_kernel, halves, 'sp', 'tp'), out_s...]
    dot_general x1 -> x0, matrix products: 8.13 us -> none  [local_step(): part = jnp.dot(attn, w_o, preferred_element_type=jnp.float32)]
    ppermute x5 -> x0, starting transfers between devices: 7.01 us -> none  [swap(): return lax.ppermute(value, axis, [(i, i ^ bit) for i in range(size)])]
    convert_element_type x2 -> x0, other arithmetic: 5.75 us -> none  [the longest x1 5.27 us: local_step(): x_out = (x_f + y4).astype(jnp.bfloat16)]
    unnamed x33 -> x28, local copies, waits for them, and re-layouts: 1.97 us -> 6.74 us
    dot_general x1, matrix products: 5.07 us -> 9.28 us  [local_step(): q_proj = jnp.dot(normed, w_q, preferred_element_type=jnp.float32)]
    dot_general x1, matrix products: 6.48 us -> 2.73 us  [local_step(): jnp.dot(normed, w_v, preferred_element_type=jnp.float32)]
  transfers between devices with their start and end apart: 5 -> 0, of which waited for: 5 -> 0; matrix products, arithmetic and copies ran while one was open for 0% -> 0% of each run, Pallas kernels for 0% -> 0%
where the time goes in v3:
time: 144 us
  Pallas kernels  114 us (79%)
  matrix products  14.8 us (10%)
  local copies, waits for them, and re-layouts  7.36 us (5%)
  other arithmetic  6.39 us (4%)
    pallas_call x1, Pallas kernels, merge(): pl.pallas_call(functools.partial(merge_kernel, halves, 'sp', 'tp'), out_s...  68.5 us
    pallas_call x1, Pallas kernels, attend(): pl.pallas_call(functools.partial(attend_kernel, n_steps, first_row, kv_he...  45.8 us
    dot_general x1, matrix products, local_step(): q_proj = jnp.dot(normed, w_q, preferred_element_type=jnp.float32)  9.28 us
    unnamed x28, local copies, waits for them, and re-layouts  6.74 us

profile of v3, /device:TPU:0, one launch (start us, length us, event | category | flops | bytes accessed | tf_op | source)
XLA Modules:
  0.0 143.7 jit_solution(14306408067682610095)
XLA Ops:
  0.6 0.0 copy-start.4
  0.6 0.9 broadcast_add_fusion
  1.5 0.0 slice-start
  1.5 2.4 %fusion = f32[256]{0:T(256)S(1)} fusion(bf16[256,4608]{1,0:T(8,128)(2,1)} %x_ref.1), kind=kLoop, calls=%fused_computation.2 | loop fusion | flops 3538688 | bytes 2360320 | tf_op jit(solution)/shard_map/reduce_sum | solution.py:23
  3.9 0.0 copy-done.4
  3.9 0.0 slice-start.1
  3.9 0.0 slice-start.2
  3.9 9.3 %convolution_bitcast_fusion = f32[32,8,16,128]{3,1,2,0:T(8,128)S(1)} fusion(bf16[4608,2048]{1,0:T(8,128)(2,1)} %param.13, bf16[256,4608]{1,0:T(8,128)(2,1)S(1)} %copy-done.4, f32[4608]{0:T(1024)S(1)} %broadcast_add_fusion, f32[256]{0:T(256)S(1)} %add_rsqrt_fusion), kind=kOutput, calls=%fused_computation.7 | convolution fusion | flops 4836556800 | bytes 23350272 | tf_op jit(solution)/shard_map/dot_general | solution.py:387
  13.2 0.0 copy-start.3
  13.2 0.4 copy.13
  13.6 0.3 copy-done.3
  13.9 0.5 multiply_cosine_fusion
  14.5 0.0 slice-start.3
  14.5 0.8 subtract_convert_fusion
  15.2 0.0 slice-done
  15.2 0.0 slice-done.1
  15.3 0.0 slice-done.2
  15.3 0.0 slice-start.4
  15.3 0.0 slice-start.5
  15.3 2.7 %convolution_bitcast_fusion.1 = f32[32,8,8,128]{3,1,2,0:T(8,128)S(1)} fusion(bf16[4608,1024]{1,0:T(8,128)(2,1)S(1)} %bitcast.27, bf16[256,4608]{1,0:T(8,128)(2,1)S(1)} %copy-done.4, f32[4608]{0:T(1024)S(1)} %broadcast_add_fusion, f32[256]{0:T(256)S(1)} %add_rsqrt_fusion), kind=kOutput, calls=%fused_computation.8 | convolution fusion | flops 2420637696 | bytes 12864512 | tf_op jit(solution)/shard_map/dot_general | solution.py:389
  18.1 0.2 copy.14
  18.3 0.5 subtract_convert_fusion.1
  18.8 1.2 pad_maximum_fusion
  20.0 0.0 slice-done.3
  20.0 0.0 slice-done.4
  20.0 0.0 slice-done.5
  20.0 2.7 %fusion.3 = bf16[32,8,8,128]{3,1,2,0:T(8,128)(2,1)S(1)} fusion(bf16[4608,1024]{1,0:T(8,128)(2,1)S(1)} %bitcast.29, bf16[256,4608]{1,0:T(8,128)(2,1)S(1)} %copy-done.4, f32[4608]{0:T(1024)S(1)} %broadcast_add_fusion, f32[256]{0:T(256)S(1)} %add_rsqrt_fusion), kind=kOutput, calls=%fused_computation.10 | convolution fusion | flops 2420899840 | bytes 12340224 | tf_op jit(solution)/shard_map/dot_general | solution.py:391
  22.7 0.1 copy.15
  22.8 0.1 pad_maximum_fusion.1.vn_hbm
  23.0 0.0 copy-start.5
  23.0 45.8 %attend.1 = (bf16[256,512,128]{2,1,0:T(8,128)(2,1)}, bf16[256,512,128]{2,1,0:T(8,128)(2,1)}, f32[256,16,128]{2,1,0:T(8,128)S(1)}, f32[16,256]{1,0:T(8,128)S(1)}, f32[16,256]{1,0:T(8,128)S(1)}) custom-call(s32[256]{0:T(256)S(1)} %copy-done.3, s32[1]{0:T(128)} %bitcast.base_ref, bf16[256,16,128]{2,1,0:T(8,128)(2,1)S(1)} %get-tuple-element.19.q_hbm, ...), custom_call_target="tpu_custom_call" | custom-call | flops 1073741824 | bytes 134217728 | tf_op jit(solution)/shard_map/attend/pallas_call | solution.py:164
  68.8 0.0 copy-start
  68.8 1.3 copy-done
  70.1 0.0 copy-start.1
  70.1 0.6 copy-done.1
  70.7 0.0 copy-start.2
  70.7 0.6 copy-done.2
  71.3 0.0 copy-done.5
  71.3 0.6 reshape.104.wpost_ref
  71.9 68.5 %merge.1 = bf16[256,4608]{1,0:T(8,128)(2,1)} custom-call(f32[4096,128]{1,0:T(8,128)} %bitcast.18, f32[16,256]{1,0:T(8,128)} %copy-done.1, f32[16,256]{1,0:T(8,128)} %copy-done.2, bf16[256,4608]{1,0:T(8,128)(2,1)} %x_ref.1, f32[1,4608]{1,0:T(1,128)} %reshape.104.wpost_ref, bf16[2048,4608]{1,0:T(8,128)(2,1)} %wo_hbm.1), custom_call_target="tpu_custom_call" | custom-call | flops 1207959552 | bytes 18874368 | tf_op jit(solution)/shard_map/merge/pallas_call | solution.py:353
  140.5 3.2 %copy.17 = bf16[256,4608]{1,0:T(8,128)(2,1)} copy(bf16[256,4608]{1,0:T(8,128)(2,1)} %merge.1) | data formatting | bytes 4718592
  (5 shorter events, 0.0 us)
Async XLA Ops:
  0.6 3.3 %copy-start.4 = (bf16[256,4608]{1,0:T(8,128)(2,1)S(1)}, bf16[256,4608]{1,0:T(8,128)(2,1)}, u32[]{:S(2)}) copy-start(bf16[256,4608]{1,0:T(8,128)(2,1)} %x_ref.1) | copy-start | bytes 7077892
  1.5 13.7 %slice-start = ((s8[9437184]{0:T(1024)(128)(4,1)}), s8[4194304]{0:T(1024)(128)(4,1)S(1)}, s32[]{:S(2)}) async-start(s8[9437184]{0:T(1024)(128)(4,1)} %bitcast.26), calls=%async_computation | async-start | bytes 8388608
  3.9 11.3 %slice-start.1 = ((s8[9437184]{0:T(1024)(128)(4,1)}), s8[4194304]{0:T(1024)(128)(4,1)S(1)}, s32[]{:S(2)}) async-start(s8[9437184]{0:T(1024)(128)(4,1)} %bitcast.26), calls=%async_computation.1 | async-start | bytes 8388608
  3.9 11.3 %slice-start.2 = ((s8[9437184]{0:T(1024)(128)(4,1)}), s8[1048576]{0:T(1024)(128)(4,1)S(1)}, s32[]{:S(2)}) async-start(s8[9437184]{0:T(1024)(128)(4,1)} %bitcast.26), calls=%async_computation.2 | async-start | bytes 2097152
  13.2 0.7 copy-start.3
  14.5 5.5 %slice-start.3 = ((s8[9437184]{0:T(1024)(128)(4,1)}), s8[4194304]{0:T(1024)(128)(4,1)S(1)}, s32[]{:S(2)}) async-start(s8[9437184]{0:T(1024)(128)(4,1)} %bitcast.28), calls=%async_computation.3 | async-start | bytes 8388608
  15.3 4.7 %slice-start.4 = ((s8[9437184]{0:T(1024)(128)(4,1)}), s8[4194304]{0:T(1024)(128)(4,1)S(1)}, s32[]{:S(2)}) async-start(s8[9437184]{0:T(1024)(128)(4,1)} %bitcast.28), calls=%async_computation.4 | async-start | bytes 8388608
  15.3 4.7 %slice-start.5 = ((s8[9437184]{0:T(1024)(128)(4,1)}), s8[1048576]{0:T(1024)(128)(4,1)S(1)}, s32[]{:S(2)}) async-start(s8[9437184]{0:T(1024)(128)(4,1)} %bitcast.28), calls=%async_computation.5 | async-start | bytes 2097152
  23.0 48.3 %copy-start.5 = (f32[4608]{0:T(1024)S(1)}, f32[4608]{0:T(1024)}, u32[]{:S(2)}) copy-start(f32[4608]{0:T(1024)} %param.17) | copy-start | bytes 55300
  68.8 1.3 copy-start
  70.1 0.6 copy-start.1
  70.7 0.6 copy-start.2

commit v4 on v2

--- a/solution.py
+++ b/solution.py
@@ -6,6 +6,7 @@
 from jax.experimental import pallas as pl
 from jax.experimental.pallas import tpu as pltpu
 from jax.sharding import PartitionSpec as P
+
 
 SOFT_CAP = 50.0
 ROPE_BASE = 10000.0
@@ -38,8 +39,9 @@
 
 def attend_kernel(n_steps, first_row, kv_heads, seq_block, pos_ref, base_ref, q_hbm, kn_hbm, vn_hbm, k_hbm, v_hbm,
                   *rest):
-    (ko_hbm, vo_hbm, o_hbm, m_ref, l_ref, kbuf, vbuf, qbuf, knbuf, vnbuf, obuf, key_ref, s_ref, p_ref, in_sem, out_sem, o_sem) = rest[-17:]
+    (ko_hbm, vo_hbm, o0_hbm, o1_hbm, o2_hbm, o3_hbm, m_ref, l_ref, kbuf, vbuf, qbuf, knbuf, vnbuf, obuf, key_ref, s_ref, p_ref, in_sem, out_sem, o_sem, st_sem) = rest[-21:]
     step_rows = ROWS_STEP
+    piece_steps = n_steps // 4
     heads, head_dim = qbuf.shape[2], qbuf.shape[3]
     cols = seq_block * kv_heads
     base = base_ref[0]
@@ -64,9 +66,17 @@
         return (pltpu.make_async_copy(kbuf.at[slot], ko_hbm.at[rows], out_sem.at[slot, 0]),
                 pltpu.make_async_copy(vbuf.at[slot], vo_hbm.at[rows], out_sem.at[slot, 1]))
 
-    def o_store(step, slot):
-        rows = pl.ds(step * step_rows, step_rows)
-        return pltpu.make_async_copy(obuf.at[slot], o_hbm.at[rows], o_sem.at[slot])
+    def o_store(step, slot, d=0):
+        at = pl.ds(lax.rem(step, piece_steps) * step_rows * heads, step_rows * heads)
+        o_hbm = (o0_hbm, o1_hbm, o2_hbm, o3_hbm)[d]
+        return pltpu.make_async_copy(obuf.at[slot], o_hbm.at[at], o_sem.at[slot])
+
+    def o_start(step, slot):
+        turn = jnp.bitwise_xor(step // piece_steps, base // seq_block)
+        for d in range(4):
+            @pl.when(turn == d)
+            def _():
+                o_store(step, slot, d).start()
 
     for step in range(min(AHEAD, n_steps)):
         for copy in loads(step, step):
@@ -121,10 +131,10 @@
             if 0 <= r < step_rows:
                 right = jnp.concatenate([vbuf[slot, r, :half, :], vbuf[slot, r, half:, :]], axis=1)
                 both = jnp.dot(p_ref[r], right, preferred_element_type=jnp.float32)
-                obuf[oslot, r] = both[:heads, :head_dim] + both[heads:, head_dim:]
+                obuf[oslot, r * heads:(r + 1) * heads, :] = both[:heads, :head_dim] + both[heads:, head_dim:]
         m_ref[...] = m_all
         l_ref[...] = l_all
-        o_store(step, oslot).start()
+        o_start(step, oslot)
         for copy in stores(step, slot):
             copy.start()
 
@@ -137,11 +147,22 @@
             def _():
                 for copy in stores(nxt - SLOTS, nslot):
                     copy.wait()
+
             for copy in loads(nxt, nslot):
                 copy.start()
+
         return carry
 
     lax.fori_loop(0, n_steps, body, 0)
+    tail = piece_steps * step_rows * heads
+    stat_copies = []
+    for d, o_hbm in enumerate((o0_hbm, o1_hbm, o2_hbm, o3_hbm)):
+        stat_copies.append(pltpu.make_async_copy(m_ref, o_hbm.at[pl.ds(tail, heads)], st_sem.at[d, 0]))
+        stat_copies.append(pltpu.make_async_copy(l_ref, o_hbm.at[pl.ds(tail + heads, heads)], st_sem.at[d, 1]))
+    for copy in stat_copies:
+        copy.start()
+    for copy in stat_copies:
+        copy.wait()
     for step in range(max(0, n_steps - SLOTS), n_steps):
         for copy in stores(step, step % SLOTS):
             copy.wait()
@@ -150,38 +171,38 @@
 
 
 def attend(pos, base, q, kn, vn, k_cache, v_cache, prev, first_row, n_rows):
-    rows, cols, head_dim = k_cache.shape
+    _, cols, head_dim = k_cache.shape
     heads = q.shape[1]
     kv_heads = kn.shape[1] // 2
     seq_block = cols // kv_heads
     n_steps = n_rows // ROWS_STEP
     hbm = pl.BlockSpec(memory_space=pl.ANY)
-    vmem = pl.BlockSpec(memory_space=pltpu.VMEM)
+    piece = jax.ShapeDtypeStruct((n_rows // 4 * heads + 2 * heads, head_dim), jnp.float32)
     smem = pl.BlockSpec(memory_space=pltpu.SMEM)
     bf = jnp.bfloat16
     aliases = {} if prev is None else {7: 0, 8: 1}
     extra = () if prev is None else tuple(prev)
     return pl.pallas_call(
         functools.partial(attend_kernel, n_steps, first_row, kv_heads, seq_block),
-        out_shape=(jax.ShapeDtypeStruct(k_cache.shape, bf), jax.ShapeDtypeStruct(v_cache.shape, bf),
-                   jax.ShapeDtypeStruct((n_rows, heads, head_dim), jnp.float32),
-                   jax.ShapeDtypeStruct((heads, n_rows), jnp.float32),
-                   jax.ShapeDtypeStruct((heads, n_rows), jnp.float32)),
+        out_shape=(jax.ShapeDtypeStruct(k_cache.shape, bf), jax.ShapeDtypeStruct(v_cache.shape, bf)) + (piece,) * 4,
         in_specs=[smem, smem, hbm, hbm, hbm, hbm, hbm] + [hbm] * len(extra),
-        out_specs=(hbm, hbm, hbm, vmem, vmem),
+        out_specs=(hbm,) * 6,
         scratch_shapes=[
+            pltpu.VMEM((heads, 128), jnp.float32),
+            pltpu.VMEM((heads, 128), jnp.float32),
             pltpu.VMEM((SLOTS, ROWS_STEP, cols, head_dim), bf),
             pltpu.VMEM((SLOTS, ROWS_STEP, cols, head_dim), bf),
             pltpu.VMEM((SLOTS, ROWS_STEP, heads, head_dim), bf),
             pltpu.VMEM((SLOTS, ROWS_STEP, 2 * kv_heads, head_dim), bf),
             pltpu.VMEM((SLOTS, ROWS_STEP, 2 * kv_heads, head_dim), bf),
-            pltpu.VMEM((2, ROWS_STEP, heads, head_dim), jnp.float32),
+            pltpu.VMEM((2, ROWS_STEP * heads, head_dim), jnp.float32),
             pltpu.VMEM((heads, cols), jnp.int32),
             pltpu.VMEM((ROWS_STEP, heads, cols), jnp.float32),
             pltpu.VMEM((ROWS_STEP, 2 * heads, cols // 2), bf),
             pltpu.SemaphoreType.DMA((SLOTS, 5)),
             pltpu.SemaphoreType.DMA((SLOTS, 2)),
             pltpu.SemaphoreType.DMA((2,)),
+            pltpu.SemaphoreType.DMA((4, 2)),
         ],
         input_output_aliases=aliases,
         compiler_params=pltpu.CompilerParams(vmem_limit_bytes=40 * 1024 * 1024),
@@ -191,13 +212,190 @@
     )(pos, base, q, kn, vn, k_cache, v_cache, *extra)
 
 
+def merge_kernel(chunks, *refs):
+    n_in = 4 * len(chunks)
+    source = [refs[4 * c:4 * c + 4] for c in range(len(chunks))]
+    pieces = [[b.at[d] for d in range(4)] for b in refs[-len(chunks):]]
+    refs = refs[:-len(chunks)]
+    (x_hbm, wpost_hbm, wo_hbm, out_ref, wo, xbuf, wpost_ref, last_in, osum, lhs, y_out, y_in, sums,
+     in_sem, p_sem, w_sem, o_send, o_recv, y_send, y_recv, g_send, g_recv, d_send, d_recv, f_send, f_recv) = refs[n_in:]
+    sp = lax.axis_index('sp')
+    tp = lax.axis_index('tp')
+    core = lax.rem(sp, 2)
+    xpos = sp // 2
+    _, width = xbuf.shape
+    n_chunks, quarter, chunk = y_out.shape
+    heads = lhs.shape[1] // 128
+    parts = [c // 4 for c in chunks]
+    core_peer = {'sp': 2 * xpos + (1 - core)}
+    x_peer = {'sp': 2 * (1 - xpos) + core}
+    far_peer = {'sp': 2 * (1 - xpos) + (1 - core)}
+    y_peer = {'tp': 1 - tp}
+    mesh_id = pl.DeviceIdType.MESH
+
+    def remote(src, dst, send, recv, peer):
+        return pltpu.make_async_remote_copy(src_ref=src, dst_ref=dst, send_sem=send, recv_sem=recv,
+                                            device_id=peer, device_id_type=mesh_id)
+
+    def w_load(n):
+        return pltpu.make_async_copy(wo_hbm.at[:, pl.ds(n * chunk, chunk)], wo.at[n], w_sem.at[n])
+
+    small = [pltpu.make_async_copy(x_hbm, xbuf, in_sem.at[0]), pltpu.make_async_copy(wpost_hbm, wpost_ref, in_sem.at[1])]
+    local = [[pltpu.make_async_copy(source[c][d], pieces[c][d], p_sem.at[c, d]) for d in range(4)] for c in range(len(chunks))]
+    for group in local:
+        for copy in group:
+            copy.start()
+    for n in range(n_chunks):
+        w_load(n).start()
+    for copy in small:
+        copy.start()
+    barrier = pltpu.get_barrier_semaphore()
+    for peer in (core_peer, x_peer, far_peer, y_peer):
+        pl.semaphore_signal(barrier, inc=1, device_id=peer, device_id_type=mesh_id)
+    pl.semaphore_wait(barrier, 4)
+
+    for copy in local[-1]:
+        copy.wait()
+    last = [remote(pieces[-1][d], last_in.at[d - 1], o_send.at[d - 1], o_recv.at[d - 1], peer)
+            for d, peer in ((2, x_peer), (3, far_peer), (1, core_peer))]
+    for copy in last:
+        copy.start()
+
+    def combine(blocks, part, row0):
+        count = part * heads
+        stats = [block[count:count + 2 * heads, :] for block in blocks]
+        top = functools.reduce(jnp.maximum, [st[:heads] for st in stats])
+        grown = [jnp.exp(st[:heads] - top) for st in stats]
+        total = sum(st[heads:] * g for st, g in zip(stats, grown))
+        shift = lax.rem(128 - sp * part, 128)
+        factors = [pltpu.roll(g / total, shift, 1) for g in grown]
+        for b in range(part):
+            at = slice(b * heads, (b + 1) * heads)
+            osum[at, :] = sum(block[at, :] * f[:, b:b + 1] for block, f in zip(blocks, factors))
+        for h in range(heads):
+            lhs[row0:row0 + part, h * 128:(h + 1) * 128] = osum[pl.ds(h, part, stride=heads), :].astype(jnp.bfloat16)
+
+    first = sum(parts[:-1])
+    row0 = 0
+    for c in range(len(chunks) - 1):
+        for copy in local[c]:
+            copy.wait()
+        combine(pieces[c], parts[c], row0)
+        row0 += parts[c]
+
+    wide = 3
+    first_at, last_at = pl.ds(0, first), pl.ds(first, quarter - first)
+    order = [(pl.ds(n, 1), first_at) for n in range(n_chunks)] + [(pl.ds(n, wide), last_at) for n in range(0, n_chunks, wide)]
+
+    def to_y(t):
+        ns, r = order[t]
+        return remote(y_out.at[ns, r], y_in.at[ns, r], y_send.at[t], y_recv.at[t], y_peer)
+
+    def to_x(t):
+        ns, r = order[t]
+        return remote(sums.at[sp, ns, r], sums.at[sp, ns, r], g_send.at[t], g_recv.at[t], x_peer)
+
+    def to_core(t):
+        ns, r = order[t]
+        return remote(sums.at[sp, ns, r], sums.at[sp, ns, r], d_send.at[t], d_recv.at[t], core_peer)
+
+    def relay(t):
+        ns, r = order[t]
+        other = 2 * (1 - xpos) + core
+        return remote(sums.at[other, ns, r], sums.at[other, ns, r], f_send.at[t], f_recv.at[t], core_peer)
+
+    def project(n, r0, count):
+        y_out[n, r0:r0 + count, :] = jnp.dot(lhs[r0:r0 + count, :], wo[n], preferred_element_type=jnp.float32)
+
+    for n in range(n_chunks):
+        w_load(n).wait()
+        project(n, 0, first)
+        to_y(n).start()
+
+    for t in range(len(order) + 1):
+        if t == 2:
+            for copy in last:
+                copy.wait()
+            combine([pieces[-1][0]] + [last_in.at[d] for d in range(3)], parts[-1], first)
+        if 2 <= t < 2 + n_chunks // wide:
+            for n in range((t - 2) * wide, (t - 1) * wide):
+                project(n, first, quarter - first)
+            to_y(n_chunks + t - 2).start()
+        if t < len(order):
+            ns, r = order[t]
+            to_y(t).wait()
+            sums[sp, ns, r, :] = y_out[ns, r, :] + y_in[ns, r, :]
+            to_x(t).start()
+            to_core(t).start()
+        if t >= 1:
+            to_x(t - 1).wait_recv()
+            relay(t - 1).start()
+    for copy in small:
+        copy.wait()
+    for t in range(len(order)):
+        to_x(t).wait_send()
+        to_core(t).wait()
+        relay(t).wait()
+
+    starts = []
+    base = 0
+    for c, part in zip(chunks, parts):
+        starts += [(base, part, k) for k in range(0, part, 16)]
+        base += c
+    for q in range(4):
+        for k, (base, part, off) in enumerate(starts):
+            at = slice(k * 16, (k + 1) * 16)
+            out_at = slice(base + q * part + off, base + q * part + off + 16)
+            square = jnp.zeros((16, chunk), jnp.float32)
+            for n in range(n_chunks):
+                u = sums[q, n, at, :]
+                square = square + u * u
+            inv = lax.rsqrt(jnp.sum(square, axis=-1, keepdims=True) * (1.0 / width) + NORM_EPS)
+            for n in range(n_chunks):
+                col = slice(n * chunk, (n + 1) * chunk)
+                y = xbuf[out_at, col].astype(jnp.float32) + sums[q, n, at, :] * inv * (1.0 + wpost_ref[:, col])
+                out_ref[out_at, col] = y.astype(jnp.bfloat16)
+
+
+def merge(chunks, pieces, x_in, w_post, w_o, n_chunks):
+    rows, width = x_in.shape
+    inner = w_o.shape[0]
+    heads = inner // 128
+    quarter = rows // 4
+    chunk = width // n_chunks
+    vmem = pl.BlockSpec(memory_space=pltpu.VMEM)
+    hbm = pl.BlockSpec(memory_space=pl.ANY)
+    f32 = jnp.float32
+    dma = pltpu.SemaphoreType.DMA
+    per_piece = dma((n_chunks + 3,))
+    flat = [p for piece in pieces for p in piece]
+    big = max(chunks) // 4 * heads
+    return pl.pallas_call(
+        functools.partial(merge_kernel, chunks),
+        out_shape=jax.ShapeDtypeStruct(x_in.shape, x_in.dtype),
+        in_specs=[hbm] * (len(flat) + 3),
+        out_specs=vmem,
+        scratch_shapes=[
+            pltpu.VMEM((n_chunks, inner, chunk), jnp.bfloat16),
+            pltpu.VMEM(x_in.shape, x_in.dtype),
+            pltpu.VMEM(w_post.shape, f32),
+            pltpu.VMEM((3,) + pieces[-1][0].shape, f32),
+            pltpu.VMEM((big, 128), f32),
+            pltpu.VMEM((quarter, inner), jnp.bfloat16),
+            pltpu.VMEM((n_chunks, quarter, chunk), f32),
+            pltpu.VMEM((n_chunks, quarter, chunk), f32),
+            pltpu.VMEM((4, n_chunks, quarter, chunk), f32),
+            dma((2,)), dma((len(chunks), 4)), dma((n_chunks,)), dma((3,)), dma((3,)),
+        ] + [per_piece] * 8 + [pltpu.VMEM((4,) + piece[0].shape, f32) for piece in pieces],
+        compiler_params=pltpu.CompilerParams(vmem_limit_bytes=56 * 1024 * 1024, collective_id=0, has_side_effects=True),
+        cost_estimate=pl.CostEstimate(flops=2 * quarter * inner * width, bytes_accessed=2 * inner * width, transcendentals=0),
+        name='merge',
+    )(*flat, x_in, w_post, w_o)
+
+
 def solution(mesh):
     cache_spec = P('dp', 'sp', 'tp', None)
     sp_size = mesh.shape['sp']
-    tp_size = mesh.shape['tp']
-
-    def swap(value, axis, size, bit):
-        return lax.ppermute(value, axis, [(i, i ^ bit) for i in range(size)])
 
     def local_step(x_in, cur_pos, w_pre, w_q, w_k, w_v, w_o, w_post, k_cache, v_cache):
         row_count, seq_block, kv_local, head_dim = k_cache.shape
@@ -215,49 +413,19 @@
         base = (sp_index * seq_block).astype(jnp.int32).reshape(1)
         kc = k_cache.reshape(row_count, seq_block * kv_local, head_dim)
         vc = v_cache.reshape(row_count, seq_block * kv_local, head_dim)
-        k_out, v_out, o, m, l = attend(cur_pos, base, q_rot, kn2, vn2, kc, vc, None, 0, row_count)
-
-        stat = jnp.concatenate([m, l], axis=0).T[:, :, None]
-        stat = jnp.broadcast_to(stat, stat.shape[:2] + (4,)).reshape(row_count, 1, head_dim)
-        pack = jnp.concatenate([o, stat], axis=1)
-
-        def unpack(p):
-            s = p[:, heads_local:].reshape(p.shape[0], 2 * heads_local, 4)[:, :, :1]
-            return p[:, :heads_local], s[:, :heads_local], s[:, heads_local:]
-
-        def merge(a, b):
-            oa, ma, la = unpack(a)
-            ob, mb, lb = unpack(b)
-            mm = jnp.maximum(ma, mb)
-            fa, fb = jnp.exp(ma - mm), jnp.exp(mb - mm)
-            return oa * fa + ob * fb, mm, la * fa + lb * fb
-
-        def repack(om, mm, lm):
-            s = jnp.concatenate([mm, lm], axis=1)
-            s = jnp.broadcast_to(s, s.shape[:2] + (4,)).reshape(om.shape[0], 1, head_dim)
-            return jnp.concatenate([om, s], axis=1)
-
-        half = row_count // 2
-        core = sp_index % 2
-        xpos = sp_index // 2
-        keep = lax.dynamic_slice_in_dim(pack, core * half, half, 0)
-        give = lax.dynamic_slice_in_dim(pack, (1 - core) * half, half, 0)
-        got = swap(give, 'sp', sp_size, 1)
-        pack = repack(*merge(keep, got))
-        quarter = half // 2
-        keep = lax.dynamic_slice_in_dim(pack, xpos * quarter, quarter, 0)
-        give = lax.dynamic_slice_in_dim(pack, (1 - xpos) * quarter, quarter, 0)
-        got = swap(give, 'sp', sp_size, 2)
-        om, mm, lm = merge(keep, got)
-        attn = (om / lm).reshape(quarter, heads_local * head_dim).astype(jnp.bfloat16)
-        part = jnp.dot(attn, w_o, preferred_element_type=jnp.float32)
-        proj_sum = part + swap(part, 'tp', tp_size, 1)
-        y = rms_scale(proj_sum, w_post)
-        other = swap(y, 'sp', sp_size, 2)
-        y2 = jnp.where(xpos == 0, jnp.concatenate([y, other], 0), jnp.concatenate([other, y], 0))
-        other = swap(y2, 'sp', sp_size, 1)
-        y4 = jnp.where(core == 0, jnp.concatenate([y2, other], 0), jnp.concatenate([other, y2], 0))
-        x_out = (x_f + y4).astype(jnp.bfloat16)
+        chunks = (row_count // 2, row_count // 4, row_count // 4)
+        prev, first_row, pieces = None, 0, []
+        for index, n_rows in enumerate(chunks):
+            *prev, p0, p1, p2, p3 = attend(cur_pos, base, q_rot, kn2, vn2, kc, vc, prev, first_row, n_rows)
+            first_row += n_rows
+            if index < len(chunks) - 1:
+                moved = []
+                for d, p in ((1, p1), (2, p2), (3, p3)):
+                    moved.append(lax.ppermute(p, 'sp', [(i, i ^ d) for i in range(sp_size)]))
+                p1, p2, p3 = moved
+            pieces.append((p0, p1, p2, p3))
+        k_out, v_out = prev
+        x_out = merge(chunks, pieces, x_in, w_post.reshape(1, -1), w_o, 9)
         return x_out, k_out.reshape(k_cache.shape), v_out.reshape(v_cache.shape)
 
     return jax.shard_map(local_step, mesh=mesh,

time: 170 us -> 141 us (0.83)
  waiting for transfers between devices: 70.3 us -> 0.04 us
  Pallas kernels: 45.8 us -> 99.8 us
  other arithmetic: 19.2 us -> 10.1 us
  matrix products: 22.3 us -> 14.8 us
  local copies, waits for them, and re-layouts: 4.36 us -> 9.83 us
    ppermute x5 -> x6, waiting for transfers between devices: 70.3 us -> 0.04 us  [local_step(): moved.append(lax.ppermute(p, 'sp', [(i, i ^ d) for i in range(sp_size)]))]
    pallas_call x0 -> x1, Pallas kernels: none -> 48.9 us  [merge(): pl.pallas_call(functools.partial(merge_kernel, chunks), out_shape=jax.Sha...]
    dot_general x1 -> x0, matrix products: 8.13 us -> none  [local_step(): part = jnp.dot(attn, w_o, preferred_element_type=jnp.float32)]
    unnamed x33 -> x51, local copies, waits for them, and re-layouts: 1.97 us -> 9.07 us
    convert_element_type x2 -> x0, other arithmetic: 5.75 us -> none  [the longest x1 5.27 us: local_step(): x_out = (x_f + y4).astype(jnp.bfloat16)]
    pallas_call x1 -> x3, Pallas kernels: 45.8 us -> 50.9 us  [attend(): pl.pallas_call(functools.partial(attend_kernel, n_steps, first_row, kv_he...]
    dot_general x1, matrix products: 5.07 us -> 9.28 us  [local_step(): q_proj = jnp.dot(normed, w_q, preferred_element_type=jnp.float32)]
    dot_general x1, matrix products: 6.48 us -> 2.75 us  [local_step(): jnp.dot(normed, w_v, preferred_element_type=jnp.float32)]
  transfers between devices with their start and end apart: 5 -> 6, of which waited for: 5 -> 0; matrix products, arithmetic and copies ran while one was open for 0% -> 0% of each run, Pallas kernels for 0% -> 9%
where the time goes in v4:
time: 141 us
  Pallas kernels  99.8 us (71%)
  matrix products  14.8 us (10%)
  other arithmetic  10.1 us (7%)
  local copies, waits for them, and re-layouts  9.83 us (7%)
  starting transfers between devices  5.62 us (4%)
    pallas_call x3, Pallas kernels, attend(): pl.pallas_call(functools.partial(attend_kernel, n_steps, first_row, kv_he...  50.9 us
    pallas_call x1, Pallas kernels, merge(): pl.pallas_call(functools.partial(merge_kernel, chunks), out_shape=jax.Sha...  48.9 us
    dot_general x1, matrix products, local_step(): q_proj = jnp.dot(normed, w_q, preferred_element_type=jnp.float32)  9.28 us
    unnamed x51, local copies, waits for them, and re-layouts  9.07 us
    ppermute x6, starting transfers between devices, local_step(): moved.append(lax.ppermute(p, 'sp', [(i, i ^ d) for i in range(sp_size)]))  5.62 us
    another operation x2, other arithmetic  3.52 us
  transfers between devices with their start and end apart: 6, of which 0 were waited for; matrix products, arithmetic and copies ran while one was open for 0% of the time, Pallas kernels for 9%

profile of v4, /device:TPU:0, one launch (start us, length us, event | category | flops | bytes accessed | tf_op | source)
XLA Modules:
  0.0 141.1 jit_solution(18032265144782489307)
XLA Ops:
  0.6 0.0 copy-start.7
  0.7 0.9 broadcast_add_fusion
  1.5 2.4 %fusion = f32[256]{0:T(256)S(1)} fusion(bf16[256,4608]{1,0:T(8,128)(2,1)} %refs_12_.1), kind=kLoop, calls=%fused_computation.2 | loop fusion | flops 3538688 | bytes 2360320 | tf_op jit(solution)/shard_map/reduce_sum | solution.py:24
  3.9 0.0 copy-done.7
  3.9 0.0 slice-start.1
  3.9 0.0 slice-start.2
  3.9 9.3 %convolution_bitcast_fusion = f32[32,8,16,128]{3,1,2,0:T(8,128)S(1)} fusion(bf16[4608,2048]{1,0:T(8,128)(2,1)} %param.13, bf16[256,4608]{1,0:T(8,128)(2,1)S(1)} %copy-done.7, f32[4608]{0:T(1024)S(1)} %broadcast_add_fusion, f32[256]{0:T(256)S(1)} %add_rsqrt_fusion), kind=kOutput, calls=%fused_computation.7 | convolution fusion | flops 4836556800 | bytes 23350272 | tf_op jit(solution)/shard_map/dot_general | solution.py:406
  13.2 0.0 copy-start.6
  13.2 0.0 slice-start.3
  13.3 0.4 copy.17
  13.6 0.3 copy-done.6
  13.9 0.0 slice-done
  13.9 0.0 slice-done.1
  13.9 0.0 slice-done.2
  13.9 0.0 slice-start.4
  14.0 0.0 slice-start.5
  14.0 2.7 %convolution_bitcast_fusion.1 = f32[32,8,8,128]{3,1,2,0:T(8,128)S(1)} fusion(bf16[4608,1024]{1,0:T(8,128)(2,1)S(1)} %bitcast.30, bf16[256,4608]{1,0:T(8,128)(2,1)S(1)} %copy-done.7, f32[4608]{0:T(1024)S(1)} %broadcast_add_fusion, f32[256]{0:T(256)S(1)} %add_rsqrt_fusion), kind=kOutput, calls=%fused_computation.8 | convolution fusion | flops 2420637696 | bytes 12864512 | tf_op jit(solution)/shard_map/dot_general | solution.py:408
  16.7 0.2 copy.18
  16.9 0.5 multiply_cosine_fusion
  17.5 2.1 %subtract_convert_fusion = (bf16[256,16,64]{2,1,0:T(8,128)(2,1)}, bf16[256,16,64]{2,1,0:T(8,128)(2,1)}) fusion(f32[256,16,128]{2,1,0:T(8,128)S(1)} %bitcast.25, f32[256,64]{1,0:T(8,128)S(1)} %get-tuple-element.44, f32[256,64]{1,0:T(8,128)S(1)} %get-tuple-element.43), kind=kLoop, calls=%fused_computation.6 | loop fusion | flops 2097152 | bytes 3276800 | tf_op jit(solution)/shard_map/convert.2
  19.5 1.4 %subtract_convert_fusion.1 = (bf16[256,8,64]{2,1,0:T(8,128)(2,1)}, bf16[256,8,64]{2,1,0:T(8,128)(2,1)}) fusion(f32[256,8,128]{2,1,0:T(8,128)S(1)} %bitcast.26, f32[256,64]{1,0:T(8,128)S(1)} %get-tuple-element.44, f32[256,64]{1,0:T(8,128)S(1)} %get-tuple-element.43), kind=kLoop, calls=%fused_computation.14 | loop fusion | flops 1048576 | bytes 1703936 | tf_op jit(solution)/shard_map/convert
  21.0 0.0 slice-done.3
  21.0 0.0 slice-done.4
  21.0 0.0 slice-done.5
  21.0 2.8 %fusion.3 = bf16[32,8,8,128]{3,1,2,0:T(8,128)(2,1)S(1)} fusion(bf16[4608,1024]{1,0:T(8,128)(2,1)S(1)} %bitcast.32, bf16[256,4608]{1,0:T(8,128)(2,1)S(1)} %copy-done.7, f32[4608]{0:T(1024)S(1)} %broadcast_add_fusion, f32[256]{0:T(256)S(1)} %add_rsqrt_fusion), kind=kOutput, calls=%fused_computation.10 | convolution fusion | flops 2420899840 | bytes 12340224 | tf_op jit(solution)/shard_map/dot_general | solution.py:410
  23.8 0.0 copy-start.8
  23.8 0.0 copy-start.9
  23.8 0.1 copy.19
  23.9 0.1 constant_dynamic-update-slice_fusion.1
  24.0 0.1 constant_dynamic-update-slice_fusion.vn_hbm
  24.1 0.9 copy-done.8
  25.0 0.3 copy-done.9
  25.3 2.8 %pad_maximum_fusion = (bf16[256,16,128]{2,1,0:T(8,128)(2,1)S(1)}, bf16[256,16,128]{2,1,0:T(8,128)(2,1)S(1)}) fusion(bf16[256,16,64]{2,1,0:T(8,128)(2,1)S(1)} %copy-done.9, bf16[256,16,64]{2,1,0:T(8,128)(2,1)S(1)} %copy-done.8, bf16[256,8,64]{2,1,0:T(8,128)(2,1)} %get-tuple-element.42, bf16[256,8,64]{2,1,0:T(8,128)(2,1)} %get-tuple-element.41), kind=kLoop, calls=%fused_computation.11 | loop fusion | flops 6291456 | bytes 3670016 | tf_op jit(solution)/shard_map/concatenate | solution.py:37
  28.1 24.1 %attend.3 = (bf16[256,512,128]{2,1,0:T(8,128)(2,1)}, bf16[256,512,128]{2,1,0:T(8,128)(2,1)}, f32[544,128]{1,0:T(8,128)S(1)}, f32[544,128]{1,0:T(8,128)S(1)}, f32...) custom-call(s32[256]{0:T(256)S(1)} %copy-done.6, s32[1]{0:T(128)} %bitcast.base_ref, ...), custom_call_target="tpu_custom_call" | custom-call | flops 536870912 | bytes 67108864 | tf_op jit(solution)/shard_map/attend/pallas_call | solution.py:185
  52.2 0.0 copy-start
  52.2 0.0 copy-start.16
  52.2 13.4 %attend.4 = (bf16[256,512,128]{2,1,0:T(8,128)(2,1)}, bf16[256,512,128]{2,1,0:T(8,128)(2,1)}, f32[288,128]{1,0:T(8,128)S(1)}, f32[288,128]{1,0:T(8,128)S(1)}, f32...) custom-call(s32[256]{0:T(256)S(1)} %copy-done.6, s32[1]{0:T(128)} %bitcast.base_ref, ...), custom_call_target="tpu_custom_call", output_to_operand_aliasing={{0}: (7, {}), {1}: (8, {})} | custom-call | flops 268435456 | bytes 33554432 | tf_op jit(solution)/shard_map/attend/pallas_call | solution.py:185
  65.6 0.0 copy-done
  65.6 0.0 copy-start.1
  65.6 0.9 collective-permute-start.3
  66.5 0.0 collective-permute-start
  66.5 2.9 %collective-permute-start.1 = (f32[544,128]{1,0:T(8,128)S(1)}, f32[544,128]{1,0:T(8,128)S(1)}, u32[]{:S(2)}, u32[]{:S(2)}) collective-permute-start(f32[544,128]{1,0:T(8,128)S(1)} %get-tuple-element.23), channel_id=1, source_target_pairs={{0,2},{1,3},{2,0},{3,1},{4,6},{5,7},{6,4},{7,5}} | collective-permute-start | bytes 835592 | tf_op jit(solution)/shard_map/ppermute | solution.py:424
  69.5 0.0 collective-permute-start.2
  69.5 1.4 collective-permute-start.4
  70.9 0.0 collective-permute-done.3.refs_5_
  70.9 0.4 collective-permute-start.5
  71.3 0.6 reshape.100.refs_13_
  71.9 13.4 %attend.5 = (bf16[256,512,128]{2,1,0:T(8,128)(2,1)}, bf16[256,512,128]{2,1,0:T(8,128)(2,1)}, f32[288,128]{1,0:T(8,128)S(1)}, f32[288,128]{1,0:T(8,128)S(1)}, f32...) custom-call(s32[256]{0:T(256)S(1)} %copy-done.6, s32[1]{0:T(128)} %bitcast.base_ref, ...), custom_call_target="tpu_custom_call", output_to_operand_aliasing={{0}: (7, {}), {1}: (8, {})} | custom-call | flops 268435456 | bytes 33554432 | tf_op jit(solution)/shard_map/attend/pallas_call | solution.py:185
  85.3 0.6 copy-done.2
  86.0 0.7 copy-done.3
  86.6 0.7 copy-done.4
  87.3 0.6 copy-done.5
  87.9 0.0 collective-permute-done.4.refs_6_
  87.9 0.0 collective-permute-done.5.refs_7_
  88.0 0.0 collective-permute-done.refs_1_
  88.0 0.0 collective-permute-done.1.refs_2_
  88.0 0.0 collective-permute-done.2.refs_3_
  88.0 0.6 copy-done.14
  88.6 0.0 copy-done.15
  88.6 0.1 copy-done.10
  88.7 0.1 copy-done.11
  88.8 0.1 copy-done.12
  88.9 48.9 %merge.1 = bf16[256,4608]{1,0:T(8,128)(2,1)} custom-call(f32[544,128]{1,0:T(8,128)} %copy-done, f32[544,128]{1,0:T(8,128)} %copy-done.10, f32[544,128]{1,0:T(8,128)} %copy-done.11, f32[544,128]{1,0:T(8,128)} %copy-done.12, f32[288,128]{1,0:T(8,128)} %copy-done.1, f32[288,128]{1,0:T(8,128)} %copy-done.13, f32[288,128]{1,0:T(8,128)} %copy-done.14, ...), custom_call_target="tpu_custom_call" | custom-call | flops 1207959552 | bytes 18874368 | tf_op jit(solution)/shard_map/merge/pallas_call | solution.py:373
  137.9 3.2 %copy.26 = bf16[256,4608]{1,0:T(8,128)(2,1)} copy(bf16[256,4608]{1,0:T(8,128)(2,1)} %merge.1) | data formatting | bytes 4718592
  (19 shorter events, 0.0 us)
Async XLA Ops:
  0.6 3.3 %copy-start.7 = (bf16[256,4608]{1,0:T(8,128)(2,1)S(1)}, bf16[256,4608]{1,0:T(8,128)(2,1)}, u32[]{:S(2)}) copy-start(bf16[256,4608]{1,0:T(8,128)(2,1)} %refs_12_.1) | copy-start | bytes 7077892
  1.5 12.4 %slice-start = ((s8[9437184]{0:T(1024)(128)(4,1)}), s8[4194304]{0:T(1024)(128)(4,1)S(1)}, s32[]{:S(2)}) async-start(s8[9437184]{0:T(1024)(128)(4,1)} %bitcast.29), calls=%async_computation | async-start | bytes 8388608
  3.9 10.0 %slice-start.1 = ((s8[9437184]{0:T(1024)(128)(4,1)}), s8[4194304]{0:T(1024)(128)(4,1)S(1)}, s32[]{:S(2)}) async-start(s8[9437184]{0:T(1024)(128)(4,1)} %bitcast.29), calls=%async_computation.1 | async-start | bytes 8388608
  3.9 10.0 %slice-start.2 = ((s8[9437184]{0:T(1024)(128)(4,1)}), s8[1048576]{0:T(1024)(128)(4,1)S(1)}, s32[]{:S(2)}) async-start(s8[9437184]{0:T(1024)(128)(4,1)} %bitcast.29), calls=%async_computation.2 | async-start | bytes 2097152
  13.2 0.7 copy-start.6
  13.2 7.7 %slice-start.3 = ((s8[9437184]{0:T(1024)(128)(4,1)}), s8[4194304]{0:T(1024)(128)(4,1)S(1)}, s32[]{:S(2)}) async-start(s8[9437184]{0:T(1024)(128)(4,1)} %bitcast.31), calls=%async_computation.3 | async-start | bytes 8388608
  13.9 7.0 %slice-start.4 = ((s8[9437184]{0:T(1024)(128)(4,1)}), s8[4194304]{0:T(1024)(128)(4,1)S(1)}, s32[]{:S(2)}) async-start(s8[9437184]{0:T(1024)(128)(4,1)} %bitcast.31), calls=%async_computation.4 | async-start | bytes 8388608
  14.0 7.0 %slice-start.5 = ((s8[9437184]{0:T(1024)(128)(4,1)}), s8[1048576]{0:T(1024)(128)(4,1)S(1)}, s32[]{:S(2)}) async-start(s8[9437184]{0:T(1024)(128)(4,1)} %bitcast.31), calls=%async_computation.5 | async-start | bytes 2097152
  23.8 1.2 copy-start.8
  23.8 1.5 %copy-start.9 = (bf16[256,16,64]{2,1,0:T(8,128)(2,1)S(1)}, bf16[256,16,64]{2,1,0:T(8,128)(2,1)}, u32[]{:S(2)}) copy-start(bf16[256,16,64]{2,1,0:T(8,128)(2,1)} %get-tuple-element.40) | copy-start | bytes 1572868
  52.2 13.4 %copy-start = (f32[544,128]{1,0:T(8,128)}, f32[544,128]{1,0:T(8,128)S(1)}, u32[]{:S(2)}) copy-start(f32[544,128]{1,0:T(8,128)S(1)} %get-tuple-element.21.refs_0_) | copy-start | bytes 835588
  52.2 19.1 %copy-start.16 = (f32[4608]{0:T(1024)S(1)}, f32[4608]{0:T(1024)}, u32[]{:S(2)}) copy-start(f32[4608]{0:T(1024)} %param.17) | copy-start | bytes 55300
  65.6 19.7 %copy-start.1 = (f32[288,128]{1,0:T(8,128)}, f32[288,128]{1,0:T(8,128)S(1)}, u32[]{:S(2)}) copy-start(f32[288,128]{1,0:T(8,128)S(1)} %get-tuple-element.27.refs_4_) | copy-start | bytes 442372
  65.6 5.2 %collective-permute-start.3 = (f32[288,128]{1,0:T(8,128)S(1)}, f32[288,128]{1,0:T(8,128)S(1)}, u32[]{:S(2)}, u32[]{:S(2)}) collective-permute-start(f32[288,128]{1,0:T(8,128)S(1)} %get-tuple-element.28), channel_id=1, source_target_pairs={{0,1},{1,0},{2,3},{3,2},{4,5},{5,4},{6,7},{7,6}} | collective-permute-start | bytes 442376 | tf_op jit(solution)/shard_map/ppermute | solution.py:424
  66.5 21.5 %collective-permute-start = (f32[544,128]{1,0:T(8,128)S(1)}, f32[544,128]{1,0:T(8,128)S(1)}, u32[]{:S(2)}, u32[]{:S(2)}) collective-permute-start(f32[544,128]{1,0:T(8,128)S(1)} %get-tuple-element.22), channel_id=1, source_target_pairs={{0,1},{1,0},{2,3},{3,2},{4,5},{5,4},{6,7},{7,6}} | collective-permute-start | bytes 835592 | tf_op jit(solution)/shard_map/ppermute | solution.py:424
  66.5 21.4 %collective-permute-start.1 = (f32[544,128]{1,0:T(8,128)S(1)}, f32[544,128]{1,0:T(8,128)S(1)}, u32[]{:S(2)}, u32[]{:S(2)}) collective-permute-start(f32[544,128]{1,0:T(8,128)S(1)} %get-tuple-element.23), channel_id=1, source_target_pairs={{0,2},{1,3},{2,0},{3,1},{4,6},{5,7},{6,4},{7,5}} | collective-permute-start | bytes 835592 | tf_op jit(solution)/shard_map/ppermute | solution.py:424
  69.5 18.5 %collective-permute-start.2 = (f32[544,128]{1,0:T(8,128)S(1)}, f32[544,128]{1,0:T(8,128)S(1)}, u32[]{:S(2)}, u32[]{:S(2)}) collective-permute-start(f32[544,128]{1,0:T(8,128)S(1)} %get-tuple-element.24), channel_id=1, source_target_pairs={{0,3},{1,2},{2,1},{3,0},{4,7},{5,6},{6,5},{7,4}} | collective-permute-start | bytes 835592 | tf_op jit(solution)/shard_map/ppermute | solution.py:424
  69.5 18.5 %collective-permute-start.4 = (f32[288,128]{1,0:T(8,128)S(1)}, f32[288,128]{1,0:T(8,128)S(1)}, u32[]{:S(2)}, u32[]{:S(2)}) collective-permute-start(f32[288,128]{1,0:T(8,128)S(1)} %get-tuple-element.29), channel_id=1, source_target_pairs={{0,2},{1,3},{2,0},{3,1},{4,6},{5,7},{6,4},{7,5}} | collective-permute-start | bytes 442376 | tf_op jit(solution)/shard_map/ppermute | solution.py:424
  70.9 14.4 %copy-start.13 = (f32[288,128]{1,0:T(8,128)}, f32[288,128]{1,0:T(8,128)S(1)}, u32[]{:S(2)}) copy-start(f32[288,128]{1,0:T(8,128)S(1)} %collective-permute-done.3.refs_5_) | copy-start | bytes 442372
  70.9 17.1 %collective-permute-start.5 = (f32[288,128]{1,0:T(8,128)S(1)}, f32[288,128]{1,0:T(8,128)S(1)}, u32[]{:S(2)}, u32[]{:S(2)}) collective-permute-start(f32[288,128]{1,0:T(8,128)S(1)} %get-tuple-element.30), channel_id=1, source_target_pairs={{0,3},{1,2},{2,1},{3,0},{4,7},{5,6},{6,5},{7,4}} | collective-permute-start | bytes 442376 | tf_op jit(solution)/shard_map/ppermute | solution.py:424
  85.3 0.7 copy-start.2
  86.0 0.7 copy-start.3
  86.6 0.7 copy-start.4
  87.3 0.7 copy-start.5
  87.9 0.7 copy-start.14
  88.0 0.7 copy-start.15
  88.0 0.8 copy-start.10
  88.0 0.9 copy-start.11
  88.0 0.9 copy-start.12

commit v5 on v4

--- a/solution.py
+++ b/solution.py
@@ -20,21 +20,118 @@
 LAG_OUT = 4
 
 
-def rms_scale(tensor, gain_w):
-    mean_sq = jnp.mean(tensor * tensor, axis=-1, keepdims=True)
-    return tensor * lax.rsqrt(mean_sq + NORM_EPS) * (1.0 + gain_w)
-
-
-def rotary(tensor, positions):
-    half_dim = tensor.shape[-1] // 2
+def rotary_tables(positions, head_dim):
+    half_dim = head_dim // 2
     inv_freq = ROPE_BASE ** (-2.0 * jnp.arange(half_dim, dtype=jnp.float32) / (2 * half_dim))
     angles = positions.astype(jnp.float32)[:, None] * inv_freq[None, :]
-    angles = angles.reshape((angles.shape[0],) + (1,) * (tensor.ndim - 2) + (half_dim,))
     cos_tab = jnp.cos(angles)
     sin_tab = jnp.sin(angles)
-    lo_half = tensor[..., :half_dim]
-    hi_half = tensor[..., half_dim:]
-    return jnp.concatenate([lo_half * cos_tab - hi_half * sin_tab, hi_half * cos_tab + lo_half * sin_tab], axis=-1)
+    return jnp.concatenate([cos_tab, cos_tab], axis=-1), jnp.concatenate([-sin_tab, sin_tab], axis=-1)
+
+
+def project_kernel(x_ref, wpre_ref, cos_ref, sin_ref, wq_hbm, wk_hbm, wv_hbm, q_ref, k_ref, v_ref,
+                   weight, normed, q_part, k_part, v_part, w_sem, send_sem, recv_sem):
+    sp = lax.axis_index('sp')
+    core = lax.rem(sp, 2)
+    peer = {'sp': sp + 1 - 2 * core}
+    mesh_id = pl.DeviceIdType.MESH
+    rows = x_ref.shape[0]
+    block = weight.shape[2]
+    per = block // 128
+    plan = []
+    for w_hbm, part, turn in ((wq_hbm, q_part, True), (wk_hbm, k_part, True), (wv_hbm, v_part, False)):
+        mine = w_hbm.shape[1] // 2
+        for j in range(mine // block):
+            plan.append((w_hbm, part, turn, mine, j, j == mine // block - 1))
+
+    def load(i):
+        w_hbm, _, _, mine, j, _ = plan[i]
+        col = pl.multiple_of(core * mine + j * block, block)
+        return pltpu.make_async_copy(w_hbm.at[:, pl.ds(col, block)], weight.at[i], w_sem.at[i])
+
+    for i in range(len(plan)):
+        load(i).start()
+    barrier = pltpu.get_barrier_semaphore()
+    pl.semaphore_signal(barrier, inc=1, device_id=peer, device_id_type=mesh_id)
+    pl.semaphore_wait(barrier, 1)
+
+    gain = 1.0 + wpre_ref[...]
+
+    def norm(k, carry):
+        at = pl.ds(pl.multiple_of(k * 16, 16), 16)
+        x = x_ref[at, :].astype(jnp.float32)
+        inv = lax.rsqrt(jnp.mean(x * x, axis=-1, keepdims=True) + NORM_EPS)
+        normed[at, :] = (x * inv * gain).astype(jnp.bfloat16)
+        return carry
+
+    lax.fori_loop(0, rows // 16, norm, 0)
+
+    sends = []
+    for i, (_, part, turn, mine, j, done) in enumerate(plan):
+        load(i).wait()
+        heads = mine // 128
+        acc = jnp.dot(normed[...], weight[i], preferred_element_type=jnp.float32)
+        for t in range(per):
+            value = acc[:, t * 128:(t + 1) * 128]
+            if turn:
+                value = value * cos_ref[...] + pltpu.roll(value, 64, 1) * sin_ref[...]
+            part[core, pl.ds(j * per + t, rows, stride=heads), :] = value
+        if done:
+            n = len(sends)
+            copy = pltpu.make_async_remote_copy(src_ref=part.at[core], dst_ref=part.at[core], send_sem=send_sem.at[n],
+                                                recv_sem=recv_sem.at[n], device_id=peer, device_id_type=mesh_id)
+            copy.start()
+            sends.append(copy)
+    for copy in sends:
+        copy.wait()
+
+    q_heads = q_part.shape[1] // rows
+    kv = k_part.shape[1] // rows
+
+    def pack(k, carry):
+        for r in range(8):
+            b = k * 8 + r
+            at = pl.ds(pl.multiple_of(b * q_heads, q_heads), q_heads)
+            q_ref[b] = jnp.concatenate([q_part[0, at, :], q_part[1, at, :]], axis=0).astype(jnp.bfloat16)
+        for part, out in ((k_part, k_ref), (v_part, v_ref)):
+            group = pl.ds(pl.multiple_of(k * 8 * kv, 8), 8 * kv)
+            low, high = part[0, group, :], part[1, group, :]
+            for r in range(8):
+                both = [low[r * kv:(r + 1) * kv], high[r * kv:(r + 1) * kv]]
+                out[k * 8 + r] = jnp.concatenate(both + both, axis=0).astype(jnp.bfloat16)
+        return carry
+
+    lax.fori_loop(0, rows // 8, pack, 0)
+
+
+def project(x_in, w_pre, cos_tab, sin_tab, w_q, w_k, w_v):
+    rows, width = x_in.shape
+    block = 256
+    q_cols, kv_cols = w_q.shape[1], w_k.shape[1]
+    n_blocks = (q_cols + 2 * kv_cols) // 2 // block
+    vmem = pl.BlockSpec(memory_space=pltpu.VMEM)
+    hbm = pl.BlockSpec(memory_space=pltpu.HBM)
+    f32, bf = jnp.float32, jnp.bfloat16
+    dma = pltpu.SemaphoreType.DMA
+    return pl.pallas_call(
+        project_kernel,
+        out_shape=(jax.ShapeDtypeStruct((rows, q_cols // 128, 128), bf),
+                   jax.ShapeDtypeStruct((rows, kv_cols // 64, 128), bf),
+                   jax.ShapeDtypeStruct((rows, kv_cols // 64, 128), bf)),
+        in_specs=[vmem] * 4 + [hbm] * 3,
+        out_specs=(vmem,) * 3,
+        scratch_shapes=[
+            pltpu.VMEM((n_blocks, width, block), bf),
+            pltpu.VMEM((rows, width), bf),
+            pltpu.VMEM((2, rows * q_cols // 256, 128), f32),
+            pltpu.VMEM((2, rows * kv_cols // 256, 128), f32),
+            pltpu.VMEM((2, rows * kv_cols // 256, 128), f32),
+            dma((n_blocks,)), dma((3,)), dma((3,)),
+        ],
+        compiler_params=pltpu.CompilerParams(vmem_limit_bytes=44 * 1024 * 1024, collective_id=1, has_side_effects=True),
+        cost_estimate=pl.CostEstimate(flops=rows * width * (q_cols + 2 * kv_cols), bytes_accessed=width * (q_cols + 2 * kv_cols), transcendentals=0),
+        name='project',
+    )(x_in, w_pre, cos_tab, sin_tab, w_q, w_k, w_v)
 
 
 def attend_kernel(n_steps, first_row, kv_heads, seq_block, pos_ref, base_ref, q_hbm, kn_hbm, vn_hbm, k_hbm, v_hbm,
@@ -177,7 +274,7 @@
     seq_block = cols // kv_heads
     n_steps = n_rows // ROWS_STEP
     hbm = pl.BlockSpec(memory_space=pl.ANY)
-    piece = jax.ShapeDtypeStruct((n_rows // 4 * heads + 2 * heads, head_dim), jnp.float32)
+    piece = pltpu.HBM((n_rows // 4 * heads + 2 * heads, head_dim), jnp.float32)
     smem = pl.BlockSpec(memory_space=pltpu.SMEM)
     bf = jnp.bfloat16
     aliases = {} if prev is None else {7: 0, 8: 1}
@@ -186,7 +283,7 @@
         functools.partial(attend_kernel, n_steps, first_row, kv_heads, seq_block),
         out_shape=(jax.ShapeDtypeStruct(k_cache.shape, bf), jax.ShapeDtypeStruct(v_cache.shape, bf)) + (piece,) * 4,
         in_specs=[smem, smem, hbm, hbm, hbm, hbm, hbm] + [hbm] * len(extra),
-        out_specs=(hbm,) * 6,
+        out_specs=(hbm, hbm) + (pl.BlockSpec(memory_space=pltpu.HBM),) * 4,
         scratch_shapes=[
             pltpu.VMEM((heads, 128), jnp.float32),
             pltpu.VMEM((heads, 128), jnp.float32),
@@ -373,7 +470,7 @@
     return pl.pallas_call(
         functools.partial(merge_kernel, chunks),
         out_shape=jax.ShapeDtypeStruct(x_in.shape, x_in.dtype),
-        in_specs=[hbm] * (len(flat) + 3),
+        in_specs=[pl.BlockSpec(memory_space=pltpu.HBM)] * (len(flat) + 3),
         out_specs=vmem,
         scratch_shapes=[
             pltpu.VMEM((n_chunks, inner, chunk), jnp.bfloat16),
@@ -399,17 +496,9 @@
 
     def local_step(x_in, cur_pos, w_pre, w_q, w_k, w_v, w_o, w_post, k_cache, v_cache):
         row_count, seq_block, kv_local, head_dim = k_cache.shape
-        heads_local = w_q.shape[1] // head_dim
         sp_index = lax.axis_index('sp')
-        x_f = x_in.astype(jnp.float32)
-        normed = rms_scale(x_f, w_pre).astype(jnp.bfloat16)
-        q_proj = jnp.dot(normed, w_q, preferred_element_type=jnp.float32)
-        q_rot = rotary(q_proj.reshape(row_count, heads_local, head_dim), cur_pos).astype(jnp.bfloat16)
-        k_proj = jnp.dot(normed, w_k, preferred_element_type=jnp.float32)
-        k_new = rotary(k_proj.reshape(row_count, kv_local, head_dim), cur_pos).astype(jnp.bfloat16)
-        v_new = jnp.dot(normed, w_v, preferred_element_type=jnp.float32).reshape(row_count, kv_local, head_dim).astype(jnp.bfloat16)
-        kn2 = jnp.concatenate([k_new, k_new], axis=1)
-        vn2 = jnp.concatenate([v_new, v_new], axis=1)
+        cos_tab, sin_tab = rotary_tables(cur_pos, head_dim)
+        q_rot, kn2, vn2 = project(x_in, w_pre.reshape(1, -1), cos_tab, sin_tab, w_q, w_k, w_v)
         base = (sp_index * seq_block).astype(jnp.int32).reshape(1)
         kc = k_cache.reshape(row_count, seq_block * kv_local, head_dim)
         vc = v_cache.reshape(row_count, seq_block * kv_local, head_dim)

time: 141 us -> 134 us (0.950)
  Pallas kernels: 99.8 us -> 117 us
  matrix products: 14.8 us -> 0 us
  other arithmetic: 10.1 us -> 1.36 us
  local copies, waits for them, and re-layouts: 9.83 us -> 7.19 us
  waiting for transfers between devices: 0.04 us -> 2.36 us
    pallas_call x0 -> x1, Pallas kernels: none -> 16.8 us  [project(): pl.pallas_call(project_kernel, out_shape=(jax.ShapeDtypeStruct((rows, q_c...]
    dot_general x3 -> x0, matrix products: 14.8 us -> none  [the longest x1 9.28 us: local_step(): q_proj = jnp.dot(normed, w_q, preferred_element_type=jnp.float32)]
    another operation x2 -> x0, other arithmetic: 3.52 us -> none
    unnamed x51 -> x25, local copies, waits for them, and re-layouts: 9.07 us -> 5.83 us
    concatenate x1, other arithmetic: 2.75 us -> 0.13 us  [rotary_tables(): jnp.concatenate([cos_tab, cos_tab], axis=-1)]
    reduce_sum x1 -> x0, other arithmetic: 2.36 us -> none  [rms_scale(): mean_sq = jnp.mean(tensor * tensor, axis=-1, keepdims=True)]
    ppermute x6, waiting for transfers between devices: 0.04 us -> 2.36 us  [local_step(): moved.append(lax.ppermute(p, 'sp', [(i, i ^ d) for i in range(sp_size)]))]
    pallas_call x3, Pallas kernels: 50.9 us -> 52.5 us  [attend(): pl.pallas_call(functools.partial(attend_kernel, n_steps, first_row, kv_he...]
  transfers between devices with their start and end apart: 6 -> 6, of which waited for: 0 -> 2; matrix products, arithmetic and copies ran while one was open for 0% -> 0% of each run, Pallas kernels for 9% -> 10%
where the time goes in v5:
time: 134 us
  Pallas kernels  117 us (87%)
  local copies, waits for them, and re-layouts  7.19 us (5%)
  starting transfers between devices  5.15 us (4%)
  waiting for transfers between devices  2.36 us (2%)
  other arithmetic  1.36 us (1%)
    pallas_call x3, Pallas kernels, attend(): pl.pallas_call(functools.partial(attend_kernel, n_steps, first_row, kv_he...  52.5 us
    pallas_call x1, Pallas kernels, merge(): pl.pallas_call(functools.partial(merge_kernel, chunks), out_shape=jax.Sha...  47.8 us
    pallas_call x1, Pallas kernels, project(): pl.pallas_call(project_kernel, out_shape=(jax.ShapeDtypeStruct((rows, q_c...  16.8 us
    unnamed x25, local copies, waits for them, and re-layouts  5.83 us
    ppermute x6, starting transfers between devices, local_step(): moved.append(lax.ppermute(p, 'sp', [(i, i ^ d) for i in range(sp_size)]))  5.15 us
  transfers between devices with their start and end apart: 6, of which 2 were waited for; matrix products, arithmetic and copies ran while one was open for 0% of the time, Pallas kernels for 10%

profile of v5, /device:TPU:0, one launch (start us, length us, event | category | flops | bytes accessed | tf_op | source)
XLA Modules:
  0.0 134.0 jit_solution(9193779460916015676)
XLA Ops:
  0.6 0.0 copy-start.1
  0.7 0.7 reshape.34.wpre_ref
  1.4 0.7 convert_element_type.3
  2.1 0.5 fusion
  2.6 0.1 pad_maximum_fusion
  2.8 0.0 copy-start
  2.8 1.7 %copy-done = bf16[256,4608]{1,0:T(8,128)(2,1)S(1)} copy-done((bf16[256,4608]{1,0:T(8,128)(2,1)S(1)}, bf16[256,4608]{1,0:T(8,128)(2,1)}, u32[]{:S(2)}) %copy-start) | copy-done | bytes 2359320
  4.4 16.8 %project.1 = (bf16[256,16,128]{2,1,0:T(8,128)(2,1)S(1)}, bf16[256,16,128]{2,1,0:T(8,128)(2,1)S(1)}, bf16[256,16,128]{2,1,0:T(8,128)(2,1)S(1)}) custom-call(bf16[256,4608]{1,0:T(8,128)(2,1)S(1)} %copy-done, f32[1,4608]{1,0:T(1,128)S(1)} %reshape.34.wpre_ref, f32[256,128]{1,0:T(8,128)S(1)} %get-tuple-element.48.cos_ref, ...), custom_call_target="tpu_custom_call" | custom-call | flops 4831838208 | bytes 18874368 | tf_op jit(solution)/shard_map/project/pallas_call | solution.py:116
  21.3 0.0 copy-done.1
  21.3 24.7 %attend.3 = (bf16[256,512,128]{2,1,0:T(8,128)(2,1)}, bf16[256,512,128]{2,1,0:T(8,128)(2,1)}, f32[544,128]{1,0:T(8,128)}, f32[544,128]{1,0:T(8,128)}, f32[544,128]{1,0:T(8,128)}, /*index=5*/f32[544,128]{1,0:T(8,128)}) custom-call(s32[256]{0:T(256)S(1)} %copy-done.1, s32[1]{0:T(128)} %bitcast.base_ref, bf16[256,16,128]{2,1,0:T(8,128)(2,1)S(1)} %get-tuple-element.24.q_hbm, ...), custom_call_target="tpu_custom_call" | custom-call | flops 536870912 | bytes 67108864 | tf_op jit(solution)/shard_map/attend/pallas_call | solution.py:282
  46.0 0.0 copy-start.11
  46.0 0.0 copy-start.10
  46.0 0.0 copy-start.9
  46.0 0.0 copy-start.8
  46.0 13.9 %attend.4 = (bf16[256,512,128]{2,1,0:T(8,128)(2,1)}, bf16[256,512,128]{2,1,0:T(8,128)(2,1)}, f32[288,128]{1,0:T(8,128)}, f32[288,128]{1,0:T(8,128)}, f32[288,128]{1,0:T(8,128)}, /*index=5*/f32[288,128]{1,0:T(8,128)}) custom-call(s32[256]{0:T(256)S(1)} %copy-done.1, s32[1]{0:T(128)} %bitcast.base_ref, ...), custom_call_target="tpu_custom_call", output_to_operand_aliasing={{0}: (7, {}), {1}: (8, {})} | custom-call | flops 268435456 | bytes 33554432 | tf_op jit(solution)/shard_map/attend/pallas_call | solution.py:282
  59.9 0.4 collective-permute-start.3
  60.3 0.0 copy-done.11
  60.3 0.1 collective-permute-start
  60.5 0.0 copy-done.10
  60.5 2.8 %collective-permute-start.1 = (f32[544,128]{1,0:T(8,128)S(1)}, f32[544,128]{1,0:T(8,128)S(1)}, u32[]{:S(2)}, u32[]{:S(2)}) collective-permute-start(f32[544,128]{1,0:T(8,128)S(1)} %copy-done.10), channel_id=1, source_target_pairs={{0,2},{1,3},{2,0},{3,1},{4,6},{5,7},{6,4},{7,5}} | collective-permute-start | bytes 835592 | tf_op jit(solution)/shard_map/ppermute | solution.py:513
  63.3 0.0 copy-done.9
  63.3 0.0 collective-permute-start.2
  63.3 1.5 %collective-permute-start.4 = (f32[288,128]{1,0:T(8,128)}, f32[288,128]{1,0:T(8,128)S(1)}, u32[]{:S(2)}, u32[]{:S(2)}) collective-permute-start(f32[288,128]{1,0:T(8,128)} %get-tuple-element.35), channel_id=1, source_target_pairs={{0,2},{1,3},{2,0},{3,1},{4,6},{5,7},{6,4},{7,5}} | collective-permute-start | bytes 442376 | tf_op jit(solution)/shard_map/ppermute | solution.py:513
  64.8 0.0 collective-permute-done.3.refs_5_
  64.8 0.0 copy-start.5
  64.8 0.3 collective-permute-start.5
  65.1 0.0 copy-done.8
  65.1 0.6 reshape.37.refs_13_
  65.7 13.9 %attend.5 = (bf16[256,512,128]{2,1,0:T(8,128)(2,1)}, bf16[256,512,128]{2,1,0:T(8,128)(2,1)}, f32[288,128]{1,0:T(8,128)}, f32[288,128]{1,0:T(8,128)}, f32[288,128]{1,0:T(8,128)}, /*index=5*/f32[288,128]{1,0:T(8,128)}) custom-call(s32[256]{0:T(256)S(1)} %copy-done.1, s32[1]{0:T(128)} %bitcast.base_ref, ...), custom_call_target="tpu_custom_call", output_to_operand_aliasing={{0}: (7, {}), {1}: (8, {})} | custom-call | flops 268435456 | bytes 33554432 | tf_op jit(solution)/shard_map/attend/pallas_call | solution.py:282
  79.7 0.0 copy-done.5
  79.7 0.3 collective-permute-done.4.refs_6_
  80.0 0.0 copy-start.6
  80.0 2.1 %collective-permute-done.5.refs_7_ = f32[288,128]{1,0:T(8,128)S(1)} collective-permute-done((f32[288,128]{1,0:T(8,128)}, f32[288,128]{1,0:T(8,128)S(1)}, u32[]{:S(2)}, u32[]{:S(2)}) %collective-permute-start.5) | collective-permute-done | bytes 147488 | tf_op jit(solution)/shard_map/ppermute | solution.py:513
  82.0 0.0 copy-start.7
  82.0 0.0 collective-permute-done.refs_1_
  82.0 0.0 copy-start.2
  82.0 0.0 collective-permute-done.1.refs_2_
  82.0 0.0 copy-start.3
  82.0 0.0 collective-permute-done.2.refs_3_
  82.1 0.0 copy-start.4
  82.1 0.0 copy-done.6
  82.1 0.6 copy-done.7
  82.7 0.1 copy-done.2
  82.8 0.1 copy-done.3
  82.9 0.1 copy-done.4
  83.0 47.8 %merge.1 = bf16[256,4608]{1,0:T(8,128)(2,1)} custom-call(f32[544,128]{1,0:T(8,128)} %get-tuple-element.27.refs_0_, f32[544,128]{1,0:T(8,128)} %copy-done.2, f32[544,128]{1,0:T(8,128)} %copy-done.3, f32[544,128]{1,0:T(8,128)} %copy-done.4, f32[288,128]{1,0:T(8,128)} %get-tuple-element.33.refs_4_, f32[288,128]{1,0:T(8,128)} %copy-done.5, ...), custom_call_target="tpu_custom_call" | custom-call | flops 1207959552 | bytes 18874368 | tf_op jit(solution)/shard_map/merge/pallas_call | solution.py:470
  130.8 3.2 %copy.22 = bf16[256,4608]{1,0:T(8,128)(2,1)} copy(bf16[256,4608]{1,0:T(8,128)(2,1)} %merge.1) | data formatting | bytes 4718592
  (1 shorter events, 0.0 us)
Async XLA Ops:
  0.6 20.7 %copy-start.1 = (s32[256]{0:T(256)S(1)}, s32[256]{0:T(256)}, u32[]{:S(2)}) copy-start(s32[256]{0:T(256)} %pos_ref.5) | copy-start | bytes 3076
  2.8 1.7 %copy-start = (bf16[256,4608]{1,0:T(8,128)(2,1)S(1)}, bf16[256,4608]{1,0:T(8,128)(2,1)}, u32[]{:S(2)}) copy-start(bf16[256,4608]{1,0:T(8,128)(2,1)} %refs_12_.1) | copy-start | bytes 7077892
  46.0 14.4 %copy-start.11 = (f32[544,128]{1,0:T(8,128)S(1)}, f32[544,128]{1,0:T(8,128)}, u32[]{:S(2)}) copy-start(f32[544,128]{1,0:T(8,128)} %get-tuple-element.28) | copy-start | bytes 835588
  46.0 14.5 %copy-start.10 = (f32[544,128]{1,0:T(8,128)S(1)}, f32[544,128]{1,0:T(8,128)}, u32[]{:S(2)}) copy-start(f32[544,128]{1,0:T(8,128)} %get-tuple-element.29) | copy-start | bytes 835588
  46.0 17.3 %copy-start.9 = (f32[544,128]{1,0:T(8,128)S(1)}, f32[544,128]{1,0:T(8,128)}, u32[]{:S(2)}) copy-start(f32[544,128]{1,0:T(8,128)} %get-tuple-element.30) | copy-start | bytes 835588
  46.0 19.1 %copy-start.8 = (f32[4608]{0:T(1024)S(1)}, f32[4608]{0:T(1024)}, u32[]{:S(2)}) copy-start(f32[4608]{0:T(1024)} %param.17) | copy-start | bytes 55300
  59.9 4.9 %collective-permute-start.3 = (f32[288,128]{1,0:T(8,128)}, f32[288,128]{1,0:T(8,128)S(1)}, u32[]{:S(2)}, u32[]{:S(2)}) collective-permute-start(f32[288,128]{1,0:T(8,128)} %get-tuple-element.34), channel_id=1, source_target_pairs={{0,1},{1,0},{2,3},{3,2},{4,5},{5,4},{6,7},{7,6}} | collective-permute-start | bytes 442376 | tf_op jit(solution)/shard_map/ppermute | solution.py:513
  60.3 21.7 %collective-permute-start = (f32[544,128]{1,0:T(8,128)S(1)}, f32[544,128]{1,0:T(8,128)S(1)}, u32[]{:S(2)}, u32[]{:S(2)}) collective-permute-start(f32[544,128]{1,0:T(8,128)S(1)} %copy-done.11), channel_id=1, source_target_pairs={{0,1},{1,0},{2,3},{3,2},{4,5},{5,4},{6,7},{7,6}} | collective-permute-start | bytes 835592 | tf_op jit(solution)/shard_map/ppermute | solution.py:513
  60.5 21.5 %collective-permute-start.1 = (f32[544,128]{1,0:T(8,128)S(1)}, f32[544,128]{1,0:T(8,128)S(1)}, u32[]{:S(2)}, u32[]{:S(2)}) collective-permute-start(f32[544,128]{1,0:T(8,128)S(1)} %copy-done.10), channel_id=1, source_target_pairs={{0,2},{1,3},{2,0},{3,1},{4,6},{5,7},{6,4},{7,5}} | collective-permute-start | bytes 835592 | tf_op jit(solution)/shard_map/ppermute | solution.py:513
  63.3 18.7 %collective-permute-start.2 = (f32[544,128]{1,0:T(8,128)S(1)}, f32[544,128]{1,0:T(8,128)S(1)}, u32[]{:S(2)}, u32[]{:S(2)}) collective-permute-start(f32[544,128]{1,0:T(8,128)S(1)} %copy-done.9), channel_id=1, source_target_pairs={{0,3},{1,2},{2,1},{3,0},{4,7},{5,6},{6,5},{7,4}} | collective-permute-start | bytes 835592 | tf_op jit(solution)/shard_map/ppermute | solution.py:513
  63.3 16.6 %collective-permute-start.4 = (f32[288,128]{1,0:T(8,128)}, f32[288,128]{1,0:T(8,128)S(1)}, u32[]{:S(2)}, u32[]{:S(2)}) collective-permute-start(f32[288,128]{1,0:T(8,128)} %get-tuple-element.35), channel_id=1, source_target_pairs={{0,2},{1,3},{2,0},{3,1},{4,6},{5,7},{6,4},{7,5}} | collective-permute-start | bytes 442376 | tf_op jit(solution)/shard_map/ppermute | solution.py:513
  64.8 14.8 %copy-start.5 = (f32[288,128]{1,0:T(8,128)}, f32[288,128]{1,0:T(8,128)S(1)}, u32[]{:S(2)}) copy-start(f32[288,128]{1,0:T(8,128)S(1)} %collective-permute-done.3.refs_5_) | copy-start | bytes 442372
  64.8 17.2 %collective-permute-start.5 = (f32[288,128]{1,0:T(8,128)}, f32[288,128]{1,0:T(8,128)S(1)}, u32[]{:S(2)}, u32[]{:S(2)}) collective-permute-start(f32[288,128]{1,0:T(8,128)} %get-tuple-element.36), channel_id=1, source_target_pairs={{0,3},{1,2},{2,1},{3,0},{4,7},{5,6},{6,5},{7,4}} | collective-permute-start | bytes 442376 | tf_op jit(solution)/shard_map/ppermute | solution.py:513
  80.0 2.1 %copy-start.6 = (f32[288,128]{1,0:T(8,128)}, f32[288,128]{1,0:T(8,128)S(1)}, u32[]{:S(2)}) copy-start(f32[288,128]{1,0:T(8,128)S(1)} %collective-permute-done.4.refs_6_) | copy-start | bytes 442372
  82.0 0.7 copy-start.7
  82.0 0.8 copy-start.2
  82.0 0.9 copy-start.3
  82.1 0.9 copy-start.4

commit v6 on v5

--- a/solution.py
+++ b/solution.py
@@ -2,6 +2,7 @@
 
 import jax
 import jax.numpy as jnp
+import numpy as np
 from jax import lax
 from jax.experimental import pallas as pl
 from jax.experimental.pallas import tpu as pltpu
@@ -13,24 +14,24 @@
 NORM_EPS = 1e-6
 LOG2E = 1.4426950408889634
 
-ROWS_STEP = 16
-SLOTS = 5
-AHEAD = 3
+ROWS_STEP = 8
+SLOTS = 8
+AHEAD = 5
 LAG_SOFT = 2
 LAG_OUT = 4
 
 
-def rotary_tables(positions, head_dim):
+def rotary_table(length, head_dim):
     half_dim = head_dim // 2
-    inv_freq = ROPE_BASE ** (-2.0 * jnp.arange(half_dim, dtype=jnp.float32) / (2 * half_dim))
-    angles = positions.astype(jnp.float32)[:, None] * inv_freq[None, :]
-    cos_tab = jnp.cos(angles)
-    sin_tab = jnp.sin(angles)
-    return jnp.concatenate([cos_tab, cos_tab], axis=-1), jnp.concatenate([-sin_tab, sin_tab], axis=-1)
-
-
-def project_kernel(x_ref, wpre_ref, cos_ref, sin_ref, wq_hbm, wk_hbm, wv_hbm, q_ref, k_ref, v_ref,
-                   weight, normed, q_part, k_part, v_part, w_sem, send_sem, recv_sem):
+    inv_freq = np.power(np.float32(ROPE_BASE), -2.0 * np.arange(half_dim, dtype=np.float32) / np.float32(2 * half_dim)).astype(np.float32)
+    angles = np.arange(length, dtype=np.float32)[:, None] * inv_freq[None, :]
+    cos_tab = np.cos(angles.astype(np.float64))
+    sin_tab = np.sin(angles.astype(np.float64))
+    return np.concatenate([cos_tab, cos_tab, -sin_tab, sin_tab], axis=-1).astype(np.float32)
+
+
+def project_kernel(pos_ref, x_hbm, wpre_ref, table_ref, wq_hbm, wk_hbm, wv_hbm, q_ref, k_ref, v_ref,
+                   x_ref, gain_ref, cos_ref, sin_ref, weight, normed, q_part, k_part, v_part, x_sem, w_sem, send_sem, recv_sem):
     sp = lax.axis_index('sp')
     core = lax.rem(sp, 2)
     peer = {'sp': sp + 1 - 2 * core}
@@ -49,13 +50,29 @@
         col = pl.multiple_of(core * mine + j * block, block)
         return pltpu.make_async_copy(w_hbm.at[:, pl.ds(col, block)], weight.at[i], w_sem.at[i])
 
+    x_loads = [pltpu.make_async_copy(x_hbm.at[pl.ds(k * (rows // 4), rows // 4)], x_ref.at[pl.ds(k * (rows // 4), rows // 4)],
+                                     x_sem.at[k]) for k in range(4)]
+    for copy in x_loads:
+        copy.start()
     for i in range(len(plan)):
         load(i).start()
     barrier = pltpu.get_barrier_semaphore()
     pl.semaphore_signal(barrier, inc=1, device_id=peer, device_id_type=mesh_id)
     pl.semaphore_wait(barrier, 1)
 
-    gain = 1.0 + wpre_ref[...]
+    for j in range(wpre_ref.shape[0]):
+        gain_ref[:, j * 128:(j + 1) * 128] = 1.0 + wpre_ref[j:j + 1, :]
+    gain = gain_ref[...]
+
+    def look_up(k, carry):
+        for r in range(8):
+            b = k * 8 + r
+            row = table_ref[pl.ds(pos_ref[b], 1), :]
+            cos_ref[pl.ds(b, 1), :] = row[:, :128]
+            sin_ref[pl.ds(b, 1), :] = row[:, 128:]
+        return carry
+
+    lax.fori_loop(0, rows // 8, look_up, 0)
 
     def norm(k, carry):
         at = pl.ds(pl.multiple_of(k * 16, 16), 16)
@@ -64,7 +81,9 @@
         normed[at, :] = (x * inv * gain).astype(jnp.bfloat16)
         return carry
 
-    lax.fori_loop(0, rows // 16, norm, 0)
+    for k in range(4):
+        x_loads[k].wait()
+        lax.fori_loop(k * rows // 64, (k + 1) * rows // 64, norm, 0)
 
     sends = []
     for i, (_, part, turn, mine, j, done) in enumerate(plan):
@@ -104,9 +123,9 @@
     lax.fori_loop(0, rows // 8, pack, 0)
 
 
-def project(x_in, w_pre, cos_tab, sin_tab, w_q, w_k, w_v):
+def project(cur_pos, x_in, w_pre, table, w_q, w_k, w_v):
     rows, width = x_in.shape
-    block = 256
+    block = 512
     q_cols, kv_cols = w_q.shape[1], w_k.shape[1]
     n_blocks = (q_cols + 2 * kv_cols) // 2 // block
     vmem = pl.BlockSpec(memory_space=pltpu.VMEM)
@@ -118,20 +137,24 @@
         out_shape=(jax.ShapeDtypeStruct((rows, q_cols // 128, 128), bf),
                    jax.ShapeDtypeStruct((rows, kv_cols // 64, 128), bf),
                    jax.ShapeDtypeStruct((rows, kv_cols // 64, 128), bf)),
-        in_specs=[vmem] * 4 + [hbm] * 3,
+        in_specs=[pl.BlockSpec(memory_space=pltpu.SMEM), hbm, vmem, vmem] + [hbm] * 3,
         out_specs=(vmem,) * 3,
         scratch_shapes=[
+            pltpu.VMEM((rows, width), bf),
+            pltpu.VMEM((1, width), f32),
+            pltpu.VMEM((rows, 128), f32),
+            pltpu.VMEM((rows, 128), f32),
             pltpu.VMEM((n_blocks, width, block), bf),
             pltpu.VMEM((rows, width), bf),
             pltpu.VMEM((2, rows * q_cols // 256, 128), f32),
             pltpu.VMEM((2, rows * kv_cols // 256, 128), f32),
             pltpu.VMEM((2, rows * kv_cols // 256, 128), f32),
-            dma((n_blocks,)), dma((3,)), dma((3,)),
+            dma((4,)), dma((n_blocks,)), dma((3,)), dma((3,)),
         ],
-        compiler_params=pltpu.CompilerParams(vmem_limit_bytes=44 * 1024 * 1024, collective_id=1, has_side_effects=True),
+        compiler_params=pltpu.CompilerParams(vmem_limit_bytes=62 * 1024 * 1024, collective_id=1, has_side_effects=True),
         cost_estimate=pl.CostEstimate(flops=rows * width * (q_cols + 2 * kv_cols), bytes_accessed=width * (q_cols + 2 * kv_cols), transcendentals=0),
         name='project',
-    )(x_in, w_pre, cos_tab, sin_tab, w_q, w_k, w_v)
+    )(cur_pos, x_in, w_pre, table, w_q, w_k, w_v)
 
 
 def attend_kernel(n_steps, first_row, kv_heads, seq_block, pos_ref, base_ref, q_hbm, kn_hbm, vn_hbm, k_hbm, v_hbm,
@@ -380,59 +403,89 @@
         combine(pieces[c], parts[c], row0)
         row0 += parts[c]
 
+    first_at, last_at = pl.ds(0, first), pl.ds(first, quarter - first)
+    split = ((2, 2, 2, 2, 1), (1, 2, 2, 2, 2))
     wide = 3
-    first_at, last_at = pl.ds(0, first), pl.ds(first, quarter - first)
-    order = [(pl.ds(n, 1), first_at) for n in range(n_chunks)] + [(pl.ds(n, wide), last_at) for n in range(0, n_chunks, wide)]
-
-    def to_y(t):
-        ns, r = order[t]
+    orders = []
+    for sizes in split:
+        begin, order = 0, []
+        for size in sizes:
+            order.append((begin, size, first_at))
+            begin += size
+        orders.append(order + [(n, wide, last_at) for n in range(0, n_chunks, wide)])
+    n_first = len(split[0])
+    n_pieces = len(orders[0])
+
+    def to_y(v, t):
+        n, size, r = orders[v][t]
+        ns = pl.ds(n, size)
         return remote(y_out.at[ns, r], y_in.at[ns, r], y_send.at[t], y_recv.at[t], y_peer)
 
-    def to_x(t):
-        ns, r = order[t]
+    def to_x(v, t):
+        n, size, r = orders[v][t]
+        ns = pl.ds(n, size)
         return remote(sums.at[sp, ns, r], sums.at[sp, ns, r], g_send.at[t], g_recv.at[t], x_peer)
 
-    def to_core(t):
-        ns, r = order[t]
+    def to_core(v, t):
+        n, size, r = orders[v][t]
+        ns = pl.ds(n, size)
         return remote(sums.at[sp, ns, r], sums.at[sp, ns, r], d_send.at[t], d_recv.at[t], core_peer)
 
-    def relay(t):
-        ns, r = order[t]
+    def relay(v, t):
+        n, size, r = orders[v][t]
+        ns = pl.ds(n, size)
         other = 2 * (1 - xpos) + core
         return remote(sums.at[other, ns, r], sums.at[other, ns, r], f_send.at[t], f_recv.at[t], core_peer)
 
-    def project(n, r0, count):
+    def project_rows(n, r0, count):
         y_out[n, r0:r0 + count, :] = jnp.dot(lhs[r0:r0 + count, :], wo[n], preferred_element_type=jnp.float32)
 
     for n in range(n_chunks):
         w_load(n).wait()
-        project(n, 0, first)
-        to_y(n).start()
-
-    for t in range(len(order) + 1):
-        if t == 2:
+        project_rows(n, 0, first)
+        for v in range(2):
+            for t in range(n_first):
+                if sum(orders[v][t][:2]) == n + 1:
+                    @pl.when(core == v)
+                    def _():
+                        to_y(v, t).start()
+
+    def step(v, t):
+        if t < n_pieces:
+            n, size, r = orders[v][t]
+            ns = pl.ds(n, size)
+            to_y(v, t).wait()
+            sums[sp, ns, r, :] = y_out[ns, r, :] + y_in[ns, r, :]
+            to_x(v, t).start()
+            to_core(v, t).start()
+        if t >= 1:
+            to_x(v, t - 1).wait_recv()
+            relay(v, t - 1).start()
+
+    for t in range(n_pieces + 1):
+        if t == 1:
             for copy in last:
                 copy.wait()
             combine([pieces[-1][0]] + [last_in.at[d] for d in range(3)], parts[-1], first)
-        if 2 <= t < 2 + n_chunks // wide:
-            for n in range((t - 2) * wide, (t - 1) * wide):
-                project(n, first, quarter - first)
-            to_y(n_chunks + t - 2).start()
-        if t < len(order):
-            ns, r = order[t]
-            to_y(t).wait()
-            sums[sp, ns, r, :] = y_out[ns, r, :] + y_in[ns, r, :]
-            to_x(t).start()
-            to_core(t).start()
-        if t >= 1:
-            to_x(t - 1).wait_recv()
-            relay(t - 1).start()
+        if 1 <= t < 1 + n_chunks // wide:
+            for n in range((t - 1) * wide, t * wide):
+                project_rows(n, first, quarter - first)
+            to_y(0, n_first + t - 1).start()
+        for v in range(2):
+            @pl.when(core == v)
+            def _():
+                step(v, t)
     for copy in small:
         copy.wait()
-    for t in range(len(order)):
-        to_x(t).wait_send()
-        to_core(t).wait()
-        relay(t).wait()
+    for v in range(2):
+        @pl.when(core == v)
+        def _():
+            for t in range(n_pieces):
+                to_x(v, t).wait_send()
+                to_core(v, t).wait_send()
+                relay(v, t).wait_send()
+                to_core(1 - v, t).wait_recv()
+                relay(1 - v, t).wait_recv()
 
     starts = []
     base = 0
@@ -497,8 +550,8 @@
     def local_step(x_in, cur_pos, w_pre, w_q, w_k, w_v, w_o, w_post, k_cache, v_cache):
         row_count, seq_block, kv_local, head_dim = k_cache.shape
         sp_index = lax.axis_index('sp')
-        cos_tab, sin_tab = rotary_tables(cur_pos, head_dim)
-        q_rot, kn2, vn2 = project(x_in, w_pre.reshape(1, -1), cos_tab, sin_tab, w_q, w_k, w_v)
+        table = rotary_table(sp_size * seq_block, head_dim)
+        q_rot, kn2, vn2 = project(cur_pos, x_in, w_pre.reshape(-1, 128), table, w_q, w_k, w_v)
         base = (sp_index * seq_block).astype(jnp.int32).reshape(1)
         kc = k_cache.reshape(row_count, seq_block * kv_local, head_dim)
         vc = v_cache.reshape(row_count, seq_block * kv_local, head_dim)

time: 134 us -> 135 us (level)
  other arithmetic: 1.36 us -> 0 us
    unnamed x25 -> x29, local copies, waits for them, and re-layouts: 5.83 us -> 7.84 us
where the time goes in v6:
time: 135 us
  Pallas kernels  118 us (87%)
  local copies, waits for them, and re-layouts  8.46 us (6%)
  starting transfers between devices  4.95 us (4%)
  waiting for transfers between devices  3.13 us (2%)
    pallas_call x3, Pallas kernels, attend(): pl.pallas_call(functools.partial(attend_kernel, n_steps, first_row, kv_he...  51.7 us
    pallas_call x1, Pallas kernels, merge(): pl.pallas_call(functools.partial(merge_kernel, chunks), out_shape=jax.Sha...  48.5 us
    pallas_call x1, Pallas kernels, project(): pl.pallas_call(project_kernel, out_shape=(jax.ShapeDtypeStruct((rows, q_c...  17.7 us
    unnamed x29, local copies, waits for them, and re-layouts  7.84 us
    ppermute x6, starting transfers between devices, local_step(): moved.append(lax.ppermute(p, 'sp', [(i, i ^ d) for i in range(sp_size)]))  4.95 us
    ppermute x6, waiting for transfers between devices, local_step(): moved.append(lax.ppermute(p, 'sp', [(i, i ^ d) for i in range(sp_size)]))  3.13 us
  transfers between devices with their start and end apart: 6, of which 2 were waited for; matrix products, arithmetic and copies ran while one was open for 0% of the time, Pallas kernels for 10%

profile of v6, /device:TPU:0, one launch (start us, length us, event | category | flops | bytes accessed | tf_op | source)
XLA Modules:
  0.0 135.2 jit_solution(12407317467883975752)
XLA Ops:
  0.6 0.0 copy-start.3
  0.6 17.7 %project.1 = (bf16[256,16,128]{2,1,0:T(8,128)(2,1)}, bf16[256,16,128]{2,1,0:T(8,128)(2,1)}, bf16[256,16,128]{2,1,0:T(8,128)(2,1)}) custom-call(s32[256]{0:T(256)} %pos_ref.7, bf16[256,4608]{1,0:T(8,128)(2,1)} %refs_12_.1, f32[36,128]{1,0:T(8,128)} %bitcast.14, f32[256,256]{1,0:T(8,128)} %constant.8.clone.table_ref, bf16[4608,2048]{1,0:T(8,128)(2,1)} %wq_hbm.1, ...), custom_call_target="tpu_custom_call" | custom-call | flops 4831838208 | bytes 18874368 | tf_op jit(solution)/shard_map/project/pallas_call | solution.py:135
  18.3 0.0 copy-done.3
  18.4 0.0 copy-start
  18.4 1.2 copy-done
  19.6 0.0 copy-start.1
  19.6 1.2 copy-done.1
  20.8 0.0 copy-start.2
  20.8 1.2 copy-done.2
  22.0 24.5 %attend.3 = (bf16[256,512,128]{2,1,0:T(8,128)(2,1)}, bf16[256,512,128]{2,1,0:T(8,128)(2,1)}, f32[544,128]{1,0:T(8,128)}, f32[544,128]{1,0:T(8,128)}, f32[544,128]{1,0:T(8,128)}, /*index=5*/f32[544,128]{1,0:T(8,128)}) custom-call(s32[256]{0:T(256)S(1)} %copy-done.3, s32[1]{0:T(128)} %bitcast.base_ref, bf16[256,16,128]{2,1,0:T(8,128)(2,1)S(1)} %copy-done, ...), custom_call_target="tpu_custom_call" | custom-call | flops 536870912 | bytes 67108864 | tf_op jit(solution)/shard_map/attend/pallas_call | solution.py:305
  46.5 0.0 copy-start.13
  46.5 0.0 copy-start.12
  46.5 0.0 copy-start.11
  46.5 0.0 copy-start.10
  46.5 13.6 %attend.4 = (bf16[256,512,128]{2,1,0:T(8,128)(2,1)}, bf16[256,512,128]{2,1,0:T(8,128)(2,1)}, f32[288,128]{1,0:T(8,128)}, f32[288,128]{1,0:T(8,128)}, f32[288,128]{1,0:T(8,128)}, /*index=5*/f32[288,128]{1,0:T(8,128)}) custom-call(s32[256]{0:T(256)S(1)} %copy-done.3, s32[1]{0:T(128)} %bitcast.base_ref, ...), custom_call_target="tpu_custom_call", output_to_operand_aliasing={{0}: (7, {}), {1}: (8, {})} | custom-call | flops 268435456 | bytes 33554432 | tf_op jit(solution)/shard_map/attend/pallas_call | solution.py:305
  60.2 0.2 collective-permute-start.3
  60.3 0.0 copy-done.13
  60.3 0.4 collective-permute-start
  60.7 0.0 copy-done.12
  60.7 2.6 %collective-permute-start.1 = (f32[544,128]{1,0:T(8,128)S(1)}, f32[544,128]{1,0:T(8,128)S(1)}, u32[]{:S(2)}, u32[]{:S(2)}) collective-permute-start(f32[544,128]{1,0:T(8,128)S(1)} %copy-done.12), channel_id=1, source_target_pairs={{0,2},{1,3},{2,0},{3,1},{4,6},{5,7},{6,4},{7,5}} | collective-permute-start | bytes 835592 | tf_op jit(solution)/shard_map/ppermute | solution.py:566
  63.3 0.0 copy-done.11
  63.3 0.0 collective-permute-start.2
  63.3 1.7 %collective-permute-start.4 = (f32[288,128]{1,0:T(8,128)}, f32[288,128]{1,0:T(8,128)S(1)}, u32[]{:S(2)}, u32[]{:S(2)}) collective-permute-start(f32[288,128]{1,0:T(8,128)} %get-tuple-element.35), channel_id=1, source_target_pairs={{0,2},{1,3},{2,0},{3,1},{4,6},{5,7},{6,4},{7,5}} | collective-permute-start | bytes 442376 | tf_op jit(solution)/shard_map/ppermute | solution.py:566
  65.1 0.0 collective-permute-done.3.refs_5_
  65.1 0.0 copy-start.7
  65.1 0.1 collective-permute-start.5
  65.1 0.0 copy-done.10
  65.1 0.6 reshape.31.refs_13_
  65.7 13.6 %attend.5 = (bf16[256,512,128]{2,1,0:T(8,128)(2,1)}, bf16[256,512,128]{2,1,0:T(8,128)(2,1)}, f32[288,128]{1,0:T(8,128)}, f32[288,128]{1,0:T(8,128)}, f32[288,128]{1,0:T(8,128)}, /*index=5*/f32[288,128]{1,0:T(8,128)}) custom-call(s32[256]{0:T(256)S(1)} %copy-done.3, s32[1]{0:T(128)} %bitcast.base_ref, ...), custom_call_target="tpu_custom_call", output_to_operand_aliasing={{0}: (7, {}), {1}: (8, {})} | custom-call | flops 268435456 | bytes 33554432 | tf_op jit(solution)/shard_map/attend/pallas_call | solution.py:305
  79.4 0.0 copy-done.7
  79.4 0.6 collective-permute-done.4.refs_6_
  80.0 0.0 copy-start.8
  80.0 2.5 %collective-permute-done.5.refs_7_ = f32[288,128]{1,0:T(8,128)S(1)} collective-permute-done((f32[288,128]{1,0:T(8,128)}, f32[288,128]{1,0:T(8,128)S(1)}, u32[]{:S(2)}, u32[]{:S(2)}) %collective-permute-start.5) | collective-permute-done | bytes 147488 | tf_op jit(solution)/shard_map/ppermute | solution.py:566
  82.5 0.0 copy-start.9
  82.5 0.0 collective-permute-done.refs_1_
  82.5 0.0 copy-start.4
  82.5 0.0 collective-permute-done.1.refs_2_
  82.5 0.0 copy-start.5
  82.5 0.0 collective-permute-done.2.refs_3_
  82.5 0.0 copy-start.6
  82.5 0.0 copy-done.8
  82.5 0.6 copy-done.9
  83.2 0.1 copy-done.4
  83.3 0.1 copy-done.5
  83.4 0.1 copy-done.6
  83.5 48.5 %merge.1 = bf16[256,4608]{1,0:T(8,128)(2,1)} custom-call(f32[544,128]{1,0:T(8,128)} %get-tuple-element.27.refs_0_, f32[544,128]{1,0:T(8,128)} %copy-done.4, f32[544,128]{1,0:T(8,128)} %copy-done.5, f32[544,128]{1,0:T(8,128)} %copy-done.6, f32[288,128]{1,0:T(8,128)} %get-tuple-element.33.refs_4_, f32[288,128]{1,0:T(8,128)} %copy-done.7, ...), custom_call_target="tpu_custom_call" | custom-call | flops 1207959552 | bytes 18874368 | tf_op jit(solution)/shard_map/merge/pallas_call | solution.py:523
  132.0 3.2 %copy.23 = bf16[256,4608]{1,0:T(8,128)(2,1)} copy(bf16[256,4608]{1,0:T(8,128)(2,1)} %merge.1) | data formatting | bytes 4718592
Async XLA Ops:
  0.6 17.7 %copy-start.3 = (s32[256]{0:T(256)S(1)}, s32[256]{0:T(256)}, u32[]{:S(2)}) copy-start(s32[256]{0:T(256)} %pos_ref.7) | copy-start | bytes 3076
  18.4 1.2 copy-start
  19.6 1.2 copy-start.1
  20.8 1.2 copy-start.2
  46.5 13.8 %copy-start.13 = (f32[544,128]{1,0:T(8,128)S(1)}, f32[544,128]{1,0:T(8,128)}, u32[]{:S(2)}) copy-start(f32[544,128]{1,0:T(8,128)} %get-tuple-element.28) | copy-start | bytes 835588
  46.5 14.2 %copy-start.12 = (f32[544,128]{1,0:T(8,128)S(1)}, f32[544,128]{1,0:T(8,128)}, u32[]{:S(2)}) copy-start(f32[544,128]{1,0:T(8,128)} %get-tuple-element.29) | copy-start | bytes 835588
  46.5 16.8 %copy-start.11 = (f32[544,128]{1,0:T(8,128)S(1)}, f32[544,128]{1,0:T(8,128)}, u32[]{:S(2)}) copy-start(f32[544,128]{1,0:T(8,128)} %get-tuple-element.30) | copy-start | bytes 835588
  46.5 18.6 %copy-start.10 = (f32[4608]{0:T(1024)S(1)}, f32[4608]{0:T(1024)}, u32[]{:S(2)}) copy-start(f32[4608]{0:T(1024)} %param.18) | copy-start | bytes 55300
  60.2 4.9 %collective-permute-start.3 = (f32[288,128]{1,0:T(8,128)}, f32[288,128]{1,0:T(8,128)S(1)}, u32[]{:S(2)}, u32[]{:S(2)}) collective-permute-start(f32[288,128]{1,0:T(8,128)} %get-tuple-element.34), channel_id=1, source_target_pairs={{0,1},{1,0},{2,3},{3,2},{4,5},{5,4},{6,7},{7,6}} | collective-permute-start | bytes 442376 | tf_op jit(solution)/shard_map/ppermute | solution.py:566
  60.3 22.2 %collective-permute-start = (f32[544,128]{1,0:T(8,128)S(1)}, f32[544,128]{1,0:T(8,128)S(1)}, u32[]{:S(2)}, u32[]{:S(2)}) collective-permute-start(f32[544,128]{1,0:T(8,128)S(1)} %copy-done.13), channel_id=1, source_target_pairs={{0,1},{1,0},{2,3},{3,2},{4,5},{5,4},{6,7},{7,6}} | collective-permute-start | bytes 835592 | tf_op jit(solution)/shard_map/ppermute | solution.py:566
  60.7 21.8 %collective-permute-start.1 = (f32[544,128]{1,0:T(8,128)S(1)}, f32[544,128]{1,0:T(8,128)S(1)}, u32[]{:S(2)}, u32[]{:S(2)}) collective-permute-start(f32[544,128]{1,0:T(8,128)S(1)} %copy-done.12), channel_id=1, source_target_pairs={{0,2},{1,3},{2,0},{3,1},{4,6},{5,7},{6,4},{7,5}} | collective-permute-start | bytes 835592 | tf_op jit(solution)/shard_map/ppermute | solution.py:566
  63.3 19.2 %collective-permute-start.2 = (f32[544,128]{1,0:T(8,128)S(1)}, f32[544,128]{1,0:T(8,128)S(1)}, u32[]{:S(2)}, u32[]{:S(2)}) collective-permute-start(f32[544,128]{1,0:T(8,128)S(1)} %copy-done.11), channel_id=1, source_target_pairs={{0,3},{1,2},{2,1},{3,0},{4,7},{5,6},{6,5},{7,4}} | collective-permute-start | bytes 835592 | tf_op jit(solution)/shard_map/ppermute | solution.py:566
  63.3 16.6 %collective-permute-start.4 = (f32[288,128]{1,0:T(8,128)}, f32[288,128]{1,0:T(8,128)S(1)}, u32[]{:S(2)}, u32[]{:S(2)}) collective-permute-start(f32[288,128]{1,0:T(8,128)} %get-tuple-element.35), channel_id=1, source_target_pairs={{0,2},{1,3},{2,0},{3,1},{4,6},{5,7},{6,4},{7,5}} | collective-permute-start | bytes 442376 | tf_op jit(solution)/shard_map/ppermute | solution.py:566
  65.1 14.3 %copy-start.7 = (f32[288,128]{1,0:T(8,128)}, f32[288,128]{1,0:T(8,128)S(1)}, u32[]{:S(2)}) copy-start(f32[288,128]{1,0:T(8,128)S(1)} %collective-permute-done.3.refs_5_) | copy-start | bytes 442372
  65.1 17.4 %collective-permute-start.5 = (f32[288,128]{1,0:T(8,128)}, f32[288,128]{1,0:T(8,128)S(1)}, u32[]{:S(2)}, u32[]{:S(2)}) collective-permute-start(f32[288,128]{1,0:T(8,128)} %get-tuple-element.36), channel_id=1, source_target_pairs={{0,3},{1,2},{2,1},{3,0},{4,7},{5,6},{6,5},{7,4}} | collective-permute-start | bytes 442376 | tf_op jit(solution)/shard_map/ppermute | solution.py:566
  80.0 2.6 %copy-start.8 = (f32[288,128]{1,0:T(8,128)}, f32[288,128]{1,0:T(8,128)S(1)}, u32[]{:S(2)}) copy-start(f32[288,128]{1,0:T(8,128)S(1)} %collective-permute-done.4.refs_6_) | copy-start | bytes 442372
  82.5 0.7 copy-start.9
  82.5 0.8 copy-start.4
  82.5 0.9 copy-start.5
  82.5 0.9 copy-start.6

commit v7 on v6

--- a/solution.py
+++ b/solution.py
@@ -31,7 +31,8 @@
 
 
 def project_kernel(pos_ref, x_hbm, wpre_ref, table_ref, wq_hbm, wk_hbm, wv_hbm, q_ref, k_ref, v_ref,
-                   x_ref, gain_ref, cos_ref, sin_ref, weight, normed, q_part, k_part, v_part, x_sem, w_sem, send_sem, recv_sem):
+                   x_ref, gain_ref, cos_ref, sin_ref, weight, normed, q_part, k_part, v_part, x_sem, w_sem, send_sem, recv_sem,
+                   out_sem):
     sp = lax.axis_index('sp')
     core = lax.rem(sp, 2)
     peer = {'sp': sp + 1 - 2 * core}
@@ -85,7 +86,8 @@
         x_loads[k].wait()
         lax.fori_loop(k * rows // 64, (k + 1) * rows // 64, norm, 0)
 
-    sends = []
+    outs = ((q_part, q_ref), (k_part, k_ref), (v_part, v_ref))
+    sends, writes = [], []
     for i, (_, part, turn, mine, j, done) in enumerate(plan):
         load(i).wait()
         heads = mine // 128
@@ -101,26 +103,18 @@
                                                 recv_sem=recv_sem.at[n], device_id=peer, device_id_type=mesh_id)
             copy.start()
             sends.append(copy)
+            out = pltpu.make_async_copy(part.at[core], outs[n][1].at[core], out_sem.at[0, n])
+            out.start()
+            writes.append(out)
+    for n, copy in enumerate(sends):
+        copy.wait_recv()
+        out = pltpu.make_async_copy(outs[n][0].at[1 - core], outs[n][1].at[1 - core], out_sem.at[1, n])
+        out.start()
+        writes.append(out)
     for copy in sends:
+        copy.wait_send()
+    for copy in writes:
         copy.wait()
-
-    q_heads = q_part.shape[1] // rows
-    kv = k_part.shape[1] // rows
-
-    def pack(k, carry):
-        for r in range(8):
-            b = k * 8 + r
-            at = pl.ds(pl.multiple_of(b * q_heads, q_heads), q_heads)
-            q_ref[b] = jnp.concatenate([q_part[0, at, :], q_part[1, at, :]], axis=0).astype(jnp.bfloat16)
-        for part, out in ((k_part, k_ref), (v_part, v_ref)):
-            group = pl.ds(pl.multiple_of(k * 8 * kv, 8), 8 * kv)
-            low, high = part[0, group, :], part[1, group, :]
-            for r in range(8):
-                both = [low[r * kv:(r + 1) * kv], high[r * kv:(r + 1) * kv]]
-                out[k * 8 + r] = jnp.concatenate(both + both, axis=0).astype(jnp.bfloat16)
-        return carry
-
-    lax.fori_loop(0, rows // 8, pack, 0)
 
 
 def project(cur_pos, x_in, w_pre, table, w_q, w_k, w_v):
@@ -134,11 +128,10 @@
     dma = pltpu.SemaphoreType.DMA
     return pl.pallas_call(
         project_kernel,
-        out_shape=(jax.ShapeDtypeStruct((rows, q_cols // 128, 128), bf),
-                   jax.ShapeDtypeStruct((rows, kv_cols // 64, 128), bf),
-                   jax.ShapeDtypeStruct((rows, kv_cols // 64, 128), bf)),
+        out_shape=(pltpu.HBM((2, rows * q_cols // 256, 128), f32), pltpu.HBM((2, rows * kv_cols // 256, 128), f32),
+                   pltpu.HBM((2, rows * kv_cols // 256, 128), f32)),
         in_specs=[pl.BlockSpec(memory_space=pltpu.SMEM), hbm, vmem, vmem] + [hbm] * 3,
-        out_specs=(vmem,) * 3,
+        out_specs=(hbm,) * 3,
         scratch_shapes=[
             pltpu.VMEM((rows, width), bf),
             pltpu.VMEM((1, width), f32),
@@ -149,7 +142,7 @@
             pltpu.VMEM((2, rows * q_cols // 256, 128), f32),
             pltpu.VMEM((2, rows * kv_cols // 256, 128), f32),
             pltpu.VMEM((2, rows * kv_cols // 256, 128), f32),
-            dma((4,)), dma((n_blocks,)), dma((3,)), dma((3,)),
+            dma((4,)), dma((n_blocks,)), dma((3,)), dma((3,)), dma((2, 3)),
         ],
         compiler_params=pltpu.CompilerParams(vmem_limit_bytes=62 * 1024 * 1024, collective_id=1, has_side_effects=True),
         cost_estimate=pl.CostEstimate(flops=rows * width * (q_cols + 2 * kv_cols), bytes_accessed=width * (q_cols + 2 * kv_cols), transcendentals=0),
@@ -162,7 +155,8 @@
     (ko_hbm, vo_hbm, o0_hbm, o1_hbm, o2_hbm, o3_hbm, m_ref, l_ref, kbuf, vbuf, qbuf, knbuf, vnbuf, obuf, key_ref, s_ref, p_ref, in_sem, out_sem, o_sem, st_sem) = rest[-21:]
     step_rows = ROWS_STEP
     piece_steps = n_steps // 4
-    heads, head_dim = qbuf.shape[2], qbuf.shape[3]
+    heads, head_dim = m_ref.shape
+    q_half, kv_half = heads // 2, kv_heads // 2
     cols = seq_block * kv_heads
     base = base_ref[0]
 
@@ -173,13 +167,20 @@
     lane_id = lax.broadcasted_iota(jnp.int32, m_ref.shape, 1)
     half_id = lax.broadcasted_iota(jnp.int32, (2 * kv_heads, head_dim), 0) // kv_heads
 
+    def heads_of(step, count):
+        return pl.ds((first_row + step * step_rows) * count, step_rows * count)
+
+    def both_halves(ref, slot, r, count):
+        at = slice(r * count, (r + 1) * count)
+        return [ref[slot, 0, at, :], ref[slot, 1, at, :]]
+
     def loads(step, slot):
         rows = pl.ds(first_row + step * step_rows, step_rows)
         return (pltpu.make_async_copy(k_hbm.at[rows], kbuf.at[slot], in_sem.at[slot, 0]),
                 pltpu.make_async_copy(v_hbm.at[rows], vbuf.at[slot], in_sem.at[slot, 1]),
-                pltpu.make_async_copy(q_hbm.at[rows], qbuf.at[slot], in_sem.at[slot, 2]),
-                pltpu.make_async_copy(kn_hbm.at[rows], knbuf.at[slot], in_sem.at[slot, 3]),
-                pltpu.make_async_copy(vn_hbm.at[rows], vnbuf.at[slot], in_sem.at[slot, 4]))
+                pltpu.make_async_copy(q_hbm.at[:, heads_of(step, q_half)], qbuf.at[slot], in_sem.at[slot, 2]),
+                pltpu.make_async_copy(kn_hbm.at[:, heads_of(step, kv_half)], knbuf.at[slot], in_sem.at[slot, 3]),
+                pltpu.make_async_copy(vn_hbm.at[:, heads_of(step, kv_half)], vnbuf.at[slot], in_sem.at[slot, 4]))
 
     def stores(step, slot):
         rows = pl.ds(first_row + step * step_rows, step_rows)
@@ -217,8 +218,10 @@
             at = jnp.clip(local, 0, seq_block - 1)
             pair = pl.ds(pl.multiple_of((at // 2) * (2 * kv_heads), 2 * kv_heads), 2 * kv_heads)
             hit = half_id == jnp.where(inside, lax.rem(at, 2), 2)
-            kbuf[slot, r, pair, :] = jnp.where(hit, knbuf[slot, r], kbuf[slot, r, pair, :])
-            vbuf[slot, r, pair, :] = jnp.where(hit, vnbuf[slot, r], vbuf[slot, r, pair, :])
+            k_row = jnp.concatenate(both_halves(knbuf, slot, r, kv_half) * 2, axis=0).astype(jnp.bfloat16)
+            v_row = jnp.concatenate(both_halves(vnbuf, slot, r, kv_half) * 2, axis=0).astype(jnp.bfloat16)
+            kbuf[slot, r, pair, :] = jnp.where(hit, k_row, kbuf[slot, r, pair, :])
+            vbuf[slot, r, pair, :] = jnp.where(hit, v_row, vbuf[slot, r, pair, :])
 
         @pl.when(step >= 2)
         def _():
@@ -230,7 +233,8 @@
         for tick in range(step_rows + LAG_OUT):
             r = tick
             if r < step_rows:
-                raw = lax.dot_general(qbuf[slot, r], kbuf[slot, r], (((1,), (1,)), ((), ())),
+                q_row = jnp.concatenate(both_halves(qbuf, slot, r, q_half), axis=0).astype(jnp.bfloat16)
+                raw = lax.dot_general(q_row, kbuf[slot, r], (((1,), (1,)), ((), ())),
                                       preferred_element_type=jnp.float32)
                 s_ref[r] = raw
             r = tick - LAG_SOFT
@@ -291,9 +295,9 @@
 
 
 def attend(pos, base, q, kn, vn, k_cache, v_cache, prev, first_row, n_rows):
-    _, cols, head_dim = k_cache.shape
-    heads = q.shape[1]
-    kv_heads = kn.shape[1] // 2
+    rows, cols, head_dim = k_cache.shape
+    heads = 2 * q.shape[1] // rows
+    kv_heads = 2 * kn.shape[1] // rows
     seq_block = cols // kv_heads
     n_steps = n_rows // ROWS_STEP
     hbm = pl.BlockSpec(memory_space=pl.ANY)
@@ -312,9 +316,9 @@
             pltpu.VMEM((heads, 128), jnp.float32),
             pltpu.VMEM((SLOTS, ROWS_STEP, cols, head_dim), bf),
             pltpu.VMEM((SLOTS, ROWS_STEP, cols, head_dim), bf),
-            pltpu.VMEM((SLOTS, ROWS_STEP, heads, head_dim), bf),
-            pltpu.VMEM((SLOTS, ROWS_STEP, 2 * kv_heads, head_dim), bf),
-            pltpu.VMEM((SLOTS, ROWS_STEP, 2 * kv_heads, head_dim), bf),
+            pltpu.VMEM((SLOTS, 2, ROWS_STEP * heads // 2, head_dim), jnp.float32),
+            pltpu.VMEM((SLOTS, 2, ROWS_STEP * kv_heads // 2, head_dim), jnp.float32),
+            pltpu.VMEM((SLOTS, 2, ROWS_STEP * kv_heads // 2, head_dim), jnp.float32),
             pltpu.VMEM((2, ROWS_STEP * heads, head_dim), jnp.float32),
             pltpu.VMEM((heads, cols), jnp.int32),
             pltpu.VMEM((ROWS_STEP, heads, cols), jnp.float32),
@@ -325,7 +329,7 @@
             pltpu.SemaphoreType.DMA((4, 2)),
         ],
         input_output_aliases=aliases,
-        compiler_params=pltpu.CompilerParams(vmem_limit_bytes=40 * 1024 * 1024),
+        compiler_params=pltpu.CompilerParams(vmem_limit_bytes=62 * 1024 * 1024),
         cost_estimate=pl.CostEstimate(flops=n_rows * heads * cols * head_dim * 4,
                                       bytes_accessed=n_rows * cols * head_dim * 8, transcendentals=0),
         name='attend',
@@ -413,7 +417,6 @@
             order.append((begin, size, first_at))
             begin += size
         orders.append(order + [(n, wide, last_at) for n in range(0, n_chunks, wide)])
-    n_first = len(split[0])
     n_pieces = len(orders[0])
 
     def to_y(v, t):
@@ -444,7 +447,7 @@
         w_load(n).wait()
         project_rows(n, 0, first)
         for v in range(2):
-            for t in range(n_first):
+            for t in range(2):
                 if sum(orders[v][t][:2]) == n + 1:
                     @pl.when(core == v)
                     def _():
@@ -455,6 +458,8 @@
             n, size, r = orders[v][t]
             ns = pl.ds(n, size)
             to_y(v, t).wait()
+            if t + 2 < n_pieces:
+                to_y(v, t + 2).start()
             sums[sp, ns, r, :] = y_out[ns, r, :] + y_in[ns, r, :]
             to_x(v, t).start()
             to_core(v, t).start()
@@ -470,7 +475,6 @@
         if 1 <= t < 1 + n_chunks // wide:
             for n in range((t - 1) * wide, t * wide):
                 project_rows(n, first, quarter - first)
-            to_y(0, n_first + t - 1).start()
         for v in range(2):
             @pl.when(core == v)
             def _():
@@ -540,7 +544,7 @@
         compiler_params=pltpu.CompilerParams(vmem_limit_bytes=56 * 1024 * 1024, collective_id=0, has_side_effects=True),
         cost_estimate=pl.CostEstimate(flops=2 * quarter * inner * width, bytes_accessed=2 * inner * width, transcendentals=0),
         name='merge',
-    )(*flat, x_in, w_post, w_o)
+    )(*flat, x_in, w_post, pltpu.with_memory_space_constraint(w_o, pltpu.HBM))
 
 
 def solution(mesh):

time: 135 us -> 132 us (0.978)
  local copies, waits for them, and re-layouts: 8.46 us -> 4.8 us
    unnamed x29 -> x19, local copies, waits for them, and re-layouts: 7.84 us -> 4.15 us
    pallas_call x3, Pallas kernels: 51.7 us -> 53.1 us  [attend(): pl.pallas_call(functools.partial(attend_kernel, n_steps, first_row, kv_he...]
  transfers between devices with their start and end apart: 6 -> 6, of which waited for: 2 -> 2; matrix products, arithmetic and copies ran while one was open for 0% -> 0% of each run, Pallas kernels for 10% -> 11%
where the time goes in v7:
time: 132 us; the launch traced here: 131 us
  Pallas kernels  118 us (89%)
  starting transfers between devices  4.89 us (4%)
  local copies, waits for them, and re-layouts  4.8 us (4%)
  waiting for transfers between devices  2.99 us (2%)
    pallas_call x3, Pallas kernels, attend(): pl.pallas_call(functools.partial(attend_kernel, n_steps, first_row, kv_he...  53.1 us
    pallas_call x1, Pallas kernels, merge(): pl.pallas_call(functools.partial(merge_kernel, chunks), out_shape=jax.Sha...  48.4 us
    pallas_call x1, Pallas kernels, project(): pl.pallas_call(project_kernel, out_shape=(pltpu.HBM((2, rows * q_cols //...  16.5 us
    ppermute x6, starting transfers between devices, local_step(): moved.append(lax.ppermute(p, 'sp', [(i, i ^ d) for i in range(sp_size)]))  4.89 us
    unnamed x19, local copies, waits for them, and re-layouts  4.15 us
    ppermute x6, waiting for transfers between devices, local_step(): moved.append(lax.ppermute(p, 'sp', [(i, i ^ d) for i in range(sp_size)]))  2.99 us
  transfers between devices with their start and end apart: 6, of which 2 were waited for; matrix products, arithmetic and copies ran while one was open for 0% of the time, Pallas kernels for 11%

profile of v7, /device:TPU:0, one launch (start us, length us, event | category | flops | bytes accessed | tf_op | source)
XLA Modules:
  0.0 131.4 jit_solution(10643775374162417961)
XLA Ops:
  0.6 16.5 %project.1 = (f32[2,2048,128]{2,1,0:T(8,128)}, f32[2,1024,128]{2,1,0:T(8,128)}, f32[2,1024,128]{2,1,0:T(8,128)}) custom-call(s32[256]{0:T(256)} %pos_ref.7, bf16[256,4608]{1,0:T(8,128)(2,1)} %refs_12_.1, f32[36,128]{1,0:T(8,128)} %bitcast.14, f32[256,256]{1,0:T(8,128)} %constant.8.clone.table_ref, bf16[4608,2048]{1,0:T(8,128)(2,1)} %wq_hbm.1, ...), custom_call_target="tpu_custom_call" | custom-call | flops 4831838208 | bytes 18874368 | tf_op jit(solution)/shard_map/project/pallas_call | solution.py:129
  17.1 25.2 %attend.3 = (bf16[256,512,128]{2,1,0:T(8,128)(2,1)}, bf16[256,512,128]{2,1,0:T(8,128)(2,1)}, f32[544,128]{1,0:T(8,128)}, f32[544,128]{1,0:T(8,128)}, f32[544,128]{1,0:T(8,128)}, /*index=5*/f32[544,128]{1,0:T(8,128)}) custom-call(s32[256]{0:T(256)} %pos_ref.7, s32[1]{0:T(128)} %bitcast.base_ref, f32[2,2048,128]{2,1,0:T(8,128)} %get-tuple-element.24.q_hbm, ...), custom_call_target="tpu_custom_call" | custom-call | flops 536870912 | bytes 67108864 | tf_op jit(solution)/shard_map/attend/pallas_call | solution.py:309
  42.3 0.0 copy-start.8
  42.3 0.0 copy-start.7
  42.3 0.0 copy-start.6
  42.3 14.0 %attend.4 = (bf16[256,512,128]{2,1,0:T(8,128)(2,1)}, bf16[256,512,128]{2,1,0:T(8,128)(2,1)}, f32[288,128]{1,0:T(8,128)}, f32[288,128]{1,0:T(8,128)}, f32[288,128]{1,0:T(8,128)}, /*index=5*/f32[288,128]{1,0:T(8,128)}) custom-call(s32[256]{0:T(256)} %pos_ref.7, s32[1]{0:T(128)} %bitcast.base_ref, ...), custom_call_target="tpu_custom_call", output_to_operand_aliasing={{0}: (7, {}), {1}: (8, {})} | custom-call | flops 268435456 | bytes 33554432 | tf_op jit(solution)/shard_map/attend/pallas_call | solution.py:309
  56.3 0.0 collective-permute-start.3
  56.4 0.5 collective-permute-start
  56.9 0.0 copy-done.8
  56.9 2.5 %collective-permute-start.1 = (f32[544,128]{1,0:T(8,128)S(1)}, f32[544,128]{1,0:T(8,128)S(1)}, u32[]{:S(2)}, u32[]{:S(2)}) collective-permute-start(f32[544,128]{1,0:T(8,128)S(1)} %copy-done.8), channel_id=1, source_target_pairs={{0,2},{1,3},{2,0},{3,1},{4,6},{5,7},{6,4},{7,5}} | collective-permute-start | bytes 835592 | tf_op jit(solution)/shard_map/ppermute | solution.py:570
  59.4 0.0 copy-done.7
  59.4 0.1 collective-permute-start.2
  59.5 1.7 %collective-permute-start.4 = (f32[288,128]{1,0:T(8,128)}, f32[288,128]{1,0:T(8,128)S(1)}, u32[]{:S(2)}, u32[]{:S(2)}) collective-permute-start(f32[288,128]{1,0:T(8,128)} %get-tuple-element.35), channel_id=1, source_target_pairs={{0,2},{1,3},{2,0},{3,1},{4,6},{5,7},{6,4},{7,5}} | collective-permute-start | bytes 442376 | tf_op jit(solution)/shard_map/ppermute | solution.py:570
  61.2 0.0 collective-permute-done.3.refs_5_
  61.2 0.0 copy-start.3
  61.2 0.0 collective-permute-start.5
  61.3 0.0 copy-done.6
  61.3 0.6 reshape.31.refs_13_
  61.9 13.9 %attend.5 = (bf16[256,512,128]{2,1,0:T(8,128)(2,1)}, bf16[256,512,128]{2,1,0:T(8,128)(2,1)}, f32[288,128]{1,0:T(8,128)}, f32[288,128]{1,0:T(8,128)}, f32[288,128]{1,0:T(8,128)}, /*index=5*/f32[288,128]{1,0:T(8,128)}) custom-call(s32[256]{0:T(256)} %pos_ref.7, s32[1]{0:T(128)} %bitcast.base_ref, ...), custom_call_target="tpu_custom_call", output_to_operand_aliasing={{0}: (7, {}), {1}: (8, {})} | custom-call | flops 268435456 | bytes 33554432 | tf_op jit(solution)/shard_map/attend/pallas_call | solution.py:309
  75.8 0.0 copy-done.3
  75.8 0.2 collective-permute-done.4.refs_6_
  76.0 0.0 copy-start.4
  76.0 2.7 %collective-permute-done.5.refs_7_ = f32[288,128]{1,0:T(8,128)S(1)} collective-permute-done((f32[288,128]{1,0:T(8,128)}, f32[288,128]{1,0:T(8,128)S(1)}, u32[]{:S(2)}, u32[]{:S(2)}) %collective-permute-start.5) | collective-permute-done | bytes 147488 | tf_op jit(solution)/shard_map/ppermute | solution.py:570
  78.8 0.0 copy-start.5
  78.8 0.0 collective-permute-done.refs_1_
  78.8 0.0 copy-start
  78.8 0.0 collective-permute-done.1.refs_2_
  78.8 0.0 copy-start.1
  78.8 0.0 collective-permute-done.2.refs_3_
  78.8 0.0 copy-start.2
  78.8 0.0 copy-done.4
  78.8 0.6 copy-done.5
  79.4 0.1 copy-done
  79.6 0.1 copy-done.1
  79.7 0.1 copy-done.2
  79.7 48.4 %merge.1 = bf16[256,4608]{1,0:T(8,128)(2,1)} custom-call(f32[544,128]{1,0:T(8,128)} %get-tuple-element.27.refs_0_, f32[544,128]{1,0:T(8,128)} %copy-done, f32[544,128]{1,0:T(8,128)} %copy-done.1, f32[544,128]{1,0:T(8,128)} %copy-done.2, f32[288,128]{1,0:T(8,128)} %get-tuple-element.33.refs_4_, f32[288,128]{1,0:T(8,128)} %copy-done.3, f32[288,128]{1,0:T(8,128)} %copy-done.4, ...), custom_call_target="tpu_custom_call" | custom-call | flops 1207959552 | bytes 18874368 | tf_op jit(solution)/shard_map/merge/pallas_call | solution.py:527
  128.1 3.2 %copy.23 = bf16[256,4608]{1,0:T(8,128)(2,1)} copy(bf16[256,4608]{1,0:T(8,128)(2,1)} %merge.1) | data formatting | bytes 4718592
Async XLA Ops:
  42.3 14.6 %copy-start.8 = (f32[544,128]{1,0:T(8,128)S(1)}, f32[544,128]{1,0:T(8,128)}, u32[]{:S(2)}) copy-start(f32[544,128]{1,0:T(8,128)} %get-tuple-element.29) | copy-start | bytes 835588
  42.3 17.1 %copy-start.7 = (f32[544,128]{1,0:T(8,128)S(1)}, f32[544,128]{1,0:T(8,128)}, u32[]{:S(2)}) copy-start(f32[544,128]{1,0:T(8,128)} %get-tuple-element.30) | copy-start | bytes 835588
  42.3 18.9 %copy-start.6 = (f32[4608]{0:T(1024)S(1)}, f32[4608]{0:T(1024)}, u32[]{:S(2)}) copy-start(f32[4608]{0:T(1024)} %param.18) | copy-start | bytes 55300
  56.3 4.9 %collective-permute-start.3 = (f32[288,128]{1,0:T(8,128)}, f32[288,128]{1,0:T(8,128)S(1)}, u32[]{:S(2)}, u32[]{:S(2)}) collective-permute-start(f32[288,128]{1,0:T(8,128)} %get-tuple-element.34), channel_id=1, source_target_pairs={{0,1},{1,0},{2,3},{3,2},{4,5},{5,4},{6,7},{7,6}} | collective-permute-start | bytes 442376 | tf_op jit(solution)/shard_map/ppermute | solution.py:570
  56.4 22.4 %collective-permute-start = (f32[544,128]{1,0:T(8,128)}, f32[544,128]{1,0:T(8,128)S(1)}, u32[]{:S(2)}, u32[]{:S(2)}) collective-permute-start(f32[544,128]{1,0:T(8,128)} %get-tuple-element.28), channel_id=1, source_target_pairs={{0,1},{1,0},{2,3},{3,2},{4,5},{5,4},{6,7},{7,6}} | collective-permute-start | bytes 835592 | tf_op jit(solution)/shard_map/ppermute | solution.py:570
  56.9 21.9 %collective-permute-start.1 = (f32[544,128]{1,0:T(8,128)S(1)}, f32[544,128]{1,0:T(8,128)S(1)}, u32[]{:S(2)}, u32[]{:S(2)}) collective-permute-start(f32[544,128]{1,0:T(8,128)S(1)} %copy-done.8), channel_id=1, source_target_pairs={{0,2},{1,3},{2,0},{3,1},{4,6},{5,7},{6,4},{7,5}} | collective-permute-start | bytes 835592 | tf_op jit(solution)/shard_map/ppermute | solution.py:570
  59.4 19.4 %collective-permute-start.2 = (f32[544,128]{1,0:T(8,128)S(1)}, f32[544,128]{1,0:T(8,128)S(1)}, u32[]{:S(2)}, u32[]{:S(2)}) collective-permute-start(f32[544,128]{1,0:T(8,128)S(1)} %copy-done.7), channel_id=1, source_target_pairs={{0,3},{1,2},{2,1},{3,0},{4,7},{5,6},{6,5},{7,4}} | collective-permute-start | bytes 835592 | tf_op jit(solution)/shard_map/ppermute | solution.py:570
  59.5 16.5 %collective-permute-start.4 = (f32[288,128]{1,0:T(8,128)}, f32[288,128]{1,0:T(8,128)S(1)}, u32[]{:S(2)}, u32[]{:S(2)}) collective-permute-start(f32[288,128]{1,0:T(8,128)} %get-tuple-element.35), channel_id=1, source_target_pairs={{0,2},{1,3},{2,0},{3,1},{4,6},{5,7},{6,4},{7,5}} | collective-permute-start | bytes 442376 | tf_op jit(solution)/shard_map/ppermute | solution.py:570
  61.2 14.5 %copy-start.3 = (f32[288,128]{1,0:T(8,128)}, f32[288,128]{1,0:T(8,128)S(1)}, u32[]{:S(2)}) copy-start(f32[288,128]{1,0:T(8,128)S(1)} %collective-permute-done.3.refs_5_) | copy-start | bytes 442372
  61.2 17.5 %collective-permute-start.5 = (f32[288,128]{1,0:T(8,128)}, f32[288,128]{1,0:T(8,128)S(1)}, u32[]{:S(2)}, u32[]{:S(2)}) collective-permute-start(f32[288,128]{1,0:T(8,128)} %get-tuple-element.36), channel_id=1, source_target_pairs={{0,3},{1,2},{2,1},{3,0},{4,7},{5,6},{6,5},{7,4}} | collective-permute-start | bytes 442376 | tf_op jit(solution)/shard_map/ppermute | solution.py:570
  76.0 2.8 %copy-start.4 = (f32[288,128]{1,0:T(8,128)}, f32[288,128]{1,0:T(8,128)S(1)}, u32[]{:S(2)}) copy-start(f32[288,128]{1,0:T(8,128)S(1)} %collective-permute-done.4.refs_6_) | copy-start | bytes 442372
  78.8 0.7 copy-start.5
  78.8 0.8 copy-start
  78.8 0.9 copy-start.1
  78.8 0.9 copy-start.2

commit v8 on v7

--- a/solution.py
+++ b/solution.py
@@ -15,8 +15,9 @@
 LOG2E = 1.4426950408889634
 
 ROWS_STEP = 8
-SLOTS = 8
-AHEAD = 5
+SLOTS = 12
+AHEAD = 6
+START = 2
 LAG_SOFT = 2
 LAG_OUT = 4
 
@@ -55,8 +56,7 @@
                                      x_sem.at[k]) for k in range(4)]
     for copy in x_loads:
         copy.start()
-    for i in range(len(plan)):
-        load(i).start()
+    load(0).start()
     barrier = pltpu.get_barrier_semaphore()
     pl.semaphore_signal(barrier, inc=1, device_id=peer, device_id_type=mesh_id)
     pl.semaphore_wait(barrier, 1)
@@ -84,12 +84,16 @@
 
     for k in range(4):
         x_loads[k].wait()
+        if k == 1:
+            load(1).start()
         lax.fori_loop(k * rows // 64, (k + 1) * rows // 64, norm, 0)
 
     outs = ((q_part, q_ref), (k_part, k_ref), (v_part, v_ref))
     sends, writes = [], []
     for i, (_, part, turn, mine, j, done) in enumerate(plan):
         load(i).wait()
+        if i + 2 < len(plan):
+            load(i + 2).start()
         heads = mine // 128
         acc = jnp.dot(normed[...], weight[i], preferred_element_type=jnp.float32)
         for t in range(per):
@@ -199,7 +203,7 @@
             def _():
                 o_store(step, slot, d).start()
 
-    for step in range(min(AHEAD, n_steps)):
+    for step in range(min(START, n_steps)):
         for copy in loads(step, step):
             copy.start()
     m_ref[...] = jnp.zeros_like(m_ref)
@@ -211,6 +215,22 @@
         oslot = lax.rem(step, 2)
         for copy in loads(step, slot):
             copy.wait()
+        issued = jnp.minimum(step + AHEAD, START + 2 * step)
+        wanted = jnp.minimum(jnp.minimum(step + 1 + AHEAD, START + 2 * step + 2), n_steps)
+        for extra in range(2):
+            nxt = issued + extra
+
+            @pl.when(nxt < wanted)
+            def _():
+                nslot = lax.rem(nxt, SLOTS)
+
+                @pl.when(nxt >= SLOTS)
+                def _():
+                    for copy in stores(nxt - SLOTS, nslot):
+                        copy.wait()
+
+                for copy in loads(nxt, nslot):
+                    copy.start()
 
         for r in range(step_rows):
             local = pos_ref[first_row + step * step_rows + r] - base
@@ -261,19 +281,6 @@
         o_start(step, oslot)
         for copy in stores(step, slot):
             copy.start()
-
-        @pl.when(step + AHEAD < n_steps)
-        def _():
-            nxt = step + AHEAD
-            nslot = lax.rem(nxt, SLOTS)
-
-            @pl.when(nxt >= SLOTS)
-            def _():
-                for copy in stores(nxt - SLOTS, nslot):
-                    copy.wait()
-
-            for copy in loads(nxt, nslot):
-                copy.start()
 
         return carry
 
@@ -369,10 +376,8 @@
     for group in local:
         for copy in group:
             copy.start()
-    for n in range(n_chunks):
+    for n in range(2):
         w_load(n).start()
-    for copy in small:
-        copy.start()
     barrier = pltpu.get_barrier_semaphore()
     for peer in (core_peer, x_peer, far_peer, y_peer):
         pl.semaphore_signal(barrier, inc=1, device_id=peer, device_id_type=mesh_id)
@@ -445,6 +450,10 @@
 
     for n in range(n_chunks):
         w_load(n).wait()
+        if n + 2 < n_chunks:
+            w_load(n + 2).start()
+        else:
+            small[n + 2 - n_chunks].start()
         project_rows(n, 0, first)
         for v in range(2):
             for t in range(2):

time: 132 us -> 124 us (0.939)
  Pallas kernels: 118 us -> 111 us
    pallas_call x1, Pallas kernels: 48.4 us -> 43 us  [merge(): pl.pallas_call(functools.partial(merge_kernel, chunks), out_shape=jax.Sha...]
    pallas_call x1, Pallas kernels: 16.5 us -> 13.7 us  [project(): pl.pallas_call(project_kernel, out_shape=(pltpu.HBM((2, rows * q_cols //...]
  transfers between devices with their start and end apart: 6 -> 6, of which waited for: 2 -> 1; matrix products, arithmetic and copies ran while one was open for 0% -> 0% of each run, Pallas kernels for 11% -> 11%
where the time goes in v8:
time: 124 us
  Pallas kernels  111 us (90%)
  starting transfers between devices  4.93 us (4%)
  local copies, waits for them, and re-layouts  4.76 us (4%)
  waiting for transfers between devices  2.5 us (2%)
    pallas_call x3, Pallas kernels, attend(): pl.pallas_call(functools.partial(attend_kernel, n_steps, first_row, kv_he...  54.3 us
    pallas_call x1, Pallas kernels, merge(): pl.pallas_call(functools.partial(merge_kernel, chunks), out_shape=jax.Sha...  43 us
    pallas_call x1, Pallas kernels, project(): pl.pallas_call(project_kernel, out_shape=(pltpu.HBM((2, rows * q_cols //...  13.7 us
    ppermute x6, starting transfers between devices, local_step(): moved.append(lax.ppermute(p, 'sp', [(i, i ^ d) for i in range(sp_size)]))  4.93 us
    unnamed x19, local copies, waits for them, and re-layouts  4.15 us
    ppermute x6, waiting for transfers between devices, local_step(): moved.append(lax.ppermute(p, 'sp', [(i, i ^ d) for i in range(sp_size)]))  2.5 us
  transfers between devices with their start and end apart: 6, of which 1 were waited for; matrix products, arithmetic and copies ran while one was open for 0% of the time, Pallas kernels for 11%

profile of v8, /device:TPU:0, one launch (start us, length us, event | category | flops | bytes accessed | tf_op | source)
XLA Modules:
  0.0 123.9 jit_solution(6099430038755490067)
XLA Ops:
  0.6 13.7 %project.1 = (f32[2,2048,128]{2,1,0:T(8,128)}, f32[2,1024,128]{2,1,0:T(8,128)}, f32[2,1024,128]{2,1,0:T(8,128)}) custom-call(s32[256]{0:T(256)} %pos_ref.7, bf16[256,4608]{1,0:T(8,128)(2,1)} %refs_12_.1, f32[36,128]{1,0:T(8,128)} %bitcast.14, f32[256,256]{1,0:T(8,128)} %constant.8.clone.table_ref, bf16[4608,2048]{1,0:T(8,128)(2,1)} %wq_hbm.1, ...), custom_call_target="tpu_custom_call" | custom-call | flops 4831838208 | bytes 18874368 | tf_op jit(solution)/shard_map/project/pallas_call | solution.py:133
  14.3 25.7 %attend.3 = (bf16[256,512,128]{2,1,0:T(8,128)(2,1)}, bf16[256,512,128]{2,1,0:T(8,128)(2,1)}, f32[544,128]{1,0:T(8,128)}, f32[544,128]{1,0:T(8,128)}, f32[544,128]{1,0:T(8,128)}, /*index=5*/f32[544,128]{1,0:T(8,128)}) custom-call(s32[256]{0:T(256)} %pos_ref.7, s32[1]{0:T(128)} %bitcast.base_ref, f32[2,2048,128]{2,1,0:T(8,128)} %get-tuple-element.24.q_hbm, ...), custom_call_target="tpu_custom_call" | custom-call | flops 536870912 | bytes 67108864 | tf_op jit(solution)/shard_map/attend/pallas_call | solution.py:316
  40.1 0.0 copy-start.8
  40.1 0.0 copy-start.7
  40.1 0.0 copy-start.6
  40.1 14.3 %attend.4 = (bf16[256,512,128]{2,1,0:T(8,128)(2,1)}, bf16[256,512,128]{2,1,0:T(8,128)(2,1)}, f32[288,128]{1,0:T(8,128)}, f32[288,128]{1,0:T(8,128)}, f32[288,128]{1,0:T(8,128)}, /*index=5*/f32[288,128]{1,0:T(8,128)}) custom-call(s32[256]{0:T(256)} %pos_ref.7, s32[1]{0:T(128)} %bitcast.base_ref, ...), custom_call_target="tpu_custom_call", output_to_operand_aliasing={{0}: (7, {}), {1}: (8, {})} | custom-call | flops 268435456 | bytes 33554432 | tf_op jit(solution)/shard_map/attend/pallas_call | solution.py:316
  54.5 0.2 collective-permute-start.3
  54.6 0.4 collective-permute-start
  55.0 0.0 copy-done.8
  55.0 2.6 %collective-permute-start.1 = (f32[544,128]{1,0:T(8,128)S(1)}, f32[544,128]{1,0:T(8,128)S(1)}, u32[]{:S(2)}, u32[]{:S(2)}) collective-permute-start(f32[544,128]{1,0:T(8,128)S(1)} %copy-done.8), channel_id=1, source_target_pairs={{0,2},{1,3},{2,0},{3,1},{4,6},{5,7},{6,4},{7,5}} | collective-permute-start | bytes 835592 | tf_op jit(solution)/shard_map/ppermute | solution.py:579
  57.6 0.0 copy-done.7
  57.6 0.0 collective-permute-start.2
  57.6 1.7 %collective-permute-start.4 = (f32[288,128]{1,0:T(8,128)}, f32[288,128]{1,0:T(8,128)S(1)}, u32[]{:S(2)}, u32[]{:S(2)}) collective-permute-start(f32[288,128]{1,0:T(8,128)} %get-tuple-element.35), channel_id=1, source_target_pairs={{0,2},{1,3},{2,0},{3,1},{4,6},{5,7},{6,4},{7,5}} | collective-permute-start | bytes 442376 | tf_op jit(solution)/shard_map/ppermute | solution.py:579
  59.3 0.0 collective-permute-done.3.refs_5_
  59.3 0.0 copy-start.3
  59.3 0.1 collective-permute-start.5
  59.4 0.0 copy-done.6
  59.4 0.6 reshape.31.refs_13_
  60.0 14.2 %attend.5 = (bf16[256,512,128]{2,1,0:T(8,128)(2,1)}, bf16[256,512,128]{2,1,0:T(8,128)(2,1)}, f32[288,128]{1,0:T(8,128)}, f32[288,128]{1,0:T(8,128)}, f32[288,128]{1,0:T(8,128)}, /*index=5*/f32[288,128]{1,0:T(8,128)}) custom-call(s32[256]{0:T(256)} %pos_ref.7, s32[1]{0:T(128)} %bitcast.base_ref, ...), custom_call_target="tpu_custom_call", output_to_operand_aliasing={{0}: (7, {}), {1}: (8, {})} | custom-call | flops 268435456 | bytes 33554432 | tf_op jit(solution)/shard_map/attend/pallas_call | solution.py:316
  74.2 0.0 copy-done.3
  74.3 0.0 collective-permute-done.4.refs_6_
  74.3 0.0 copy-start.4
  74.3 2.5 %collective-permute-done.5.refs_7_ = f32[288,128]{1,0:T(8,128)S(1)} collective-permute-done((f32[288,128]{1,0:T(8,128)}, f32[288,128]{1,0:T(8,128)S(1)}, u32[]{:S(2)}, u32[]{:S(2)}) %collective-permute-start.5) | collective-permute-done | bytes 147488 | tf_op jit(solution)/shard_map/ppermute | solution.py:579
  76.8 0.0 copy-start.5
  76.8 0.0 collective-permute-done.refs_1_
  76.8 0.0 copy-start
  76.8 0.0 collective-permute-done.1.refs_2_
  76.8 0.0 copy-start.1
  76.8 0.0 collective-permute-done.2.refs_3_
  76.8 0.0 copy-start.2
  76.8 0.0 copy-done.4
  76.8 0.6 copy-done.5
  77.4 0.1 copy-done
  77.5 0.1 copy-done.1
  77.6 0.1 copy-done.2
  77.7 43.0 %merge.1 = bf16[256,4608]{1,0:T(8,128)(2,1)} custom-call(f32[544,128]{1,0:T(8,128)} %get-tuple-element.27.refs_0_, f32[544,128]{1,0:T(8,128)} %copy-done, f32[544,128]{1,0:T(8,128)} %copy-done.1, f32[544,128]{1,0:T(8,128)} %copy-done.2, f32[288,128]{1,0:T(8,128)} %get-tuple-element.33.refs_4_, f32[288,128]{1,0:T(8,128)} %copy-done.3, f32[288,128]{1,0:T(8,128)} %copy-done.4, ...), custom_call_target="tpu_custom_call" | custom-call | flops 1207959552 | bytes 18874368 | tf_op jit(solution)/shard_map/merge/pallas_call | solution.py:536
  120.7 3.2 %copy.23 = bf16[256,4608]{1,0:T(8,128)(2,1)} copy(bf16[256,4608]{1,0:T(8,128)(2,1)} %merge.1) | data formatting | bytes 4718592
Async XLA Ops:
  40.1 14.9 %copy-start.8 = (f32[544,128]{1,0:T(8,128)S(1)}, f32[544,128]{1,0:T(8,128)}, u32[]{:S(2)}) copy-start(f32[544,128]{1,0:T(8,128)} %get-tuple-element.29) | copy-start | bytes 835588
  40.1 17.5 %copy-start.7 = (f32[544,128]{1,0:T(8,128)S(1)}, f32[544,128]{1,0:T(8,128)}, u32[]{:S(2)}) copy-start(f32[544,128]{1,0:T(8,128)} %get-tuple-element.30) | copy-start | bytes 835588
  40.1 19.3 %copy-start.6 = (f32[4608]{0:T(1024)S(1)}, f32[4608]{0:T(1024)}, u32[]{:S(2)}) copy-start(f32[4608]{0:T(1024)} %param.18) | copy-start | bytes 55300
  54.5 4.9 %collective-permute-start.3 = (f32[288,128]{1,0:T(8,128)}, f32[288,128]{1,0:T(8,128)S(1)}, u32[]{:S(2)}, u32[]{:S(2)}) collective-permute-start(f32[288,128]{1,0:T(8,128)} %get-tuple-element.34), channel_id=1, source_target_pairs={{0,1},{1,0},{2,3},{3,2},{4,5},{5,4},{6,7},{7,6}} | collective-permute-start | bytes 442376 | tf_op jit(solution)/shard_map/ppermute | solution.py:579
  54.6 22.1 %collective-permute-start = (f32[544,128]{1,0:T(8,128)}, f32[544,128]{1,0:T(8,128)S(1)}, u32[]{:S(2)}, u32[]{:S(2)}) collective-permute-start(f32[544,128]{1,0:T(8,128)} %get-tuple-element.28), channel_id=1, source_target_pairs={{0,1},{1,0},{2,3},{3,2},{4,5},{5,4},{6,7},{7,6}} | collective-permute-start | bytes 835592 | tf_op jit(solution)/shard_map/ppermute | solution.py:579
  55.0 21.8 %collective-permute-start.1 = (f32[544,128]{1,0:T(8,128)S(1)}, f32[544,128]{1,0:T(8,128)S(1)}, u32[]{:S(2)}, u32[]{:S(2)}) collective-permute-start(f32[544,128]{1,0:T(8,128)S(1)} %copy-done.8), channel_id=1, source_target_pairs={{0,2},{1,3},{2,0},{3,1},{4,6},{5,7},{6,4},{7,5}} | collective-permute-start | bytes 835592 | tf_op jit(solution)/shard_map/ppermute | solution.py:579
  57.6 19.1 %collective-permute-start.2 = (f32[544,128]{1,0:T(8,128)S(1)}, f32[544,128]{1,0:T(8,128)S(1)}, u32[]{:S(2)}, u32[]{:S(2)}) collective-permute-start(f32[544,128]{1,0:T(8,128)S(1)} %copy-done.7), channel_id=1, source_target_pairs={{0,3},{1,2},{2,1},{3,0},{4,7},{5,6},{6,5},{7,4}} | collective-permute-start | bytes 835592 | tf_op jit(solution)/shard_map/ppermute | solution.py:579
  57.6 16.6 %collective-permute-start.4 = (f32[288,128]{1,0:T(8,128)}, f32[288,128]{1,0:T(8,128)S(1)}, u32[]{:S(2)}, u32[]{:S(2)}) collective-permute-start(f32[288,128]{1,0:T(8,128)} %get-tuple-element.35), channel_id=1, source_target_pairs={{0,2},{1,3},{2,0},{3,1},{4,6},{5,7},{6,4},{7,5}} | collective-permute-start | bytes 442376 | tf_op jit(solution)/shard_map/ppermute | solution.py:579
  59.3 14.9 %copy-start.3 = (f32[288,128]{1,0:T(8,128)}, f32[288,128]{1,0:T(8,128)S(1)}, u32[]{:S(2)}) copy-start(f32[288,128]{1,0:T(8,128)S(1)} %collective-permute-done.3.refs_5_) | copy-start | bytes 442372
  59.3 17.4 %collective-permute-start.5 = (f32[288,128]{1,0:T(8,128)}, f32[288,128]{1,0:T(8,128)S(1)}, u32[]{:S(2)}, u32[]{:S(2)}) collective-permute-start(f32[288,128]{1,0:T(8,128)} %get-tuple-element.36), channel_id=1, source_target_pairs={{0,3},{1,2},{2,1},{3,0},{4,7},{5,6},{6,5},{7,4}} | collective-permute-start | bytes 442376 | tf_op jit(solution)/shard_map/ppermute | solution.py:579
  74.3 2.5 %copy-start.4 = (f32[288,128]{1,0:T(8,128)}, f32[288,128]{1,0:T(8,128)S(1)}, u32[]{:S(2)}) copy-start(f32[288,128]{1,0:T(8,128)S(1)} %collective-permute-done.4.refs_6_) | copy-start | bytes 442372
  76.8 0.7 copy-start.5
  76.8 0.8 copy-start
  76.8 0.9 copy-start.1
  76.8 0.9 copy-start.2

commit v9 on v8

--- a/solution.py
+++ b/solution.py
@@ -154,7 +154,7 @@
     )(cur_pos, x_in, w_pre, table, w_q, w_k, w_v)
 
 
-def attend_kernel(n_steps, first_row, kv_heads, seq_block, pos_ref, base_ref, q_hbm, kn_hbm, vn_hbm, k_hbm, v_hbm,
+def attend_kernel(n_steps, quarter, first_row, kv_heads, seq_block, pos_ref, base_ref, q_hbm, kn_hbm, vn_hbm, k_hbm, v_hbm,
                   *rest):
     (ko_hbm, vo_hbm, o0_hbm, o1_hbm, o2_hbm, o3_hbm, m_ref, l_ref, kbuf, vbuf, qbuf, knbuf, vnbuf, obuf, key_ref, s_ref, p_ref, in_sem, out_sem, o_sem, st_sem) = rest[-21:]
     step_rows = ROWS_STEP
@@ -171,15 +171,19 @@
     lane_id = lax.broadcasted_iota(jnp.int32, m_ref.shape, 1)
     half_id = lax.broadcasted_iota(jnp.int32, (2 * kv_heads, head_dim), 0) // kv_heads
 
+    def row_of(step):
+        piece = step // piece_steps
+        return piece * quarter + first_row + (step - piece * piece_steps) * step_rows
+
     def heads_of(step, count):
-        return pl.ds((first_row + step * step_rows) * count, step_rows * count)
+        return pl.ds(row_of(step) * count, step_rows * count)
 
     def both_halves(ref, slot, r, count):
         at = slice(r * count, (r + 1) * count)
         return [ref[slot, 0, at, :], ref[slot, 1, at, :]]
 
     def loads(step, slot):
-        rows = pl.ds(first_row + step * step_rows, step_rows)
+        rows = pl.ds(row_of(step), step_rows)
         return (pltpu.make_async_copy(k_hbm.at[rows], kbuf.at[slot], in_sem.at[slot, 0]),
                 pltpu.make_async_copy(v_hbm.at[rows], vbuf.at[slot], in_sem.at[slot, 1]),
                 pltpu.make_async_copy(q_hbm.at[:, heads_of(step, q_half)], qbuf.at[slot], in_sem.at[slot, 2]),
@@ -187,12 +191,12 @@
                 pltpu.make_async_copy(vn_hbm.at[:, heads_of(step, kv_half)], vnbuf.at[slot], in_sem.at[slot, 4]))
 
     def stores(step, slot):
-        rows = pl.ds(first_row + step * step_rows, step_rows)
+        rows = pl.ds(row_of(step), step_rows)
         return (pltpu.make_async_copy(kbuf.at[slot], ko_hbm.at[rows], out_sem.at[slot, 0]),
                 pltpu.make_async_copy(vbuf.at[slot], vo_hbm.at[rows], out_sem.at[slot, 1]))
 
     def o_store(step, slot, d=0):
-        at = pl.ds(lax.rem(step, piece_steps) * step_rows * heads, step_rows * heads)
+        at = pl.ds((step - step // piece_steps * piece_steps) * step_rows * heads, step_rows * heads)
         o_hbm = (o0_hbm, o1_hbm, o2_hbm, o3_hbm)[d]
         return pltpu.make_async_copy(obuf.at[slot], o_hbm.at[at], o_sem.at[slot])
 
@@ -233,7 +237,7 @@
                     copy.start()
 
         for r in range(step_rows):
-            local = pos_ref[first_row + step * step_rows + r] - base
+            local = pos_ref[row_of(step) + r] - base
             inside = (local >= 0) & (local < seq_block)
             at = jnp.clip(local, 0, seq_block - 1)
             pair = pl.ds(pl.multiple_of((at // 2) * (2 * kv_heads), 2 * kv_heads), 2 * kv_heads)
@@ -259,7 +263,7 @@
                 s_ref[r] = raw
             r = tick - LAG_SOFT
             if 0 <= r < step_rows:
-                local = pos_ref[first_row + step * step_rows + r] - base
+                local = pos_ref[row_of(step) + r] - base
                 seen = key_ref[...] < (local + 1) * kv_heads
                 soft = jnp.where(seen, jnp.tanh(s_ref[r] * scale), -4.0)
                 top = jnp.maximum(jnp.max(soft, axis=-1, keepdims=True), -1.0)
@@ -314,7 +318,7 @@
     aliases = {} if prev is None else {7: 0, 8: 1}
     extra = () if prev is None else tuple(prev)
     return pl.pallas_call(
-        functools.partial(attend_kernel, n_steps, first_row, kv_heads, seq_block),
+        functools.partial(attend_kernel, n_steps, rows // 4, first_row, kv_heads, seq_block),
         out_shape=(jax.ShapeDtypeStruct(k_cache.shape, bf), jax.ShapeDtypeStruct(v_cache.shape, bf)) + (piece,) * 4,
         in_specs=[smem, smem, hbm, hbm, hbm, hbm, hbm] + [hbm] * len(extra),
         out_specs=(hbm, hbm) + (pl.BlockSpec(memory_space=pltpu.HBM),) * 4,
@@ -348,20 +352,19 @@
     source = [refs[4 * c:4 * c + 4] for c in range(len(chunks))]
     pieces = [[b.at[d] for d in range(4)] for b in refs[-len(chunks):]]
     refs = refs[:-len(chunks)]
-    (x_hbm, wpost_hbm, wo_hbm, out_ref, wo, xbuf, wpost_ref, last_in, osum, lhs, y_out, y_in, sums,
-     in_sem, p_sem, w_sem, o_send, o_recv, y_send, y_recv, g_send, g_recv, d_send, d_recv, f_send, f_recv) = refs[n_in:]
+    (wo_hbm, out_hbm, wo, last_in, last_out, osum, lhs, y_out, y_in, sums,
+     p_sem, w_sem, o_send, o_recv, y_send, y_recv, g_send, g_recv, d_send, d_recv, f_send, f_recv, out_sem) = refs[n_in:]
     sp = lax.axis_index('sp')
     tp = lax.axis_index('tp')
     core = lax.rem(sp, 2)
     xpos = sp // 2
-    _, width = xbuf.shape
-    n_chunks, quarter, chunk = y_out.shape
+    n_chunks, _, chunk = y_out.shape
     heads = lhs.shape[1] // 128
     parts = [c // 4 for c in chunks]
-    core_peer = {'sp': 2 * xpos + (1 - core)}
-    x_peer = {'sp': 2 * (1 - xpos) + core}
-    far_peer = {'sp': 2 * (1 - xpos) + (1 - core)}
-    y_peer = {'tp': 1 - tp}
+    core_id = 2 * xpos + (1 - core)
+    x_id = 2 * (1 - xpos) + core
+    far_id = 2 * (1 - xpos) + (1 - core)
+    core_peer, x_peer, y_peer = {'sp': core_id}, {'sp': x_id}, {'tp': 1 - tp}
     mesh_id = pl.DeviceIdType.MESH
 
     def remote(src, dst, send, recv, peer):
@@ -371,189 +374,201 @@
     def w_load(n):
         return pltpu.make_async_copy(wo_hbm.at[:, pl.ds(n * chunk, chunk)], wo.at[n], w_sem.at[n])
 
-    small = [pltpu.make_async_copy(x_hbm, xbuf, in_sem.at[0]), pltpu.make_async_copy(wpost_hbm, wpost_ref, in_sem.at[1])]
     local = [[pltpu.make_async_copy(source[c][d], pieces[c][d], p_sem.at[c, d]) for d in range(4)] for c in range(len(chunks))]
-    for group in local:
+    for group in (local[-1], local[0]):
         for copy in group:
             copy.start()
     for n in range(2):
         w_load(n).start()
     barrier = pltpu.get_barrier_semaphore()
-    for peer in (core_peer, x_peer, far_peer, y_peer):
+    for peer in (core_peer, x_peer, y_peer):
         pl.semaphore_signal(barrier, inc=1, device_id=peer, device_id_type=mesh_id)
-    pl.semaphore_wait(barrier, 4)
+    pl.semaphore_wait(barrier, 3)
 
     for copy in local[-1]:
         copy.wait()
-    last = [remote(pieces[-1][d], last_in.at[d - 1], o_send.at[d - 1], o_recv.at[d - 1], peer)
-            for d, peer in ((2, x_peer), (3, far_peer), (1, core_peer))]
-    for copy in last:
-        copy.start()
-
-    def combine(blocks, part, row0):
+    last = [remote(pieces[-1][3], last_in.at[0], o_send.at[0], o_recv.at[0], core_peer),
+            remote(pieces[-1][1], last_in.at[1], o_send.at[1], o_recv.at[1], core_peer),
+            remote(last_out, last_in.at[2], o_send.at[2], o_recv.at[2], x_peer)]
+    last[0].start()
+    last[1].start()
+
+    def shares(blocks, part):
         count = part * heads
         stats = [block[count:count + 2 * heads, :] for block in blocks]
         top = functools.reduce(jnp.maximum, [st[:heads] for st in stats])
         grown = [jnp.exp(st[:heads] - top) for st in stats]
-        total = sum(st[heads:] * g for st, g in zip(stats, grown))
-        shift = lax.rem(128 - sp * part, 128)
-        factors = [pltpu.roll(g / total, shift, 1) for g in grown]
+        return top, sum(st[heads:] * g for st, g in zip(stats, grown)), grown
+
+    def mix(blocks, weights, owner, part, out):
+        shift = lax.rem(128 - owner * part, 128)
+        factors = [pltpu.roll(w, shift, 1) for w in weights]
         for b in range(part):
             at = slice(b * heads, (b + 1) * heads)
-            osum[at, :] = sum(block[at, :] * f[:, b:b + 1] for block, f in zip(blocks, factors))
+            out[at, :] = sum(block[at, :] * f[:, b:b + 1] for block, f in zip(blocks, factors))
+
+    def combine(blocks, part, row0):
+        _, total, grown = shares(blocks, part)
+        mix(blocks, [g / total for g in grown], sp, part, osum)
         for h in range(heads):
             lhs[row0:row0 + part, h * 128:(h + 1) * 128] = osum[pl.ds(h, part, stride=heads), :].astype(jnp.bfloat16)
 
-    first = sum(parts[:-1])
-    row0 = 0
-    for c in range(len(chunks) - 1):
-        for copy in local[c]:
-            copy.wait()
-        combine(pieces[c], parts[c], row0)
-        row0 += parts[c]
-
-    first_at, last_at = pl.ds(0, first), pl.ds(first, quarter - first)
-    split = ((2, 2, 2, 2, 1), (1, 2, 2, 2, 2))
-    wide = 3
-    orders = []
-    for sizes in split:
-        begin, order = 0, []
+    for copy in local[0]:
+        copy.wait()
+    combine(pieces[0], parts[0], 0)
+
+    last[0].wait_recv()
+    pair = [pieces[-1][2], last_in.at[0]]
+    top, total, grown = shares(pair, parts[-1])
+    mix(pair, grown, x_id, parts[-1], last_out)
+    count = parts[-1] * heads
+    last_out[count:count + heads, :] = top
+    last_out[count + heads:count + 2 * heads, :] = total
+    last[2].start()
+
+    sizes = (2, 2, 2, 2, 1)
+    order = []
+    for c, part in enumerate(parts):
+        begin = 0
         for size in sizes:
-            order.append((begin, size, first_at))
+            order.append((pl.ds(begin, size), pl.ds(sum(parts[:c]), part), range(begin, begin + size)))
             begin += size
-        orders.append(order + [(n, wide, last_at) for n in range(0, n_chunks, wide)])
-    n_pieces = len(orders[0])
-
-    def to_y(v, t):
-        n, size, r = orders[v][t]
-        ns = pl.ds(n, size)
+    n_pieces = len(order)
+    n_first = len(sizes)
+
+    def to_y(t):
+        ns, r, _ = order[t]
         return remote(y_out.at[ns, r], y_in.at[ns, r], y_send.at[t], y_recv.at[t], y_peer)
 
-    def to_x(v, t):
-        n, size, r = orders[v][t]
-        ns = pl.ds(n, size)
-        return remote(sums.at[sp, ns, r], sums.at[sp, ns, r], g_send.at[t], g_recv.at[t], x_peer)
-
-    def to_core(v, t):
-        n, size, r = orders[v][t]
-        ns = pl.ds(n, size)
-        return remote(sums.at[sp, ns, r], sums.at[sp, ns, r], d_send.at[t], d_recv.at[t], core_peer)
-
-    def relay(v, t):
-        n, size, r = orders[v][t]
-        ns = pl.ds(n, size)
-        other = 2 * (1 - xpos) + core
-        return remote(sums.at[other, ns, r], sums.at[other, ns, r], f_send.at[t], f_recv.at[t], core_peer)
+    def gather(t, owner, send, recv, peer):
+        ns, r, _ = order[t]
+        return remote(sums.at[owner, ns, r], sums.at[owner, ns, r], send.at[t], recv.at[t], peer)
+
+    def to_x(t):
+        return gather(t, sp, g_send, g_recv, x_peer)
+
+    def to_core(t):
+        return gather(t, sp, d_send, d_recv, core_peer)
+
+    def relay(t):
+        return gather(t, x_id, f_send, f_recv, core_peer)
+
+    def keep(t, turn, owner):
+        ns, r, _ = order[t]
+        return pltpu.make_async_copy(sums.at[owner, ns, r], out_hbm.at[owner, ns, r], out_sem.at[turn, t])
 
     def project_rows(n, r0, count):
         y_out[n, r0:r0 + count, :] = jnp.dot(lhs[r0:r0 + count, :], wo[n], preferred_element_type=jnp.float32)
 
-    for n in range(n_chunks):
-        w_load(n).wait()
-        if n + 2 < n_chunks:
-            w_load(n + 2).start()
-        else:
-            small[n + 2 - n_chunks].start()
-        project_rows(n, 0, first)
-        for v in range(2):
-            for t in range(2):
-                if sum(orders[v][t][:2]) == n + 1:
-                    @pl.when(core == v)
-                    def _():
-                        to_y(v, t).start()
-
-    def step(v, t):
+    for t in range(n_first):
+        for n in order[t][2]:
+            w_load(n).wait()
+            if n + 2 < n_chunks:
+                w_load(n + 2).start()
+            project_rows(n, 0, parts[0])
+        if t < 2:
+            to_y(t).start()
+
+    for t in range(n_pieces + 3):
+        if t == 2:
+            for copy in last[1:]:
+                copy.wait_recv()
+            combine([pieces[-1][0], last_in.at[1], last_in.at[2]], parts[-1], parts[0])
+        if 2 <= t < 2 + n_first:
+            for n in order[n_first + t - 2][2]:
+                project_rows(n, parts[0], parts[-1])
         if t < n_pieces:
-            n, size, r = orders[v][t]
-            ns = pl.ds(n, size)
-            to_y(v, t).wait()
+            ns, r, _ = order[t]
+            to_y(t).wait()
             if t + 2 < n_pieces:
-                to_y(v, t + 2).start()
+                to_y(t + 2).start()
             sums[sp, ns, r, :] = y_out[ns, r, :] + y_in[ns, r, :]
-            to_x(v, t).start()
-            to_core(v, t).start()
-        if t >= 1:
-            to_x(v, t - 1).wait_recv()
-            relay(v, t - 1).start()
-
-    for t in range(n_pieces + 1):
-        if t == 1:
-            for copy in last:
-                copy.wait()
-            combine([pieces[-1][0]] + [last_in.at[d] for d in range(3)], parts[-1], first)
-        if 1 <= t < 1 + n_chunks // wide:
-            for n in range((t - 1) * wide, t * wide):
-                project_rows(n, first, quarter - first)
-        for v in range(2):
-            @pl.when(core == v)
-            def _():
-                step(v, t)
-    for copy in small:
-        copy.wait()
-    for v in range(2):
-        @pl.when(core == v)
-        def _():
-            for t in range(n_pieces):
-                to_x(v, t).wait_send()
-                to_core(v, t).wait_send()
-                relay(v, t).wait_send()
-                to_core(1 - v, t).wait_recv()
-                relay(1 - v, t).wait_recv()
-
-    starts = []
-    base = 0
-    for c, part in zip(chunks, parts):
-        starts += [(base, part, k) for k in range(0, part, 16)]
-        base += c
-    for q in range(4):
-        for k, (base, part, off) in enumerate(starts):
-            at = slice(k * 16, (k + 1) * 16)
-            out_at = slice(base + q * part + off, base + q * part + off + 16)
-            square = jnp.zeros((16, chunk), jnp.float32)
-            for n in range(n_chunks):
-                u = sums[q, n, at, :]
-                square = square + u * u
-            inv = lax.rsqrt(jnp.sum(square, axis=-1, keepdims=True) * (1.0 / width) + NORM_EPS)
-            for n in range(n_chunks):
-                col = slice(n * chunk, (n + 1) * chunk)
-                y = xbuf[out_at, col].astype(jnp.float32) + sums[q, n, at, :] * inv * (1.0 + wpost_ref[:, col])
-                out_ref[out_at, col] = y.astype(jnp.bfloat16)
-
-
-def merge(chunks, pieces, x_in, w_post, w_o, n_chunks):
-    rows, width = x_in.shape
-    inner = w_o.shape[0]
+            to_x(t).start()
+            to_core(t).start()
+            keep(t, 0, sp).start()
+        if 1 <= t < n_pieces + 1:
+            to_x(t - 1).wait_recv()
+            relay(t - 1).start()
+            keep(t - 1, 1, x_id).start()
+        if t >= 3:
+            to_core(t - 3).wait_recv()
+            keep(t - 3, 2, core_id).start()
+            relay(t - 3).wait_recv()
+            keep(t - 3, 3, far_id).start()
+    for copy in last:
+        copy.wait_send()
+    for t in range(n_pieces):
+        to_x(t).wait_send()
+        to_core(t).wait_send()
+        relay(t).wait_send()
+        for turn in range(4):
+            keep(t, turn, sp).wait()
+
+
+def merge(chunks, pieces, w_o, n_chunks):
+    inner, width = w_o.shape
     heads = inner // 128
-    quarter = rows // 4
+    quarter = sum(chunks) // 4
     chunk = width // n_chunks
-    vmem = pl.BlockSpec(memory_space=pltpu.VMEM)
-    hbm = pl.BlockSpec(memory_space=pl.ANY)
+    hbm = pl.BlockSpec(memory_space=pltpu.HBM)
     f32 = jnp.float32
     dma = pltpu.SemaphoreType.DMA
-    per_piece = dma((n_chunks + 3,))
     flat = [p for piece in pieces for p in piece]
-    big = max(chunks) // 4 * heads
+    block = pieces[-1][0].shape
     return pl.pallas_call(
         functools.partial(merge_kernel, chunks),
-        out_shape=jax.ShapeDtypeStruct(x_in.shape, x_in.dtype),
-        in_specs=[pl.BlockSpec(memory_space=pltpu.HBM)] * (len(flat) + 3),
-        out_specs=vmem,
+        out_shape=pltpu.HBM((4, n_chunks, quarter, chunk), f32),
+        in_specs=[hbm] * (len(flat) + 1),
+        out_specs=hbm,
         scratch_shapes=[
             pltpu.VMEM((n_chunks, inner, chunk), jnp.bfloat16),
-            pltpu.VMEM(x_in.shape, x_in.dtype),
-            pltpu.VMEM(w_post.shape, f32),
-            pltpu.VMEM((3,) + pieces[-1][0].shape, f32),
-            pltpu.VMEM((big, 128), f32),
+            pltpu.VMEM((3,) + block, f32),
+            pltpu.VMEM(block, f32),
+            pltpu.VMEM((max(chunks) // 4 * heads, 128), f32),
             pltpu.VMEM((quarter, inner), jnp.bfloat16),
             pltpu.VMEM((n_chunks, quarter, chunk), f32),
             pltpu.VMEM((n_chunks, quarter, chunk), f32),
             pltpu.VMEM((4, n_chunks, quarter, chunk), f32),
-            dma((2,)), dma((len(chunks), 4)), dma((n_chunks,)), dma((3,)), dma((3,)),
-        ] + [per_piece] * 8 + [pltpu.VMEM((4,) + piece[0].shape, f32) for piece in pieces],
+            dma((len(chunks), 4)), dma((n_chunks,)), dma((3,)), dma((3,)),
+        ] + [dma((10,))] * 8 + [dma((4, 10))] + [pltpu.VMEM((4,) + piece[0].shape, f32) for piece in pieces],
         compiler_params=pltpu.CompilerParams(vmem_limit_bytes=56 * 1024 * 1024, collective_id=0, has_side_effects=True),
         cost_estimate=pl.CostEstimate(flops=2 * quarter * inner * width, bytes_accessed=2 * inner * width, transcendentals=0),
         name='merge',
-    )(*flat, x_in, w_post, pltpu.with_memory_space_constraint(w_o, pltpu.HBM))
+    )(*flat, pltpu.with_memory_space_constraint(w_o, pltpu.HBM))
+
+
+def finish_kernel(sums_ref, x_ref, wpost_ref, out_ref, gain_ref):
+    _, n_chunks, rows, chunk = sums_ref.shape
+    for j in range(wpost_ref.shape[0]):
+        gain_ref[:, j * 128:(j + 1) * 128] = 1.0 + wpost_ref[j:j + 1, :]
+    for k in range(rows // 16):
+        at = slice(k * 16, (k + 1) * 16)
+        square = jnp.zeros((16, chunk), jnp.float32)
+        for n in range(n_chunks):
+            u = sums_ref[0, n, at, :]
+            square = square + u * u
+        inv = lax.rsqrt(jnp.sum(square, axis=-1, keepdims=True) * (1.0 / (n_chunks * chunk)) + NORM_EPS)
+        for n in range(n_chunks):
+            col = slice(n * chunk, (n + 1) * chunk)
+            y = x_ref[at, col].astype(jnp.float32) + sums_ref[0, n, at, :] * inv * gain_ref[:, col]
+            out_ref[at, col] = y.astype(jnp.bfloat16)
+
+
+def finish(sums, x_in, w_post):
+    parts, n_chunks, quarter, chunk = sums.shape
+    width = n_chunks * chunk
+    return pl.pallas_call(
+        finish_kernel,
+        grid=(parts,),
+        out_shape=jax.ShapeDtypeStruct(x_in.shape, x_in.dtype),
+        in_specs=[pl.BlockSpec((1, n_chunks, quarter, chunk), lambda q: (q, 0, 0, 0)),
+                  pl.BlockSpec((quarter, width), lambda q: (q, 0)),
+                  pl.BlockSpec(w_post.shape, lambda q: (0, 0))],
+        out_specs=pl.BlockSpec((quarter, width), lambda q: (q, 0)),
+        scratch_shapes=[pltpu.VMEM((1, width), jnp.float32)],
+        compiler_params=pltpu.CompilerParams(vmem_limit_bytes=62 * 1024 * 1024),
+        name='finish',
+    )(sums, x_in, w_post)
 
 
 def solution(mesh):
@@ -568,11 +583,11 @@
         base = (sp_index * seq_block).astype(jnp.int32).reshape(1)
         kc = k_cache.reshape(row_count, seq_block * kv_local, head_dim)
         vc = v_cache.reshape(row_count, seq_block * kv_local, head_dim)
-        chunks = (row_count // 2, row_count // 4, row_count // 4)
+        chunks = (row_count // 2, row_count // 2)
         prev, first_row, pieces = None, 0, []
         for index, n_rows in enumerate(chunks):
             *prev, p0, p1, p2, p3 = attend(cur_pos, base, q_rot, kn2, vn2, kc, vc, prev, first_row, n_rows)
-            first_row += n_rows
+            first_row += n_rows // 4
             if index < len(chunks) - 1:
                 moved = []
                 for d, p in ((1, p1), (2, p2), (3, p3)):
@@ -580,7 +595,7 @@
                 p1, p2, p3 = moved
             pieces.append((p0, p1, p2, p3))
         k_out, v_out = prev
-        x_out = merge(chunks, pieces, x_in, w_post.reshape(1, -1), w_o, 9)
+        x_out = finish(merge(chunks, pieces, w_o, 9), x_in, w_post.reshape(-1, 128))
         return x_out, k_out.reshape(k_cache.shape), v_out.reshape(v_cache.shape)
 
     return jax.shard_map(local_step, mesh=mesh,

time: 124 us -> 118 us (0.952)
  local copies, waits for them, and re-layouts: 4.76 us -> 0.87 us
  waiting for transfers between devices: 2.5 us -> 0.01 us
  Pallas kernels: 111 us -> 113 us
  starting transfers between devices: 4.93 us -> 3.02 us
    unnamed x19 -> x6, local copies, waits for them, and re-layouts: 4.15 us -> 0.87 us
    ppermute x6 -> x3, waiting for transfers between devices: 2.5 us -> 0.01 us  [local_step(): moved.append(lax.ppermute(p, 'sp', [(i, i ^ d) for i in range(sp_size)]))]
    pallas_call x4, Pallas kernels: 97.3 us -> 99.7 us  [the longest x2 51.3 us: attend(): pl.pallas_call(functools.partial(attend_kernel, n_steps, rows // 4, first...]
    ppermute x6 -> x3, starting transfers between devices: 4.93 us -> 3.02 us  [local_step(): moved.append(lax.ppermute(p, 'sp', [(i, i ^ d) for i in range(sp_size)]))]
  transfers between devices with their start and end apart: 6 -> 3, of which waited for: 1 -> 0; matrix products, arithmetic and copies ran while one was open for 0% -> 0% of each run, Pallas kernels for 11% -> 22%
where the time goes in v9:
time: 118 us
  Pallas kernels  113 us (96%)
  starting transfers between devices  3.02 us (3%)
    pallas_call x2, Pallas kernels, attend(): pl.pallas_call(functools.partial(attend_kernel, n_steps, rows // 4, first...  51.3 us
    pallas_call x1, Pallas kernels, merge(): pl.pallas_call(functools.partial(merge_kernel, chunks), out_shape=pltpu.H...  42.8 us
    pallas_call x1, Pallas kernels, project(): pl.pallas_call(project_kernel, out_shape=(pltpu.HBM((2, rows * q_cols //...  13.7 us
    pallas_call x1, Pallas kernels, finish(): pl.pallas_call(finish_kernel, grid=(parts,), out_shape=jax.ShapeDtypeStru...  5.54 us
    ppermute x3, starting transfers between devices, local_step(): moved.append(lax.ppermute(p, 'sp', [(i, i ^ d) for i in range(sp_size)]))  3.02 us
  transfers between devices with their start and end apart: 3, of which 0 were waited for; matrix products, arithmetic and copies ran while one was open for 0% of the time, Pallas kernels for 22%

profile of v9, /device:TPU:0, one launch (start us, length us, event | category | flops | bytes accessed | tf_op | source)
XLA Modules:
  0.0 118.0 jit_solution(87512363267013211)
XLA Ops:
  0.6 13.7 %project.1 = (f32[2,2048,128]{2,1,0:T(8,128)}, f32[2,1024,128]{2,1,0:T(8,128)}, f32[2,1024,128]{2,1,0:T(8,128)}) custom-call(s32[256]{0:T(256)} %pos_ref.5, bf16[256,4608]{1,0:T(8,128)(2,1)} %x_ref.1, f32[36,128]{1,0:T(8,128)} %bitcast.13, f32[256,256]{1,0:T(8,128)} %constant.8.clone.table_ref, bf16[4608,2048]{1,0:T(8,128)(2,1)} %wq_hbm.1, ...), custom_call_target="tpu_custom_call" | custom-call | flops 4831838208 | bytes 18874368 | tf_op jit(solution)/shard_map/project/pallas_call | solution.py:133
  14.3 25.7 %attend.2 = (bf16[256,512,128]{2,1,0:T(8,128)(2,1)}, bf16[256,512,128]{2,1,0:T(8,128)(2,1)}, f32[544,128]{1,0:T(8,128)}, f32[544,128]{1,0:T(8,128)}, f32[544,128]{1,0:T(8,128)}, /*index=5*/f32[544,128]{1,0:T(8,128)}) custom-call(s32[256]{0:T(256)} %pos_ref.5, s32[1]{0:T(128)} %bitcast.base_ref, f32[2,2048,128]{2,1,0:T(8,128)} %get-tuple-element.18.q_hbm, ...), custom_call_target="tpu_custom_call" | custom-call | flops 536870912 | bytes 67108864 | tf_op jit(solution)/shard_map/attend/pallas_call | solution.py:320
  40.0 0.2 collective-permute-start
  40.2 2.8 %collective-permute-start.1 = (f32[544,128]{1,0:T(8,128)}, f32[544,128]{1,0:T(8,128)S(1)}, u32[]{:S(2)}, u32[]{:S(2)}) collective-permute-start(f32[544,128]{1,0:T(8,128)} %get-tuple-element.23), channel_id=1, source_target_pairs={{0,2},{1,3},{2,0},{3,1},{4,6},{5,7},{6,4},{7,5}} | collective-permute-start | bytes 835592 | tf_op jit(solution)/shard_map/ppermute | solution.py:594
  43.0 0.0 collective-permute-start.2
  43.0 25.7 %attend.3 = (bf16[256,512,128]{2,1,0:T(8,128)(2,1)}, bf16[256,512,128]{2,1,0:T(8,128)(2,1)}, f32[544,128]{1,0:T(8,128)}, f32[544,128]{1,0:T(8,128)}, f32[544,128]{1,0:T(8,128)}, /*index=5*/f32[544,128]{1,0:T(8,128)}) custom-call(s32[256]{0:T(256)} %pos_ref.5, s32[1]{0:T(128)} %bitcast.base_ref, ...), custom_call_target="tpu_custom_call", output_to_operand_aliasing={{0}: (7, {}), {1}: (8, {})} | custom-call | flops 536870912 | bytes 67108864 | tf_op jit(solution)/shard_map/attend/pallas_call | solution.py:320
  68.7 0.0 collective-permute-done.refs_1_
  68.7 0.0 copy-start
  68.7 0.0 collective-permute-done.1.refs_2_
  68.7 0.0 copy-start.1
  68.7 0.0 collective-permute-done.2.refs_3_
  68.7 0.0 copy-start.2
  68.8 0.7 copy-done
  69.4 0.1 copy-done.1
  69.5 0.1 copy-done.2
  69.6 42.8 %merge.1.sums_ref = f32[4,9,64,512]{3,2,1,0:T(8,128)} custom-call(f32[544,128]{1,0:T(8,128)} %get-tuple-element.21.refs_0_, f32[544,128]{1,0:T(8,128)} %copy-done, f32[544,128]{1,0:T(8,128)} %copy-done.1, f32[544,128]{1,0:T(8,128)} %copy-done.2, f32[544,128]{1,0:T(8,128)} %get-tuple-element.27.refs_4_, f32[544,128]{1,0:T(8,128)} %get-tuple-element.28.refs_5_, ...), custom_call_target="tpu_custom_call" | custom-call | flops 1207959552 | bytes 18874368 | tf_op jit(solution)/shard_map/merge/pallas_call | solution.py:518
  112.4 5.5 %finish.1 = bf16[256,4608]{1,0:T(8,128)(2,1)} custom-call(f32[4,9,64,512]{3,2,1,0:T(8,128)} %merge.1.sums_ref, bf16[256,4608]{1,0:T(8,128)(2,1)} %x_ref.1, f32[36,128]{1,0:T(8,128)} %bitcast.14), custom_call_target="tpu_custom_call" | custom-call | tf_op jit(solution)/shard_map/finish/pallas_call | solution.py:560
Async XLA Ops:
  40.0 28.7 %collective-permute-start = (f32[544,128]{1,0:T(8,128)}, f32[544,128]{1,0:T(8,128)S(1)}, u32[]{:S(2)}, u32[]{:S(2)}) collective-permute-start(f32[544,128]{1,0:T(8,128)} %get-tuple-element.22), channel_id=1, source_target_pairs={{0,1},{1,0},{2,3},{3,2},{4,5},{5,4},{6,7},{7,6}} | collective-permute-start | bytes 835592 | tf_op jit(solution)/shard_map/ppermute | solution.py:594
  40.2 28.5 %collective-permute-start.1 = (f32[544,128]{1,0:T(8,128)}, f32[544,128]{1,0:T(8,128)S(1)}, u32[]{:S(2)}, u32[]{:S(2)}) collective-permute-start(f32[544,128]{1,0:T(8,128)} %get-tuple-element.23), channel_id=1, source_target_pairs={{0,2},{1,3},{2,0},{3,1},{4,6},{5,7},{6,4},{7,5}} | collective-permute-start | bytes 835592 | tf_op jit(solution)/shard_map/ppermute | solution.py:594
  43.0 25.7 %collective-permute-start.2 = (f32[544,128]{1,0:T(8,128)}, f32[544,128]{1,0:T(8,128)S(1)}, u32[]{:S(2)}, u32[]{:S(2)}) collective-permute-start(f32[544,128]{1,0:T(8,128)} %get-tuple-element.24), channel_id=1, source_target_pairs={{0,3},{1,2},{2,1},{3,0},{4,7},{5,6},{6,5},{7,4}} | collective-permute-start | bytes 835592 | tf_op jit(solution)/shard_map/ppermute | solution.py:594
  68.7 0.7 copy-start
  68.7 0.8 copy-start.1
  68.7 0.9 copy-start.2

commit v10 on v9

--- a/solution.py
+++ b/solution.py
@@ -76,7 +76,7 @@
     lax.fori_loop(0, rows // 8, look_up, 0)
 
     def norm(k, carry):
-        at = pl.ds(pl.multiple_of(k * 16, 16), 16)
+        at = pl.ds(pl.multiple_of(k * 32, 32), 32)
         x = x_ref[at, :].astype(jnp.float32)
         inv = lax.rsqrt(jnp.mean(x * x, axis=-1, keepdims=True) + NORM_EPS)
         normed[at, :] = (x * inv * gain).astype(jnp.bfloat16)
@@ -86,7 +86,7 @@
         x_loads[k].wait()
         if k == 1:
             load(1).start()
-        lax.fori_loop(k * rows // 64, (k + 1) * rows // 64, norm, 0)
+        lax.fori_loop(k * rows // 128, (k + 1) * rows // 128, norm, 0)
 
     outs = ((q_part, q_ref), (k_part, k_ref), (v_part, v_ref))
     sends, writes = [], []
@@ -100,23 +100,18 @@
             value = acc[:, t * 128:(t + 1) * 128]
             if turn:
                 value = value * cos_ref[...] + pltpu.roll(value, 64, 1) * sin_ref[...]
-            part[core, pl.ds(j * per + t, rows, stride=heads), :] = value
+            part[pl.ds(j * per + t, rows, stride=heads), :] = value
         if done:
             n = len(sends)
-            copy = pltpu.make_async_remote_copy(src_ref=part.at[core], dst_ref=part.at[core], send_sem=send_sem.at[n],
+            copy = pltpu.make_async_remote_copy(src_ref=part, dst_ref=outs[n][1].at[core], send_sem=send_sem.at[n],
                                                 recv_sem=recv_sem.at[n], device_id=peer, device_id_type=mesh_id)
             copy.start()
             sends.append(copy)
-            out = pltpu.make_async_copy(part.at[core], outs[n][1].at[core], out_sem.at[0, n])
+            out = pltpu.make_async_copy(part, outs[n][1].at[core], out_sem.at[n])
             out.start()
             writes.append(out)
-    for n, copy in enumerate(sends):
-        copy.wait_recv()
-        out = pltpu.make_async_copy(outs[n][0].at[1 - core], outs[n][1].at[1 - core], out_sem.at[1, n])
-        out.start()
-        writes.append(out)
     for copy in sends:
-        copy.wait_send()
+        copy.wait()
     for copy in writes:
         copy.wait()
 
@@ -143,10 +138,10 @@
             pltpu.VMEM((rows, 128), f32),
             pltpu.VMEM((n_blocks, width, block), bf),
             pltpu.VMEM((rows, width), bf),
-            pltpu.VMEM((2, rows * q_cols // 256, 128), f32),
-            pltpu.VMEM((2, rows * kv_cols // 256, 128), f32),
-            pltpu.VMEM((2, rows * kv_cols // 256, 128), f32),
-            dma((4,)), dma((n_blocks,)), dma((3,)), dma((3,)), dma((2, 3)),
+            pltpu.VMEM((rows * q_cols // 256, 128), f32),
+            pltpu.VMEM((rows * kv_cols // 256, 128), f32),
+            pltpu.VMEM((rows * kv_cols // 256, 128), f32),
+            dma((4,)), dma((n_blocks,)), dma((3,)), dma((3,)), dma((3,)),
         ],
         compiler_params=pltpu.CompilerParams(vmem_limit_bytes=62 * 1024 * 1024, collective_id=1, has_side_effects=True),
         cost_estimate=pl.CostEstimate(flops=rows * width * (q_cols + 2 * kv_cols), bytes_accessed=width * (q_cols + 2 * kv_cols), transcendentals=0),
@@ -413,10 +408,6 @@
         for h in range(heads):
             lhs[row0:row0 + part, h * 128:(h + 1) * 128] = osum[pl.ds(h, part, stride=heads), :].astype(jnp.bfloat16)
 
-    for copy in local[0]:
-        copy.wait()
-    combine(pieces[0], parts[0], 0)
-
     last[0].wait_recv()
     pair = [pieces[-1][2], last_in.at[0]]
     top, total, grown = shares(pair, parts[-1])
@@ -425,6 +416,10 @@
     last_out[count:count + heads, :] = top
     last_out[count + heads:count + 2 * heads, :] = total
     last[2].start()
+
+    for copy in local[0]:
+        copy.wait()
+    combine(pieces[0], parts[0], 0)
 
     sizes = (2, 2, 2, 2, 1)
     order = []
@@ -466,8 +461,7 @@
             if n + 2 < n_chunks:
                 w_load(n + 2).start()
             project_rows(n, 0, parts[0])
-        if t < 2:
-            to_y(t).start()
+        to_y(t).start()
 
     for t in range(n_pieces + 3):
         if t == 2:
@@ -477,11 +471,10 @@
         if 2 <= t < 2 + n_first:
             for n in order[n_first + t - 2][2]:
                 project_rows(n, parts[0], parts[-1])
+            to_y(n_first + t - 2).start()
         if t < n_pieces:
             ns, r, _ = order[t]
             to_y(t).wait()
-            if t + 2 < n_pieces:
-                to_y(t + 2).start()
             sums[sp, ns, r, :] = y_out[ns, r, :] + y_in[ns, r, :]
             to_x(t).start()
             to_core(t).start()
@@ -559,12 +552,12 @@
     width = n_chunks * chunk
     return pl.pallas_call(
         finish_kernel,
-        grid=(parts,),
+        grid=(parts, 2),
         out_shape=jax.ShapeDtypeStruct(x_in.shape, x_in.dtype),
-        in_specs=[pl.BlockSpec((1, n_chunks, quarter, chunk), lambda q: (q, 0, 0, 0)),
-                  pl.BlockSpec((quarter, width), lambda q: (q, 0)),
-                  pl.BlockSpec(w_post.shape, lambda q: (0, 0))],
-        out_specs=pl.BlockSpec((quarter, width), lambda q: (q, 0)),
+        in_specs=[pl.BlockSpec((1, n_chunks, quarter // 2, chunk), lambda q, k: (q, 0, k, 0)),
+                  pl.BlockSpec((quarter // 2, width), lambda q, k: (2 * q + k, 0)),
+                  pl.BlockSpec(w_post.shape, lambda q, k: (0, 0))],
+        out_specs=pl.BlockSpec((quarter // 2, width), lambda q, k: (2 * q + k, 0)),
         scratch_shapes=[pltpu.VMEM((1, width), jnp.float32)],
         compiler_params=pltpu.CompilerParams(vmem_limit_bytes=62 * 1024 * 1024),
         name='finish',

time: 118 us -> 119 us (level)
    pallas_call x1, Pallas kernels: 5.54 us -> 7.27 us  [finish(): pl.pallas_call(finish_kernel, grid=(parts, 2), out_shape=jax.ShapeDtypeSt...]
where the time goes in v10:
time: 119 us
  Pallas kernels  114 us (96%)
  starting transfers between devices  3.01 us (3%)
    pallas_call x2, Pallas kernels, attend(): pl.pallas_call(functools.partial(attend_kernel, n_steps, rows // 4, first...  51.3 us
    pallas_call x1, Pallas kernels, merge(): pl.pallas_call(functools.partial(merge_kernel, chunks), out_shape=pltpu.H...  42.8 us
    pallas_call x1, Pallas kernels, project(): pl.pallas_call(project_kernel, out_shape=(pltpu.HBM((2, rows * q_cols //...  12.5 us
    pallas_call x1, Pallas kernels, finish(): pl.pallas_call(finish_kernel, grid=(parts, 2), out_shape=jax.ShapeDtypeSt...  7.27 us
    ppermute x3, starting transfers between devices, local_step(): moved.append(lax.ppermute(p, 'sp', [(i, i ^ d) for i in range(sp_size)]))  3.01 us
  transfers between devices with their start and end apart: 3, of which 0 were waited for; matrix products, arithmetic and copies ran while one was open for 0% of the time, Pallas kernels for 22%

profile of v10, /device:TPU:0, one launch (start us, length us, event | category | flops | bytes accessed | tf_op | source)
XLA Modules:
  0.0 118.6 jit_solution(214104725291064982)
XLA Ops:
  0.6 12.5 %project.1 = (f32[2,2048,128]{2,1,0:T(8,128)}, f32[2,1024,128]{2,1,0:T(8,128)}, f32[2,1024,128]{2,1,0:T(8,128)}) custom-call(s32[256]{0:T(256)} %pos_ref.5, bf16[256,4608]{1,0:T(8,128)(2,1)} %x_ref.1, f32[36,128]{1,0:T(8,128)} %bitcast.13, f32[256,256]{1,0:T(8,128)} %constant.8.clone.table_ref, bf16[4608,2048]{1,0:T(8,128)(2,1)} %wq_hbm.1, ...), custom_call_target="tpu_custom_call" | custom-call | flops 4831838208 | bytes 18874368 | tf_op jit(solution)/shard_map/project/pallas_call | solution.py:128
  13.2 25.7 %attend.2 = (bf16[256,512,128]{2,1,0:T(8,128)(2,1)}, bf16[256,512,128]{2,1,0:T(8,128)(2,1)}, f32[544,128]{1,0:T(8,128)}, f32[544,128]{1,0:T(8,128)}, f32[544,128]{1,0:T(8,128)}, /*index=5*/f32[544,128]{1,0:T(8,128)}) custom-call(s32[256]{0:T(256)} %pos_ref.5, s32[1]{0:T(128)} %bitcast.base_ref, f32[2,2048,128]{2,1,0:T(8,128)} %get-tuple-element.18.q_hbm, ...), custom_call_target="tpu_custom_call" | custom-call | flops 536870912 | bytes 67108864 | tf_op jit(solution)/shard_map/attend/pallas_call | solution.py:315
  38.8 0.2 collective-permute-start
  39.0 2.8 %collective-permute-start.1 = (f32[544,128]{1,0:T(8,128)}, f32[544,128]{1,0:T(8,128)S(1)}, u32[]{:S(2)}, u32[]{:S(2)}) collective-permute-start(f32[544,128]{1,0:T(8,128)} %get-tuple-element.23), channel_id=1, source_target_pairs={{0,2},{1,3},{2,0},{3,1},{4,6},{5,7},{6,4},{7,5}} | collective-permute-start | bytes 835592 | tf_op jit(solution)/shard_map/ppermute | solution.py:587
  41.9 0.0 collective-permute-start.2
  41.9 25.7 %attend.3 = (bf16[256,512,128]{2,1,0:T(8,128)(2,1)}, bf16[256,512,128]{2,1,0:T(8,128)(2,1)}, f32[544,128]{1,0:T(8,128)}, f32[544,128]{1,0:T(8,128)}, f32[544,128]{1,0:T(8,128)}, /*index=5*/f32[544,128]{1,0:T(8,128)}) custom-call(s32[256]{0:T(256)} %pos_ref.5, s32[1]{0:T(128)} %bitcast.base_ref, ...), custom_call_target="tpu_custom_call", output_to_operand_aliasing={{0}: (7, {}), {1}: (8, {})} | custom-call | flops 536870912 | bytes 67108864 | tf_op jit(solution)/shard_map/attend/pallas_call | solution.py:315
  67.5 0.0 collective-permute-done.refs_1_
  67.5 0.0 copy-start
  67.6 0.0 collective-permute-done.1.refs_2_
  67.6 0.0 copy-start.1
  67.6 0.0 collective-permute-done.2.refs_3_
  67.6 0.0 copy-start.2
  67.6 0.7 copy-done
  68.3 0.1 copy-done.1
  68.4 0.1 copy-done.2
  68.5 42.8 %merge.1.sums_ref = f32[4,9,64,512]{3,2,1,0:T(8,128)} custom-call(f32[544,128]{1,0:T(8,128)} %get-tuple-element.21.refs_0_, f32[544,128]{1,0:T(8,128)} %copy-done, f32[544,128]{1,0:T(8,128)} %copy-done.1, f32[544,128]{1,0:T(8,128)} %copy-done.2, f32[544,128]{1,0:T(8,128)} %get-tuple-element.27.refs_4_, f32[544,128]{1,0:T(8,128)} %get-tuple-element.28.refs_5_, ...), custom_call_target="tpu_custom_call" | custom-call | flops 1207959552 | bytes 18874368 | tf_op jit(solution)/shard_map/merge/pallas_call | solution.py:511
  111.3 7.3 %finish.1 = bf16[256,4608]{1,0:T(8,128)(2,1)} custom-call(f32[4,9,64,512]{3,2,1,0:T(8,128)} %merge.1.sums_ref, bf16[256,4608]{1,0:T(8,128)(2,1)} %x_ref.1, f32[36,128]{1,0:T(8,128)} %bitcast.14), custom_call_target="tpu_custom_call" | custom-call | tf_op jit(solution)/shard_map/finish/pallas_call | solution.py:553
Async XLA Ops:
  38.8 28.7 %collective-permute-start = (f32[544,128]{1,0:T(8,128)}, f32[544,128]{1,0:T(8,128)S(1)}, u32[]{:S(2)}, u32[]{:S(2)}) collective-permute-start(f32[544,128]{1,0:T(8,128)} %get-tuple-element.22), channel_id=1, source_target_pairs={{0,1},{1,0},{2,3},{3,2},{4,5},{5,4},{6,7},{7,6}} | collective-permute-start | bytes 835592 | tf_op jit(solution)/shard_map/ppermute | solution.py:587
  39.0 28.5 %collective-permute-start.1 = (f32[544,128]{1,0:T(8,128)}, f32[544,128]{1,0:T(8,128)S(1)}, u32[]{:S(2)}, u32[]{:S(2)}) collective-permute-start(f32[544,128]{1,0:T(8,128)} %get-tuple-element.23), channel_id=1, source_target_pairs={{0,2},{1,3},{2,0},{3,1},{4,6},{5,7},{6,4},{7,5}} | collective-permute-start | bytes 835592 | tf_op jit(solution)/shard_map/ppermute | solution.py:587
  41.9 25.7 %collective-permute-start.2 = (f32[544,128]{1,0:T(8,128)}, f32[544,128]{1,0:T(8,128)S(1)}, u32[]{:S(2)}, u32[]{:S(2)}) collective-permute-start(f32[544,128]{1,0:T(8,128)} %get-tuple-element.24), channel_id=1, source_target_pairs={{0,3},{1,2},{2,1},{3,0},{4,7},{5,6},{6,5},{7,4}} | collective-permute-start | bytes 835592 | tf_op jit(solution)/shard_map/ppermute | solution.py:587
  67.5 0.7 copy-start
  67.6 0.8 copy-start.1
  67.6 0.9 copy-start.2

commit v11 on v10

--- a/solution.py
+++ b/solution.py
@@ -370,11 +370,8 @@
         return pltpu.make_async_copy(wo_hbm.at[:, pl.ds(n * chunk, chunk)], wo.at[n], w_sem.at[n])
 
     local = [[pltpu.make_async_copy(source[c][d], pieces[c][d], p_sem.at[c, d]) for d in range(4)] for c in range(len(chunks))]
-    for group in (local[-1], local[0]):
-        for copy in group:
-            copy.start()
-    for n in range(2):
-        w_load(n).start()
+    for copy in local[-1]:
+        copy.start()
     barrier = pltpu.get_barrier_semaphore()
     for peer in (core_peer, x_peer, y_peer):
         pl.semaphore_signal(barrier, inc=1, device_id=peer, device_id_type=mesh_id)
@@ -387,6 +384,10 @@
             remote(last_out, last_in.at[2], o_send.at[2], o_recv.at[2], x_peer)]
     last[0].start()
     last[1].start()
+    for copy in local[0]:
+        copy.start()
+    for n in range(3):
+        w_load(n).start()
 
     def shares(blocks, part):
         count = part * heads
@@ -458,8 +459,8 @@
     for t in range(n_first):
         for n in order[t][2]:
             w_load(n).wait()
-            if n + 2 < n_chunks:
-                w_load(n + 2).start()
+            if n + 3 < n_chunks:
+                w_load(n + 3).start()
             project_rows(n, 0, parts[0])
         to_y(t).start()
 
@@ -530,35 +531,57 @@
     )(*flat, pltpu.with_memory_space_constraint(w_o, pltpu.HBM))
 
 
-def finish_kernel(sums_ref, x_ref, wpost_ref, out_ref, gain_ref):
-    _, n_chunks, rows, chunk = sums_ref.shape
+def finish_kernel(sums_hbm, x_hbm, wpost_ref, out_hbm, gain_ref, sums, xbuf, obuf, in_sem, out_sem):
+    parts, n_chunks, rows, chunk = sums.shape
+
+    def loads(q):
+        at = pl.ds(q * rows, rows)
+        return (pltpu.make_async_copy(sums_hbm.at[q], sums.at[q], in_sem.at[q, 0]),
+                pltpu.make_async_copy(x_hbm.at[at], xbuf.at[at], in_sem.at[q, 1]))
+
+    def store(q):
+        at = pl.ds(q * rows, rows)
+        return pltpu.make_async_copy(obuf.at[at], out_hbm.at[at], out_sem.at[q])
+
+    for q in range(2):
+        for copy in loads(q):
+            copy.start()
     for j in range(wpost_ref.shape[0]):
         gain_ref[:, j * 128:(j + 1) * 128] = 1.0 + wpost_ref[j:j + 1, :]
-    for k in range(rows // 16):
-        at = slice(k * 16, (k + 1) * 16)
-        square = jnp.zeros((16, chunk), jnp.float32)
-        for n in range(n_chunks):
-            u = sums_ref[0, n, at, :]
-            square = square + u * u
-        inv = lax.rsqrt(jnp.sum(square, axis=-1, keepdims=True) * (1.0 / (n_chunks * chunk)) + NORM_EPS)
-        for n in range(n_chunks):
-            col = slice(n * chunk, (n + 1) * chunk)
-            y = x_ref[at, col].astype(jnp.float32) + sums_ref[0, n, at, :] * inv * gain_ref[:, col]
-            out_ref[at, col] = y.astype(jnp.bfloat16)
+    for q in range(parts):
+        for copy in loads(q):
+            copy.wait()
+        if q + 2 < parts:
+            for copy in loads(q + 2):
+                copy.start()
+        for k in range(rows // 16):
+            at = slice(k * 16, (k + 1) * 16)
+            to = slice(q * rows + k * 16, q * rows + (k + 1) * 16)
+            square = jnp.zeros((16, chunk), jnp.float32)
+            for n in range(n_chunks):
+                u = sums[q, n, at, :]
+                square = square + u * u
+            inv = lax.rsqrt(jnp.sum(square, axis=-1, keepdims=True) * (1.0 / (n_chunks * chunk)) + NORM_EPS)
+            for n in range(n_chunks):
+                col = slice(n * chunk, (n + 1) * chunk)
+                y = xbuf[to, col].astype(jnp.float32) + sums[q, n, at, :] * inv * gain_ref[:, col]
+                obuf[to, col] = y.astype(jnp.bfloat16)
+        store(q).start()
+    for q in range(parts):
+        store(q).wait()
 
 
 def finish(sums, x_in, w_post):
-    parts, n_chunks, quarter, chunk = sums.shape
-    width = n_chunks * chunk
+    parts = sums.shape[0]
+    hbm = pl.BlockSpec(memory_space=pltpu.HBM)
+    dma = pltpu.SemaphoreType.DMA
     return pl.pallas_call(
         finish_kernel,
-        grid=(parts, 2),
         out_shape=jax.ShapeDtypeStruct(x_in.shape, x_in.dtype),
-        in_specs=[pl.BlockSpec((1, n_chunks, quarter // 2, chunk), lambda q, k: (q, 0, k, 0)),
-                  pl.BlockSpec((quarter // 2, width), lambda q, k: (2 * q + k, 0)),
-                  pl.BlockSpec(w_post.shape, lambda q, k: (0, 0))],
-        out_specs=pl.BlockSpec((quarter // 2, width), lambda q, k: (2 * q + k, 0)),
-        scratch_shapes=[pltpu.VMEM((1, width), jnp.float32)],
+        in_specs=[hbm, hbm, pl.BlockSpec(memory_space=pltpu.VMEM)],
+        out_specs=hbm,
+        scratch_shapes=[pltpu.VMEM((1, x_in.shape[1]), jnp.float32), pltpu.VMEM(sums.shape, jnp.float32),
+                        pltpu.VMEM(x_in.shape, x_in.dtype), pltpu.VMEM(x_in.shape, x_in.dtype), dma((parts, 2)), dma((parts,))],
         compiler_params=pltpu.CompilerParams(vmem_limit_bytes=62 * 1024 * 1024),
         name='finish',
     )(sums, x_in, w_post)

time: 119 us -> 117 us (0.983)
  Pallas kernels: 114 us -> 112 us
    pallas_call x1, Pallas kernels: 7.27 us -> 5.78 us  [finish(): pl.pallas_call(finish_kernel, out_shape=jax.ShapeDtypeStruct(x_in.shape,...]
where the time goes in v11:
time: 117 us
  Pallas kernels  112 us (96%)
  starting transfers between devices  3.01 us (3%)
    pallas_call x2, Pallas kernels, attend(): pl.pallas_call(functools.partial(attend_kernel, n_steps, rows // 4, first...  51.3 us
    pallas_call x1, Pallas kernels, merge(): pl.pallas_call(functools.partial(merge_kernel, chunks), out_shape=pltpu.H...  42.2 us
    pallas_call x1, Pallas kernels, project(): pl.pallas_call(project_kernel, out_shape=(pltpu.HBM((2, rows * q_cols //...  12.5 us
    pallas_call x1, Pallas kernels, finish(): pl.pallas_call(finish_kernel, out_shape=jax.ShapeDtypeStruct(x_in.shape,...  5.78 us
    ppermute x3, starting transfers between devices, local_step(): moved.append(lax.ppermute(p, 'sp', [(i, i ^ d) for i in range(sp_size)]))  3.01 us
  transfers between devices with their start and end apart: 3, of which 0 were waited for; matrix products, arithmetic and copies ran while one was open for 0% of the time, Pallas kernels for 22%

profile of v11, /device:TPU:0, one launch (start us, length us, event | category | flops | bytes accessed | tf_op | source)
XLA Modules:
  0.0 116.6 jit_solution(8653492088235210875)
XLA Ops:
  0.6 12.5 %project.1 = (f32[2,2048,128]{2,1,0:T(8,128)}, f32[2,1024,128]{2,1,0:T(8,128)}, f32[2,1024,128]{2,1,0:T(8,128)}) custom-call(s32[256]{0:T(256)} %pos_ref.5, bf16[256,4608]{1,0:T(8,128)(2,1)} %x_hbm.3, f32[36,128]{1,0:T(8,128)} %bitcast.13, f32[256,256]{1,0:T(8,128)} %constant.8.clone.table_ref, bf16[4608,2048]{1,0:T(8,128)(2,1)} %wq_hbm.1, ...), custom_call_target="tpu_custom_call" | custom-call | flops 4831838208 | bytes 18874368 | tf_op jit(solution)/shard_map/project/pallas_call | solution.py:128
  13.2 25.7 %attend.2 = (bf16[256,512,128]{2,1,0:T(8,128)(2,1)}, bf16[256,512,128]{2,1,0:T(8,128)(2,1)}, f32[544,128]{1,0:T(8,128)}, f32[544,128]{1,0:T(8,128)}, f32[544,128]{1,0:T(8,128)}, /*index=5*/f32[544,128]{1,0:T(8,128)}) custom-call(s32[256]{0:T(256)} %pos_ref.5, s32[1]{0:T(128)} %bitcast.base_ref, f32[2,2048,128]{2,1,0:T(8,128)} %get-tuple-element.18.q_hbm, ...), custom_call_target="tpu_custom_call" | custom-call | flops 536870912 | bytes 67108864 | tf_op jit(solution)/shard_map/attend/pallas_call | solution.py:315
  38.8 0.2 collective-permute-start
  39.0 2.8 %collective-permute-start.1 = (f32[544,128]{1,0:T(8,128)}, f32[544,128]{1,0:T(8,128)S(1)}, u32[]{:S(2)}, u32[]{:S(2)}) collective-permute-start(f32[544,128]{1,0:T(8,128)} %get-tuple-element.23), channel_id=1, source_target_pairs={{0,2},{1,3},{2,0},{3,1},{4,6},{5,7},{6,4},{7,5}} | collective-permute-start | bytes 835592 | tf_op jit(solution)/shard_map/ppermute | solution.py:610
  41.9 0.0 collective-permute-start.2
  41.9 25.7 %attend.3 = (bf16[256,512,128]{2,1,0:T(8,128)(2,1)}, bf16[256,512,128]{2,1,0:T(8,128)(2,1)}, f32[544,128]{1,0:T(8,128)}, f32[544,128]{1,0:T(8,128)}, f32[544,128]{1,0:T(8,128)}, /*index=5*/f32[544,128]{1,0:T(8,128)}) custom-call(s32[256]{0:T(256)} %pos_ref.5, s32[1]{0:T(128)} %bitcast.base_ref, ...), custom_call_target="tpu_custom_call", output_to_operand_aliasing={{0}: (7, {}), {1}: (8, {})} | custom-call | flops 536870912 | bytes 67108864 | tf_op jit(solution)/shard_map/attend/pallas_call | solution.py:315
  67.5 0.0 collective-permute-done.refs_1_
  67.5 0.0 copy-start
  67.6 0.0 collective-permute-done.1.refs_2_
  67.6 0.0 copy-start.1
  67.6 0.0 collective-permute-done.2.refs_3_
  67.6 0.0 copy-start.2
  67.6 0.7 copy-done
  68.3 0.1 copy-done.1
  68.4 0.1 copy-done.2
  68.5 42.2 %merge.1.sums_hbm = f32[4,9,64,512]{3,2,1,0:T(8,128)} custom-call(f32[544,128]{1,0:T(8,128)} %get-tuple-element.21.refs_0_, f32[544,128]{1,0:T(8,128)} %copy-done, f32[544,128]{1,0:T(8,128)} %copy-done.1, f32[544,128]{1,0:T(8,128)} %copy-done.2, f32[544,128]{1,0:T(8,128)} %get-tuple-element.27.refs_4_, f32[544,128]{1,0:T(8,128)} %get-tuple-element.28.refs_5_, ...), custom_call_target="tpu_custom_call" | custom-call | flops 1207959552 | bytes 18874368 | tf_op jit(solution)/shard_map/merge/pallas_call | solution.py:512
  110.7 5.8 %finish.1 = bf16[256,4608]{1,0:T(8,128)(2,1)} custom-call(f32[4,9,64,512]{3,2,1,0:T(8,128)} %merge.1.sums_hbm, bf16[256,4608]{1,0:T(8,128)(2,1)} %x_hbm.3, f32[36,128]{1,0:T(8,128)} %bitcast.14), custom_call_target="tpu_custom_call" | custom-call | tf_op jit(solution)/shard_map/finish/pallas_call | solution.py:578
Async XLA Ops:
  38.8 28.7 %collective-permute-start = (f32[544,128]{1,0:T(8,128)}, f32[544,128]{1,0:T(8,128)S(1)}, u32[]{:S(2)}, u32[]{:S(2)}) collective-permute-start(f32[544,128]{1,0:T(8,128)} %get-tuple-element.22), channel_id=1, source_target_pairs={{0,1},{1,0},{2,3},{3,2},{4,5},{5,4},{6,7},{7,6}} | collective-permute-start | bytes 835592 | tf_op jit(solution)/shard_map/ppermute | solution.py:610
  39.0 28.5 %collective-permute-start.1 = (f32[544,128]{1,0:T(8,128)}, f32[544,128]{1,0:T(8,128)S(1)}, u32[]{:S(2)}, u32[]{:S(2)}) collective-permute-start(f32[544,128]{1,0:T(8,128)} %get-tuple-element.23), channel_id=1, source_target_pairs={{0,2},{1,3},{2,0},{3,1},{4,6},{5,7},{6,4},{7,5}} | collective-permute-start | bytes 835592 | tf_op jit(solution)/shard_map/ppermute | solution.py:610
  41.9 25.7 %collective-permute-start.2 = (f32[544,128]{1,0:T(8,128)}, f32[544,128]{1,0:T(8,128)S(1)}, u32[]{:S(2)}, u32[]{:S(2)}) collective-permute-start(f32[544,128]{1,0:T(8,128)} %get-tuple-element.24), channel_id=1, source_target_pairs={{0,3},{1,2},{2,1},{3,0},{4,7},{5,6},{6,5},{7,4}} | collective-permute-start | bytes 835592 | tf_op jit(solution)/shard_map/ppermute | solution.py:610
  67.5 0.7 copy-start
  67.6 0.8 copy-start.1
  67.6 0.9 copy-start.2

commit v12 on v11

--- a/solution.py
+++ b/solution.py
@@ -7,7 +7,6 @@
 from jax.experimental import pallas as pl
 from jax.experimental.pallas import tpu as pltpu
 from jax.sharding import PartitionSpec as P
-
 
 SOFT_CAP = 50.0
 ROPE_BASE = 10000.0
@@ -149,12 +148,13 @@
     )(cur_pos, x_in, w_pre, table, w_q, w_k, w_v)
 
 
-def attend_kernel(n_steps, quarter, first_row, kv_heads, seq_block, pos_ref, base_ref, q_hbm, kn_hbm, vn_hbm, k_hbm, v_hbm,
+def attend_kernel(n_steps, quarter, n_groups, kv_heads, seq_block, pos_ref, base_ref, q_hbm, kn_hbm, vn_hbm, k_hbm, v_hbm,
                   *rest):
     (ko_hbm, vo_hbm, o0_hbm, o1_hbm, o2_hbm, o3_hbm, m_ref, l_ref, kbuf, vbuf, qbuf, knbuf, vnbuf, obuf, key_ref, s_ref, p_ref, in_sem, out_sem, o_sem, st_sem) = rest[-21:]
     step_rows = ROWS_STEP
-    piece_steps = n_steps // 4
-    heads, head_dim = m_ref.shape
+    group_steps = n_steps // n_groups
+    piece_steps = group_steps // 4
+    _, heads, head_dim = m_ref.shape
     q_half, kv_half = heads // 2, kv_heads // 2
     cols = seq_block * kv_heads
     base = base_ref[0]
@@ -163,12 +163,18 @@
     col_id = lax.broadcasted_iota(jnp.int32, (heads, cols), 1)
     mine = lax.rem(col_id, kv_heads) == row_id // (heads // kv_heads)
     key_ref[...] = jnp.where(mine, col_id, cols * 4)
-    lane_id = lax.broadcasted_iota(jnp.int32, m_ref.shape, 1)
+    lane_id = lax.broadcasted_iota(jnp.int32, m_ref.shape[1:], 1)
     half_id = lax.broadcasted_iota(jnp.int32, (2 * kv_heads, head_dim), 0) // kv_heads
 
+    def split_of(step):
+        group = step // group_steps
+        inner = step - group * group_steps
+        piece = inner // piece_steps
+        return group, inner, piece, inner - piece * piece_steps
+
     def row_of(step):
-        piece = step // piece_steps
-        return piece * quarter + first_row + (step - piece * piece_steps) * step_rows
+        group, _, piece, turn = split_of(step)
+        return piece * quarter + (group * piece_steps + turn) * step_rows
 
     def heads_of(step, count):
         return pl.ds(row_of(step) * count, step_rows * count)
@@ -191,12 +197,13 @@
                 pltpu.make_async_copy(vbuf.at[slot], vo_hbm.at[rows], out_sem.at[slot, 1]))
 
     def o_store(step, slot, d=0):
-        at = pl.ds((step - step // piece_steps * piece_steps) * step_rows * heads, step_rows * heads)
+        group, _, _, turn = split_of(step)
+        at = pl.ds(turn * step_rows * heads, step_rows * heads)
         o_hbm = (o0_hbm, o1_hbm, o2_hbm, o3_hbm)[d]
-        return pltpu.make_async_copy(obuf.at[slot], o_hbm.at[at], o_sem.at[slot])
+        return pltpu.make_async_copy(obuf.at[slot], o_hbm.at[group, at], o_sem.at[slot])
 
     def o_start(step, slot):
-        turn = jnp.bitwise_xor(step // piece_steps, base // seq_block)
+        turn = jnp.bitwise_xor(split_of(step)[2], base // seq_block)
         for d in range(4):
             @pl.when(turn == d)
             def _():
@@ -227,7 +234,6 @@
                 def _():
                     for copy in stores(nxt - SLOTS, nslot):
                         copy.wait()
-
                 for copy in loads(nxt, nslot):
                     copy.start()
 
@@ -246,8 +252,9 @@
         def _():
             o_store(step - 2, oslot).wait()
 
-        m_all = m_ref[...]
-        l_all = l_ref[...]
+        group, inner, _, _ = split_of(step)
+        m_all = m_ref[group]
+        l_all = l_ref[group]
         half = cols // 2
         for tick in range(step_rows + LAG_OUT):
             r = tick
@@ -267,7 +274,7 @@
                 weight = weight.astype(jnp.bfloat16)
                 p_ref[r, :heads] = weight[:, :half]
                 p_ref[r, heads:] = weight[:, half:]
-                here = lane_id == step * step_rows + r
+                here = lane_id == inner * step_rows + r
                 m_all = jnp.where(here, top * SOFT_CAP, m_all)
                 l_all = jnp.where(here, total, l_all)
             r = tick - LAG_OUT
@@ -275,8 +282,8 @@
                 right = jnp.concatenate([vbuf[slot, r, :half, :], vbuf[slot, r, half:, :]], axis=1)
                 both = jnp.dot(p_ref[r], right, preferred_element_type=jnp.float32)
                 obuf[oslot, r * heads:(r + 1) * heads, :] = both[:heads, :head_dim] + both[heads:, head_dim:]
-        m_ref[...] = m_all
-        l_ref[...] = l_all
+        m_ref[group] = m_all
+        l_ref[group] = l_all
         o_start(step, oslot)
         for copy in stores(step, slot):
             copy.start()
@@ -287,8 +294,8 @@
     tail = piece_steps * step_rows * heads
     stat_copies = []
     for d, o_hbm in enumerate((o0_hbm, o1_hbm, o2_hbm, o3_hbm)):
-        stat_copies.append(pltpu.make_async_copy(m_ref, o_hbm.at[pl.ds(tail, heads)], st_sem.at[d, 0]))
-        stat_copies.append(pltpu.make_async_copy(l_ref, o_hbm.at[pl.ds(tail + heads, heads)], st_sem.at[d, 1]))
+        stat_copies.append(pltpu.make_async_copy(m_ref, o_hbm.at[:, pl.ds(tail, heads)], st_sem.at[d, 0]))
+        stat_copies.append(pltpu.make_async_copy(l_ref, o_hbm.at[:, pl.ds(tail + heads, heads)], st_sem.at[d, 1]))
     for copy in stat_copies:
         copy.start()
     for copy in stat_copies:
@@ -300,26 +307,24 @@
         o_store(step, step % 2).wait()
 
 
-def attend(pos, base, q, kn, vn, k_cache, v_cache, prev, first_row, n_rows):
+def attend(pos, base, q, kn, vn, k_cache, v_cache, n_groups):
     rows, cols, head_dim = k_cache.shape
     heads = 2 * q.shape[1] // rows
     kv_heads = 2 * kn.shape[1] // rows
     seq_block = cols // kv_heads
-    n_steps = n_rows // ROWS_STEP
+    n_steps = rows // ROWS_STEP
     hbm = pl.BlockSpec(memory_space=pl.ANY)
-    piece = pltpu.HBM((n_rows // 4 * heads + 2 * heads, head_dim), jnp.float32)
+    piece = pltpu.HBM((n_groups, rows // (4 * n_groups) * heads + 2 * heads, head_dim), jnp.float32)
     smem = pl.BlockSpec(memory_space=pltpu.SMEM)
     bf = jnp.bfloat16
-    aliases = {} if prev is None else {7: 0, 8: 1}
-    extra = () if prev is None else tuple(prev)
     return pl.pallas_call(
-        functools.partial(attend_kernel, n_steps, rows // 4, first_row, kv_heads, seq_block),
+        functools.partial(attend_kernel, n_steps, rows // 4, n_groups, kv_heads, seq_block),
         out_shape=(jax.ShapeDtypeStruct(k_cache.shape, bf), jax.ShapeDtypeStruct(v_cache.shape, bf)) + (piece,) * 4,
-        in_specs=[smem, smem, hbm, hbm, hbm, hbm, hbm] + [hbm] * len(extra),
+        in_specs=[smem, smem, hbm, hbm, hbm, hbm, hbm],
         out_specs=(hbm, hbm) + (pl.BlockSpec(memory_space=pltpu.HBM),) * 4,
         scratch_shapes=[
-            pltpu.VMEM((heads, 128), jnp.float32),
-            pltpu.VMEM((heads, 128), jnp.float32),
+            pltpu.VMEM((n_groups, heads, 128), jnp.float32),
+            pltpu.VMEM((n_groups, heads, 128), jnp.float32),
             pltpu.VMEM((SLOTS, ROWS_STEP, cols, head_dim), bf),
             pltpu.VMEM((SLOTS, ROWS_STEP, cols, head_dim), bf),
             pltpu.VMEM((SLOTS, 2, ROWS_STEP * heads // 2, head_dim), jnp.float32),
@@ -334,28 +339,24 @@
             pltpu.SemaphoreType.DMA((2,)),
             pltpu.SemaphoreType.DMA((4, 2)),
         ],
-        input_output_aliases=aliases,
         compiler_params=pltpu.CompilerParams(vmem_limit_bytes=62 * 1024 * 1024),
-        cost_estimate=pl.CostEstimate(flops=n_rows * heads * cols * head_dim * 4,
-                                      bytes_accessed=n_rows * cols * head_dim * 8, transcendentals=0),
+        cost_estimate=pl.CostEstimate(flops=rows * heads * cols * head_dim * 4,
+                                      bytes_accessed=rows * cols * head_dim * 8, transcendentals=0),
         name='attend',
-    )(pos, base, q, kn, vn, k_cache, v_cache, *extra)
-
-
-def merge_kernel(chunks, *refs):
-    n_in = 4 * len(chunks)
-    source = [refs[4 * c:4 * c + 4] for c in range(len(chunks))]
-    pieces = [[b.at[d] for d in range(4)] for b in refs[-len(chunks):]]
-    refs = refs[:-len(chunks)]
-    (wo_hbm, out_hbm, wo, last_in, last_out, osum, lhs, y_out, y_in, sums,
-     p_sem, w_sem, o_send, o_recv, y_send, y_recv, g_send, g_recv, d_send, d_recv, f_send, f_recv, out_sem) = refs[n_in:]
+    )(pos, base, q, kn, vn, k_cache, v_cache)
+
+
+def merge_kernel(b0, b1, b2, b3, wo_hbm, out_hbm, wo, mine, near, pair_in, x_in, pair_out, osum, lhs, y_out, y_in, sums,
+                 p_sem, w_sem, o_send, o_recv, y_send, y_recv, g_send, g_recv, d_send, d_recv, f_send, f_recv, out_sem):
     sp = lax.axis_index('sp')
     tp = lax.axis_index('tp')
     core = lax.rem(sp, 2)
     xpos = sp // 2
-    n_chunks, _, chunk = y_out.shape
+    n_chunks, quarter, chunk = y_out.shape
     heads = lhs.shape[1] // 128
-    parts = [c // 4 for c in chunks]
+    n_groups = mine.shape[1]
+    part = quarter // n_groups
+    count = part * heads
     core_id = 2 * xpos + (1 - core)
     x_id = 2 * (1 - xpos) + core
     far_id = 2 * (1 - xpos) + (1 - core)
@@ -369,75 +370,77 @@
     def w_load(n):
         return pltpu.make_async_copy(wo_hbm.at[:, pl.ds(n * chunk, chunk)], wo.at[n], w_sem.at[n])
 
-    local = [[pltpu.make_async_copy(source[c][d], pieces[c][d], p_sem.at[c, d]) for d in range(4)] for c in range(len(chunks))]
-    for copy in local[-1]:
-        copy.start()
+    local = [pltpu.make_async_copy(b, mine.at[d], p_sem.at[d]) for d, b in enumerate((b0, b1, b2, b3))]
+    local[3].start()
+    local[2].start()
     barrier = pltpu.get_barrier_semaphore()
     for peer in (core_peer, x_peer, y_peer):
         pl.semaphore_signal(barrier, inc=1, device_id=peer, device_id_type=mesh_id)
     pl.semaphore_wait(barrier, 3)
 
-    for copy in local[-1]:
-        copy.wait()
-    last = [remote(pieces[-1][3], last_in.at[0], o_send.at[0], o_recv.at[0], core_peer),
-            remote(pieces[-1][1], last_in.at[1], o_send.at[1], o_recv.at[1], core_peer),
-            remote(last_out, last_in.at[2], o_send.at[2], o_recv.at[2], x_peer)]
-    last[0].start()
-    last[1].start()
-    for copy in local[0]:
+    far = [remote(mine.at[3, c], pair_in.at[c], o_send.at[0, c], o_recv.at[0, c], core_peer) for c in range(n_groups)]
+    to_near = [remote(mine.at[1, c], near.at[c], o_send.at[1, c], o_recv.at[1, c], core_peer) for c in range(n_groups)]
+    over_x = [remote(pair_out.at[c], x_in.at[c], o_send.at[2, c], o_recv.at[2, c], x_peer) for c in range(n_groups)]
+    local[3].wait()
+    for copy in far:
         copy.start()
+    local[1].start()
+    local[0].start()
     for n in range(3):
         w_load(n).start()
 
-    def shares(blocks, part):
-        count = part * heads
+    def shares(blocks):
         stats = [block[count:count + 2 * heads, :] for block in blocks]
         top = functools.reduce(jnp.maximum, [st[:heads] for st in stats])
         grown = [jnp.exp(st[:heads] - top) for st in stats]
         return top, sum(st[heads:] * g for st, g in zip(stats, grown)), grown
 
-    def mix(blocks, weights, owner, part, out):
+    def mix(blocks, weights, owner, out):
         shift = lax.rem(128 - owner * part, 128)
         factors = [pltpu.roll(w, shift, 1) for w in weights]
         for b in range(part):
             at = slice(b * heads, (b + 1) * heads)
             out[at, :] = sum(block[at, :] * f[:, b:b + 1] for block, f in zip(blocks, factors))
 
-    def combine(blocks, part, row0):
-        _, total, grown = shares(blocks, part)
-        mix(blocks, [g / total for g in grown], sp, part, osum)
+    local[2].wait()
+    for c in range(n_groups):
+        far[c].wait_recv()
+        pair = [mine.at[2, c], pair_in.at[c]]
+        top, total, grown = shares(pair)
+        mix(pair, grown, x_id, pair_out.at[c])
+        pair_out[c, count:count + heads, :] = top
+        pair_out[c, count + heads:count + 2 * heads, :] = total
+        over_x[c].start()
+        if c == 0:
+            local[1].wait()
+            for copy in to_near:
+                copy.start()
+    local[0].wait()
+
+    def combine(c):
+        to_near[c].wait_recv()
+        over_x[c].wait_recv()
+        blocks = [mine.at[0, c], near.at[c], x_in.at[c]]
+        _, total, grown = shares(blocks)
+        mix(blocks, [g / total for g in grown], sp, osum)
         for h in range(heads):
-            lhs[row0:row0 + part, h * 128:(h + 1) * 128] = osum[pl.ds(h, part, stride=heads), :].astype(jnp.bfloat16)
-
-    last[0].wait_recv()
-    pair = [pieces[-1][2], last_in.at[0]]
-    top, total, grown = shares(pair, parts[-1])
-    mix(pair, grown, x_id, parts[-1], last_out)
-    count = parts[-1] * heads
-    last_out[count:count + heads, :] = top
-    last_out[count + heads:count + 2 * heads, :] = total
-    last[2].start()
-
-    for copy in local[0]:
-        copy.wait()
-    combine(pieces[0], parts[0], 0)
-
-    sizes = (2, 2, 2, 2, 1)
-    order = []
-    for c, part in enumerate(parts):
-        begin = 0
-        for size in sizes:
-            order.append((pl.ds(begin, size), pl.ds(sum(parts[:c]), part), range(begin, begin + size)))
-            begin += size
+            lhs[c * part:(c + 1) * part, h * 128:(h + 1) * 128] = osum[pl.ds(h, part, stride=heads), :].astype(jnp.bfloat16)
+
+    wide = 3
+    order = [(c, n) for c in range(n_groups) for n in range(0, n_chunks, wide)]
     n_pieces = len(order)
-    n_first = len(sizes)
+    per = n_chunks // wide
+
+    def where(t):
+        c, n = order[t]
+        return pl.ds(n, wide), pl.ds(c * part, part)
 
     def to_y(t):
-        ns, r, _ = order[t]
+        ns, r = where(t)
         return remote(y_out.at[ns, r], y_in.at[ns, r], y_send.at[t], y_recv.at[t], y_peer)
 
     def gather(t, owner, send, recv, peer):
-        ns, r, _ = order[t]
+        ns, r = where(t)
         return remote(sums.at[owner, ns, r], sums.at[owner, ns, r], send.at[t], recv.at[t], peer)
 
     def to_x(t):
@@ -450,31 +453,33 @@
         return gather(t, x_id, f_send, f_recv, core_peer)
 
     def keep(t, turn, owner):
-        ns, r, _ = order[t]
+        ns, r = where(t)
         return pltpu.make_async_copy(sums.at[owner, ns, r], out_hbm.at[owner, ns, r], out_sem.at[turn, t])
 
-    def project_rows(n, r0, count):
-        y_out[n, r0:r0 + count, :] = jnp.dot(lhs[r0:r0 + count, :], wo[n], preferred_element_type=jnp.float32)
-
-    for t in range(n_first):
-        for n in order[t][2]:
-            w_load(n).wait()
-            if n + 3 < n_chunks:
-                w_load(n + 3).start()
-            project_rows(n, 0, parts[0])
+    def project(t):
+        c, first = order[t]
+        at = slice(c * part, (c + 1) * part)
+        for n in range(first, first + wide):
+            if c == 0:
+                w_load(n).wait()
+                if n + 3 < n_chunks:
+                    w_load(n + 3).start()
+            y_out[n, at, :] = jnp.dot(lhs[at, :], wo[n], preferred_element_type=jnp.float32)
         to_y(t).start()
 
+    combine(0)
+    for t in range(per):
+        project(t)
+    ahead = per
     for t in range(n_pieces + 3):
-        if t == 2:
-            for copy in last[1:]:
-                copy.wait_recv()
-            combine([pieces[-1][0], last_in.at[1], last_in.at[2]], parts[-1], parts[0])
-        if 2 <= t < 2 + n_first:
-            for n in order[n_first + t - 2][2]:
-                project_rows(n, parts[0], parts[-1])
-            to_y(n_first + t - 2).start()
+        for _ in range(2 if t < per else 1):
+            if t >= 0 and ahead < n_pieces:
+                if ahead % per == 0:
+                    combine(ahead // per)
+                project(ahead)
+                ahead += 1
         if t < n_pieces:
-            ns, r, _ = order[t]
+            ns, r = where(t)
             to_y(t).wait()
             sums[sp, ns, r, :] = y_out[ns, r, :] + y_in[ns, r, :]
             to_x(t).start()
@@ -489,7 +494,7 @@
             keep(t - 3, 2, core_id).start()
             relay(t - 3).wait_recv()
             keep(t - 3, 3, far_id).start()
-    for copy in last:
+    for copy in far + to_near + over_x:
         copy.wait_send()
     for t in range(n_pieces):
         to_x(t).wait_send()
@@ -499,36 +504,37 @@
             keep(t, turn, sp).wait()
 
 
-def merge(chunks, pieces, w_o, n_chunks):
+def merge(blocks, w_o, n_chunks):
     inner, width = w_o.shape
-    heads = inner // 128
-    quarter = sum(chunks) // 4
+    n_groups, height, head_dim = blocks[0].shape
+    heads = inner // head_dim
+    quarter = n_groups * (height // heads - 2)
     chunk = width // n_chunks
     hbm = pl.BlockSpec(memory_space=pltpu.HBM)
     f32 = jnp.float32
     dma = pltpu.SemaphoreType.DMA
-    flat = [p for piece in pieces for p in piece]
-    block = pieces[-1][0].shape
+    n_pieces = n_groups * n_chunks // 3
+    block = pltpu.VMEM((n_groups, height, head_dim), f32)
     return pl.pallas_call(
-        functools.partial(merge_kernel, chunks),
+        merge_kernel,
         out_shape=pltpu.HBM((4, n_chunks, quarter, chunk), f32),
-        in_specs=[hbm] * (len(flat) + 1),
+        in_specs=[hbm] * 5,
         out_specs=hbm,
         scratch_shapes=[
             pltpu.VMEM((n_chunks, inner, chunk), jnp.bfloat16),
-            pltpu.VMEM((3,) + block, f32),
-            pltpu.VMEM(block, f32),
-            pltpu.VMEM((max(chunks) // 4 * heads, 128), f32),
+            pltpu.VMEM((4, n_groups, height, head_dim), f32),
+            block, block, block, block,
+            pltpu.VMEM((height, head_dim), f32),
             pltpu.VMEM((quarter, inner), jnp.bfloat16),
             pltpu.VMEM((n_chunks, quarter, chunk), f32),
             pltpu.VMEM((n_chunks, quarter, chunk), f32),
             pltpu.VMEM((4, n_chunks, quarter, chunk), f32),
-            dma((len(chunks), 4)), dma((n_chunks,)), dma((3,)), dma((3,)),
-        ] + [dma((10,))] * 8 + [dma((4, 10))] + [pltpu.VMEM((4,) + piece[0].shape, f32) for piece in pieces],
+            dma((4,)), dma((n_chunks,)), dma((3, n_groups)), dma((3, n_groups)),
+        ] + [dma((n_pieces,))] * 8 + [dma((4, n_pieces))],
         compiler_params=pltpu.CompilerParams(vmem_limit_bytes=56 * 1024 * 1024, collective_id=0, has_side_effects=True),
         cost_estimate=pl.CostEstimate(flops=2 * quarter * inner * width, bytes_accessed=2 * inner * width, transcendentals=0),
         name='merge',
-    )(*flat, pltpu.with_memory_space_constraint(w_o, pltpu.HBM))
+    )(*blocks, pltpu.with_memory_space_constraint(w_o, pltpu.HBM))
 
 
 def finish_kernel(sums_hbm, x_hbm, wpost_ref, out_hbm, gain_ref, sums, xbuf, obuf, in_sem, out_sem):
@@ -599,19 +605,8 @@
         base = (sp_index * seq_block).astype(jnp.int32).reshape(1)
         kc = k_cache.reshape(row_count, seq_block * kv_local, head_dim)
         vc = v_cache.reshape(row_count, seq_block * kv_local, head_dim)
-        chunks = (row_count // 2, row_count // 2)
-        prev, first_row, pieces = None, 0, []
-        for index, n_rows in enumerate(chunks):
-            *prev, p0, p1, p2, p3 = attend(cur_pos, base, q_rot, kn2, vn2, kc, vc, prev, first_row, n_rows)
-            first_row += n_rows // 4
-            if index < len(chunks) - 1:
-                moved = []
-                for d, p in ((1, p1), (2, p2), (3, p3)):
-                    moved.append(lax.ppermute(p, 'sp', [(i, i ^ d) for i in range(sp_size)]))
-                p1, p2, p3 = moved
-            pieces.append((p0, p1, p2, p3))
-        k_out, v_out = prev
-        x_out = finish(merge(chunks, pieces, w_o, 9), x_in, w_post.reshape(-1, 128))
+        k_out, v_out, *blocks = attend(cur_pos, base, q_rot, kn2, vn2, kc, vc, 4)
+        x_out = finish(merge(blocks, w_o, 9), x_in, w_post.reshape(-1, 128))
         return x_out, k_out.reshape(k_cache.shape), v_out.reshape(v_cache.shape)
 
     return jax.shard_map(local_step, mesh=mesh,

time: 117 us -> 118 us (level)
  Pallas kernels: 112 us -> 117 us
  starting transfers between devices: 3.01 us -> 0 us
    pallas_call x3 -> x2, Pallas kernels: 93.5 us -> 99 us  [the longest x1 50.4 us: merge(): pl.pallas_call(merge_kernel, out_shape=pltpu.HBM((4, n_chunks, quarter, c...]
    ppermute x3 -> x0, starting transfers between devices: 3.01 us -> none  [local_step(): moved.append(lax.ppermute(p, 'sp', [(i, i ^ d) for i in range(sp_size)]))]
  transfers between devices with their start and end apart: 3 -> 0, of which waited for: 0 -> 0; matrix products, arithmetic and copies ran while one was open for 0% -> 0% of each run, Pallas kernels for 22% -> 0%
where the time goes in v12:
time: 118 us
  Pallas kernels  117 us (99%)
    pallas_call x1, Pallas kernels, merge(): pl.pallas_call(merge_kernel, out_shape=pltpu.HBM((4, n_chunks, quarter, c...  50.4 us
    pallas_call x1, Pallas kernels, attend(): pl.pallas_call(functools.partial(attend_kernel, n_steps, rows // 4, n_gro...  48.6 us
    pallas_call x1, Pallas kernels, project(): pl.pallas_call(project_kernel, out_shape=(pltpu.HBM((2, rows * q_cols //...  12.4 us
    pallas_call x1, Pallas kernels, finish(): pl.pallas_call(finish_kernel, out_shape=jax.ShapeDtypeStruct(x_in.shape,...  5.78 us

profile of v12, /device:TPU:0, one launch (start us, length us, event | category | flops | bytes accessed | tf_op | source)
XLA Modules:
  0.0 118.0 jit_solution(2654880438503062358)
XLA Ops:
  0.6 12.4 %project.1 = (f32[2,2048,128]{2,1,0:T(8,128)}, f32[2,1024,128]{2,1,0:T(8,128)}, f32[2,1024,128]{2,1,0:T(8,128)}) custom-call(s32[256]{0:T(256)} %pos_ref.3, bf16[256,4608]{1,0:T(8,128)(2,1)} %x_hbm.3, f32[36,128]{1,0:T(8,128)} %bitcast.9, f32[256,256]{1,0:T(8,128)} %constant.8.clone.table_ref, bf16[4608,2048]{1,0:T(8,128)(2,1)} %wq_hbm.1, ...), custom_call_target="tpu_custom_call" | custom-call | flops 4831838208 | bytes 18874368 | tf_op jit(solution)/shard_map/project/pallas_call | solution.py:127
  13.0 48.6 %attend.1 = (bf16[256,512,128]{2,1,0:T(8,128)(2,1)}, bf16[256,512,128]{2,1,0:T(8,128)(2,1)}, f32[4,288,128]{2,1,0:T(8,128)}, f32[4,288,128]{2,1,0:T(8,128)}, f32...) custom-call(s32[256]{0:T(256)} %pos_ref.3, s32[1]{0:T(128)} %bitcast.base_ref, f32[2,2048,128]{2,1,0:T(8,128)} %get-tuple-element.12.q_hbm, ...), custom_call_target="tpu_custom_call" | custom-call | flops 1073741824 | bytes 134217728 | tf_op jit(solution)/shard_map/attend/pallas_call | solution.py:320
  61.6 50.4 %merge.1.sums_hbm = f32[4,9,64,512]{3,2,1,0:T(8,128)} custom-call(f32[4,288,128]{2,1,0:T(8,128)} %get-tuple-element.15.b0, f32[4,288,128]{2,1,0:T(8,128)} %get-tuple-element.16.b1, f32[4,288,128]{2,1,0:T(8,128)} %get-tuple-element.17.b2, f32[4,288,128]{2,1,0:T(8,128)} %get-tuple-element.18.b3, bf16[2048,4608]{1,0:T(8,128)(2,1)} %wo_hbm.1), custom_call_target="tpu_custom_call" | custom-call | flops 1207959552 | bytes 18874368 | tf_op jit(solution)/shard_map/merge/pallas_call | solution.py:518
  112.0 5.8 %finish.1 = bf16[256,4608]{1,0:T(8,128)(2,1)} custom-call(f32[4,9,64,512]{3,2,1,0:T(8,128)} %merge.1.sums_hbm, bf16[256,4608]{1,0:T(8,128)(2,1)} %x_hbm.3, f32[36,128]{1,0:T(8,128)} %bitcast.10), custom_call_target="tpu_custom_call" | custom-call | tf_op jit(solution)/shard_map/finish/pallas_call | solution.py:584

commit v13 on v11

--- a/solution.py
+++ b/solution.py
@@ -347,8 +347,8 @@
     source = [refs[4 * c:4 * c + 4] for c in range(len(chunks))]
     pieces = [[b.at[d] for d in range(4)] for b in refs[-len(chunks):]]
     refs = refs[:-len(chunks)]
-    (wo_hbm, out_hbm, wo, last_in, last_out, osum, lhs, y_out, y_in, sums,
-     p_sem, w_sem, o_send, o_recv, y_send, y_recv, g_send, g_recv, d_send, d_recv, f_send, f_recv, out_sem) = refs[n_in:]
+    (wo_hbm, sums, wo, last_in, last_out, osum, lhs, y_out, y_in,
+     p_sem, w_sem, o_send, o_recv, y_send, y_recv, g_send, g_recv, d_send, d_recv, f_send, f_recv) = refs[n_in:]
     sp = lax.axis_index('sp')
     tp = lax.axis_index('tp')
     core = lax.rem(sp, 2)
@@ -358,7 +358,6 @@
     parts = [c // 4 for c in chunks]
     core_id = 2 * xpos + (1 - core)
     x_id = 2 * (1 - xpos) + core
-    far_id = 2 * (1 - xpos) + (1 - core)
     core_peer, x_peer, y_peer = {'sp': core_id}, {'sp': x_id}, {'tp': 1 - tp}
     mesh_id = pl.DeviceIdType.MESH
 
@@ -448,10 +447,6 @@
 
     def relay(t):
         return gather(t, x_id, f_send, f_recv, core_peer)
-
-    def keep(t, turn, owner):
-        ns, r, _ = order[t]
-        return pltpu.make_async_copy(sums.at[owner, ns, r], out_hbm.at[owner, ns, r], out_sem.at[turn, t])
 
     def project_rows(n, r0, count):
         y_out[n, r0:r0 + count, :] = jnp.dot(lhs[r0:r0 + count, :], wo[n], preferred_element_type=jnp.float32)
@@ -479,24 +474,18 @@
             sums[sp, ns, r, :] = y_out[ns, r, :] + y_in[ns, r, :]
             to_x(t).start()
             to_core(t).start()
-            keep(t, 0, sp).start()
         if 1 <= t < n_pieces + 1:
             to_x(t - 1).wait_recv()
             relay(t - 1).start()
-            keep(t - 1, 1, x_id).start()
         if t >= 3:
             to_core(t - 3).wait_recv()
-            keep(t - 3, 2, core_id).start()
             relay(t - 3).wait_recv()
-            keep(t - 3, 3, far_id).start()
     for copy in last:
         copy.wait_send()
     for t in range(n_pieces):
         to_x(t).wait_send()
         to_core(t).wait_send()
         relay(t).wait_send()
-        for turn in range(4):
-            keep(t, turn, sp).wait()
 
 
 def merge(chunks, pieces, w_o, n_chunks):
@@ -507,13 +496,14 @@
     hbm = pl.BlockSpec(memory_space=pltpu.HBM)
     f32 = jnp.float32
     dma = pltpu.SemaphoreType.DMA
-    flat = [p for piece in pieces for p in piece]
+    flat = [p if 0 < d and c < len(chunks) - 1 else pltpu.with_memory_space_constraint(p, pltpu.HBM)
+            for c, piece in enumerate(pieces) for d, p in enumerate(piece)]
     block = pieces[-1][0].shape
     return pl.pallas_call(
         functools.partial(merge_kernel, chunks),
-        out_shape=pltpu.HBM((4, n_chunks, quarter, chunk), f32),
+        out_shape=jax.ShapeDtypeStruct((4, n_chunks, quarter, chunk), f32),
         in_specs=[hbm] * (len(flat) + 1),
-        out_specs=hbm,
+        out_specs=pl.BlockSpec(memory_space=pltpu.VMEM),
         scratch_shapes=[
             pltpu.VMEM((n_chunks, inner, chunk), jnp.bfloat16),
             pltpu.VMEM((3,) + block, f32),
@@ -522,38 +512,24 @@
             pltpu.VMEM((quarter, inner), jnp.bfloat16),
             pltpu.VMEM((n_chunks, quarter, chunk), f32),
             pltpu.VMEM((n_chunks, quarter, chunk), f32),
-            pltpu.VMEM((4, n_chunks, quarter, chunk), f32),
             dma((len(chunks), 4)), dma((n_chunks,)), dma((3,)), dma((3,)),
-        ] + [dma((10,))] * 8 + [dma((4, 10))] + [pltpu.VMEM((4,) + piece[0].shape, f32) for piece in pieces],
-        compiler_params=pltpu.CompilerParams(vmem_limit_bytes=56 * 1024 * 1024, collective_id=0, has_side_effects=True),
+        ] + [dma((10,))] * 8 + [pltpu.VMEM((4,) + piece[0].shape, f32) for piece in pieces],
+        compiler_params=pltpu.CompilerParams(vmem_limit_bytes=40 * 1024 * 1024, collective_id=0, has_side_effects=True),
         cost_estimate=pl.CostEstimate(flops=2 * quarter * inner * width, bytes_accessed=2 * inner * width, transcendentals=0),
         name='merge',
     )(*flat, pltpu.with_memory_space_constraint(w_o, pltpu.HBM))
 
 
-def finish_kernel(sums_hbm, x_hbm, wpost_ref, out_hbm, gain_ref, sums, xbuf, obuf, in_sem, out_sem):
+def finish_kernel(sums, xbuf, wpost_ref, out_hbm, gain_ref, obuf, out_sem):
     parts, n_chunks, rows, chunk = sums.shape
-
-    def loads(q):
-        at = pl.ds(q * rows, rows)
-        return (pltpu.make_async_copy(sums_hbm.at[q], sums.at[q], in_sem.at[q, 0]),
-                pltpu.make_async_copy(x_hbm.at[at], xbuf.at[at], in_sem.at[q, 1]))
 
     def store(q):
         at = pl.ds(q * rows, rows)
         return pltpu.make_async_copy(obuf.at[at], out_hbm.at[at], out_sem.at[q])
 
-    for q in range(2):
-        for copy in loads(q):
-            copy.start()
     for j in range(wpost_ref.shape[0]):
         gain_ref[:, j * 128:(j + 1) * 128] = 1.0 + wpost_ref[j:j + 1, :]
     for q in range(parts):
-        for copy in loads(q):
-            copy.wait()
-        if q + 2 < parts:
-            for copy in loads(q + 2):
-                copy.start()
         for k in range(rows // 16):
             at = slice(k * 16, (k + 1) * 16)
             to = slice(q * rows + k * 16, q * rows + (k + 1) * 16)
@@ -578,11 +554,10 @@
     return pl.pallas_call(
         finish_kernel,
         out_shape=jax.ShapeDtypeStruct(x_in.shape, x_in.dtype),
-        in_specs=[hbm, hbm, pl.BlockSpec(memory_space=pltpu.VMEM)],
+        in_specs=[pl.BlockSpec(memory_space=pltpu.VMEM)] * 3,
         out_specs=hbm,
-        scratch_shapes=[pltpu.VMEM((1, x_in.shape[1]), jnp.float32), pltpu.VMEM(sums.shape, jnp.float32),
-                        pltpu.VMEM(x_in.shape, x_in.dtype), pltpu.VMEM(x_in.shape, x_in.dtype), dma((parts, 2)), dma((parts,))],
-        compiler_params=pltpu.CompilerParams(vmem_limit_bytes=62 * 1024 * 1024),
+        scratch_shapes=[pltpu.VMEM((1, x_in.shape[1]), jnp.float32), pltpu.VMEM(x_in.shape, x_in.dtype), dma((parts,))],
+        compiler_params=pltpu.CompilerParams(vmem_limit_bytes=24 * 1024 * 1024),
         name='finish',
     )(sums, x_in, w_post)
 

time: 117 us -> 111 us (0.949)
  Pallas kernels: 112 us -> 106 us
    pallas_call x1, Pallas kernels: 5.78 us -> 1.96 us  [finish(): pl.pallas_call(finish_kernel, out_shape=jax.ShapeDtypeStruct(x_in.shape,...]
    pallas_call x1, Pallas kernels: 42.2 us -> 40.6 us  [merge(): pl.pallas_call(functools.partial(merge_kernel, chunks), out_shape=jax.Sha...]
  transfers between devices with their start and end apart: 3 -> 3, of which waited for: 0 -> 0; matrix products, arithmetic and copies ran while one was open for 0% -> 0% of each run, Pallas kernels for 22% -> 23%
where the time goes in v13:
time: 111 us; the launch traced here: 110 us
  Pallas kernels  106 us (95%)
  starting transfers between devices  3.01 us (3%)
    pallas_call x2, Pallas kernels, attend(): pl.pallas_call(functools.partial(attend_kernel, n_steps, rows // 4, first...  51.3 us
    pallas_call x1, Pallas kernels, merge(): pl.pallas_call(functools.partial(merge_kernel, chunks), out_shape=jax.Sha...  40.6 us
    pallas_call x1, Pallas kernels, project(): pl.pallas_call(project_kernel, out_shape=(pltpu.HBM((2, rows * q_cols //...  12.5 us
    ppermute x3, starting transfers between devices, local_step(): moved.append(lax.ppermute(p, 'sp', [(i, i ^ d) for i in range(sp_size)]))  3.01 us
  transfers between devices with their start and end apart: 3, of which 0 were waited for; matrix products, arithmetic and copies ran while one was open for 0% of the time, Pallas kernels for 23%

profile of v13, /device:TPU:0, one launch (start us, length us, event | category | flops | bytes accessed | tf_op | source)
XLA Modules:
  0.0 110.4 jit_solution(18031471790827471749)
XLA Ops:
  0.6 12.5 %project.1 = (f32[2,2048,128]{2,1,0:T(8,128)}, f32[2,1024,128]{2,1,0:T(8,128)}, f32[2,1024,128]{2,1,0:T(8,128)}) custom-call(s32[256]{0:T(256)} %pos_ref.5, bf16[256,4608]{1,0:T(8,128)(2,1)} %xbuf.1, f32[36,128]{1,0:T(8,128)} %bitcast.14, f32[256,256]{1,0:T(8,128)} %constant.8.clone.table_ref, bf16[4608,2048]{1,0:T(8,128)(2,1)} %wq_hbm.1, ...), custom_call_target="tpu_custom_call" | custom-call | flops 4831838208 | bytes 18874368 | tf_op jit(solution)/shard_map/project/pallas_call | solution.py:128
  13.2 25.7 %attend.2 = (bf16[256,512,128]{2,1,0:T(8,128)(2,1)}, bf16[256,512,128]{2,1,0:T(8,128)(2,1)}, f32[544,128]{1,0:T(8,128)}, f32[544,128]{1,0:T(8,128)}, f32[544,128]{1,0:T(8,128)}, /*index=5*/f32[544,128]{1,0:T(8,128)}) custom-call(s32[256]{0:T(256)} %pos_ref.5, s32[1]{0:T(128)} %bitcast.base_ref, f32[2,2048,128]{2,1,0:T(8,128)} %get-tuple-element.18.q_hbm, ...), custom_call_target="tpu_custom_call" | custom-call | flops 536870912 | bytes 67108864 | tf_op jit(solution)/shard_map/attend/pallas_call | solution.py:315
  38.8 0.2 collective-permute-start
  39.0 2.8 %collective-permute-start.1 = (f32[544,128]{1,0:T(8,128)}, f32[544,128]{1,0:T(8,128)S(1)}, u32[]{:S(2)}, u32[]{:S(2)}) collective-permute-start(f32[544,128]{1,0:T(8,128)} %get-tuple-element.23), channel_id=1, source_target_pairs={{0,2},{1,3},{2,0},{3,1},{4,6},{5,7},{6,4},{7,5}} | collective-permute-start | bytes 835592 | tf_op jit(solution)/shard_map/ppermute | solution.py:585
  41.9 0.0 collective-permute-start.2
  41.9 25.7 %attend.3 = (bf16[256,512,128]{2,1,0:T(8,128)(2,1)}, bf16[256,512,128]{2,1,0:T(8,128)(2,1)}, f32[544,128]{1,0:T(8,128)}, f32[544,128]{1,0:T(8,128)}, f32[544,128]{1,0:T(8,128)}, /*index=5*/f32[544,128]{1,0:T(8,128)}) custom-call(s32[256]{0:T(256)} %pos_ref.5, s32[1]{0:T(128)} %bitcast.base_ref, ...), custom_call_target="tpu_custom_call", output_to_operand_aliasing={{0}: (7, {}), {1}: (8, {})} | custom-call | flops 536870912 | bytes 67108864 | tf_op jit(solution)/shard_map/attend/pallas_call | solution.py:315
  67.5 0.0 copy-start
  67.5 0.0 copy-start.1
  67.6 0.0 collective-permute-done.refs_1_
  67.6 0.0 collective-permute-done.1.refs_2_
  67.6 0.0 collective-permute-done.2.refs_3_
  67.6 40.6 %merge.1.sums = f32[4,9,64,512]{3,2,1,0:T(8,128)S(1)} custom-call(f32[544,128]{1,0:T(8,128)} %get-tuple-element.21.refs_0_, f32[544,128]{1,0:T(8,128)S(1)} %collective-permute-done.refs_1_, f32[544,128]{1,0:T(8,128)S(1)} %collective-permute-done.1.refs_2_, f32[544,128]{1,0:T(8,128)S(1)} %collective-permute-done.2.refs_3_, ...), custom_call_target="tpu_custom_call" | custom-call | flops 1207959552 | bytes 18874368 | tf_op jit(solution)/shard_map/merge/pallas_call | solution.py:502
  108.2 0.0 copy-done
  108.2 0.0 copy-done.1
  108.3 2.0 %finish.1 = bf16[256,4608]{1,0:T(8,128)(2,1)} custom-call(f32[4,9,64,512]{3,2,1,0:T(8,128)S(1)} %merge.1.sums, bf16[256,4608]{1,0:T(8,128)(2,1)S(1)} %copy-done, f32[36,128]{1,0:T(8,128)S(1)} %bitcast.7), custom_call_target="tpu_custom_call" | custom-call | tf_op jit(solution)/shard_map/finish/pallas_call | solution.py:554
Async XLA Ops:
  38.8 28.7 %collective-permute-start = (f32[544,128]{1,0:T(8,128)}, f32[544,128]{1,0:T(8,128)S(1)}, u32[]{:S(2)}, u32[]{:S(2)}) collective-permute-start(f32[544,128]{1,0:T(8,128)} %get-tuple-element.22), channel_id=1, source_target_pairs={{0,1},{1,0},{2,3},{3,2},{4,5},{5,4},{6,7},{7,6}} | collective-permute-start | bytes 835592 | tf_op jit(solution)/shard_map/ppermute | solution.py:585
  39.0 28.6 %collective-permute-start.1 = (f32[544,128]{1,0:T(8,128)}, f32[544,128]{1,0:T(8,128)S(1)}, u32[]{:S(2)}, u32[]{:S(2)}) collective-permute-start(f32[544,128]{1,0:T(8,128)} %get-tuple-element.23), channel_id=1, source_target_pairs={{0,2},{1,3},{2,0},{3,1},{4,6},{5,7},{6,4},{7,5}} | collective-permute-start | bytes 835592 | tf_op jit(solution)/shard_map/ppermute | solution.py:585
  41.9 25.7 %collective-permute-start.2 = (f32[544,128]{1,0:T(8,128)}, f32[544,128]{1,0:T(8,128)S(1)}, u32[]{:S(2)}, u32[]{:S(2)}) collective-permute-start(f32[544,128]{1,0:T(8,128)} %get-tuple-element.24), channel_id=1, source_target_pairs={{0,3},{1,2},{2,1},{3,0},{4,7},{5,6},{6,5},{7,4}} | collective-permute-start | bytes 835592 | tf_op jit(solution)/shard_map/ppermute | solution.py:585
  67.5 40.7 %copy-start = (bf16[256,4608]{1,0:T(8,128)(2,1)S(1)}, bf16[256,4608]{1,0:T(8,128)(2,1)}, u32[]{:S(2)}) copy-start(bf16[256,4608]{1,0:T(8,128)(2,1)} %xbuf.1) | copy-start | bytes 7077892
  67.5 40.7 %copy-start.1 = (f32[4608]{0:T(1024)S(1)}, f32[4608]{0:T(1024)}, u32[]{:S(2)}) copy-start(f32[4608]{0:T(1024)} %param.18) | copy-start | bytes 55300

commit v14 on v13

--- a/solution.py
+++ b/solution.py
@@ -15,9 +15,9 @@
 LOG2E = 1.4426950408889634
 
 ROWS_STEP = 8
-SLOTS = 12
-AHEAD = 6
-START = 2
+SLOTS = 9
+AHEAD = 5
+START = 5
 LAG_SOFT = 2
 LAG_OUT = 4
 

time: 111 us -> 110 us (level)
  no operation moved by 1% of the time
where the time goes in v14:
time: 110 us; the launch traced here: 109 us
  Pallas kernels  106 us (96%)
  starting transfers between devices  3.01 us (3%)
    pallas_call x2, Pallas kernels, attend(): pl.pallas_call(functools.partial(attend_kernel, n_steps, rows // 4, first...  50.4 us
    pallas_call x1, Pallas kernels, merge(): pl.pallas_call(functools.partial(merge_kernel, chunks), out_shape=jax.Sha...  40.8 us
    pallas_call x1, Pallas kernels, project(): pl.pallas_call(project_kernel, out_shape=(pltpu.HBM((2, rows * q_cols //...  12.5 us
    ppermute x3, starting transfers between devices, local_step(): moved.append(lax.ppermute(p, 'sp', [(i, i ^ d) for i in range(sp_size)]))  3.01 us
  transfers between devices with their start and end apart: 3, of which 0 were waited for; matrix products, arithmetic and copies ran while one was open for 0% of the time, Pallas kernels for 23%

profile of v14, /device:TPU:0, one launch (start us, length us, event | category | flops | bytes accessed | tf_op | source)
XLA Modules:
  0.0 109.4 jit_solution(5455356937937702348)
XLA Ops:
  0.6 12.5 %project.1 = (f32[2,2048,128]{2,1,0:T(8,128)}, f32[2,1024,128]{2,1,0:T(8,128)}, f32[2,1024,128]{2,1,0:T(8,128)}) custom-call(s32[256]{0:T(256)} %pos_ref.5, bf16[256,4608]{1,0:T(8,128)(2,1)} %xbuf.1, f32[36,128]{1,0:T(8,128)} %bitcast.14, f32[256,256]{1,0:T(8,128)} %constant.8.clone.table_ref, bf16[4608,2048]{1,0:T(8,128)(2,1)} %wq_hbm.1, ...), custom_call_target="tpu_custom_call" | custom-call | flops 4831838208 | bytes 18874368 | tf_op jit(solution)/shard_map/project/pallas_call | solution.py:128
  13.2 25.2 %attend.2 = (bf16[256,512,128]{2,1,0:T(8,128)(2,1)}, bf16[256,512,128]{2,1,0:T(8,128)(2,1)}, f32[544,128]{1,0:T(8,128)}, f32[544,128]{1,0:T(8,128)}, f32[544,128]{1,0:T(8,128)}, /*index=5*/f32[544,128]{1,0:T(8,128)}) custom-call(s32[256]{0:T(256)} %pos_ref.5, s32[1]{0:T(128)} %bitcast.base_ref, f32[2,2048,128]{2,1,0:T(8,128)} %get-tuple-element.18.q_hbm, ...), custom_call_target="tpu_custom_call" | custom-call | flops 536870912 | bytes 67108864 | tf_op jit(solution)/shard_map/attend/pallas_call | solution.py:315
  38.3 0.2 collective-permute-start
  38.5 2.8 %collective-permute-start.1 = (f32[544,128]{1,0:T(8,128)}, f32[544,128]{1,0:T(8,128)S(1)}, u32[]{:S(2)}, u32[]{:S(2)}) collective-permute-start(f32[544,128]{1,0:T(8,128)} %get-tuple-element.23), channel_id=1, source_target_pairs={{0,2},{1,3},{2,0},{3,1},{4,6},{5,7},{6,4},{7,5}} | collective-permute-start | bytes 835592 | tf_op jit(solution)/shard_map/ppermute | solution.py:585
  41.3 0.0 collective-permute-start.2
  41.4 25.2 %attend.3 = (bf16[256,512,128]{2,1,0:T(8,128)(2,1)}, bf16[256,512,128]{2,1,0:T(8,128)(2,1)}, f32[544,128]{1,0:T(8,128)}, f32[544,128]{1,0:T(8,128)}, f32[544,128]{1,0:T(8,128)}, /*index=5*/f32[544,128]{1,0:T(8,128)}) custom-call(s32[256]{0:T(256)} %pos_ref.5, s32[1]{0:T(128)} %bitcast.base_ref, ...), custom_call_target="tpu_custom_call", output_to_operand_aliasing={{0}: (7, {}), {1}: (8, {})} | custom-call | flops 536870912 | bytes 67108864 | tf_op jit(solution)/shard_map/attend/pallas_call | solution.py:315
  66.6 0.0 copy-start
  66.6 0.0 copy-start.1
  66.6 0.0 collective-permute-done.refs_1_
  66.6 0.0 collective-permute-done.1.refs_2_
  66.6 0.0 collective-permute-done.2.refs_3_
  66.6 40.8 %merge.1.sums = f32[4,9,64,512]{3,2,1,0:T(8,128)S(1)} custom-call(f32[544,128]{1,0:T(8,128)} %get-tuple-element.21.refs_0_, f32[544,128]{1,0:T(8,128)S(1)} %collective-permute-done.refs_1_, f32[544,128]{1,0:T(8,128)S(1)} %collective-permute-done.1.refs_2_, f32[544,128]{1,0:T(8,128)S(1)} %collective-permute-done.2.refs_3_, ...), custom_call_target="tpu_custom_call" | custom-call | flops 1207959552 | bytes 18874368 | tf_op jit(solution)/shard_map/merge/pallas_call | solution.py:502
  107.4 0.0 copy-done
  107.4 0.0 copy-done.1
  107.4 2.0 %finish.1 = bf16[256,4608]{1,0:T(8,128)(2,1)} custom-call(f32[4,9,64,512]{3,2,1,0:T(8,128)S(1)} %merge.1.sums, bf16[256,4608]{1,0:T(8,128)(2,1)S(1)} %copy-done, f32[36,128]{1,0:T(8,128)S(1)} %bitcast.7), custom_call_target="tpu_custom_call" | custom-call | tf_op jit(solution)/shard_map/finish/pallas_call | solution.py:554
Async XLA Ops:
  38.3 28.3 %collective-permute-start = (f32[544,128]{1,0:T(8,128)}, f32[544,128]{1,0:T(8,128)S(1)}, u32[]{:S(2)}, u32[]{:S(2)}) collective-permute-start(f32[544,128]{1,0:T(8,128)} %get-tuple-element.22), channel_id=1, source_target_pairs={{0,1},{1,0},{2,3},{3,2},{4,5},{5,4},{6,7},{7,6}} | collective-permute-start | bytes 835592 | tf_op jit(solution)/shard_map/ppermute | solution.py:585
  38.5 28.1 %collective-permute-start.1 = (f32[544,128]{1,0:T(8,128)}, f32[544,128]{1,0:T(8,128)S(1)}, u32[]{:S(2)}, u32[]{:S(2)}) collective-permute-start(f32[544,128]{1,0:T(8,128)} %get-tuple-element.23), channel_id=1, source_target_pairs={{0,2},{1,3},{2,0},{3,1},{4,6},{5,7},{6,4},{7,5}} | collective-permute-start | bytes 835592 | tf_op jit(solution)/shard_map/ppermute | solution.py:585
  41.3 25.3 %collective-permute-start.2 = (f32[544,128]{1,0:T(8,128)}, f32[544,128]{1,0:T(8,128)S(1)}, u32[]{:S(2)}, u32[]{:S(2)}) collective-permute-start(f32[544,128]{1,0:T(8,128)} %get-tuple-element.24), channel_id=1, source_target_pairs={{0,3},{1,2},{2,1},{3,0},{4,7},{5,6},{6,5},{7,4}} | collective-permute-start | bytes 835592 | tf_op jit(solution)/shard_map/ppermute | solution.py:585
  66.6 40.8 %copy-start = (bf16[256,4608]{1,0:T(8,128)(2,1)S(1)}, bf16[256,4608]{1,0:T(8,128)(2,1)}, u32[]{:S(2)}) copy-start(bf16[256,4608]{1,0:T(8,128)(2,1)} %xbuf.1) | copy-start | bytes 7077892
  66.6 40.8 %copy-start.1 = (f32[4608]{0:T(1024)S(1)}, f32[4608]{0:T(1024)}, u32[]{:S(2)}) copy-start(f32[4608]{0:T(1024)} %param.18) | copy-start | bytes 55300
